TPU v7x, 128 devices: a whole 4x4x4 slice. The times are simulated.
128 devices in a mesh: lat: 16 (over x, z_lo, core), lon: 8 (over z_hi, y).
Axes of the slice: x: 4, y: 4, z: 4 (z_hi: 2, z_lo: 2; z = z_hi * 2 + z_lo), core: 2. Of those that a mesh axis runs over, the one named last changes fastest.
Arguments:
- current: bfloat16 [69, 512, 1024], P(None, 'lat', 'lon')
- next_fields: bfloat16 [128, 512, 1024], P(('lat', 'lon')), may hold values from -6 to 6
- reader_slot: int32 [69], replicated, may hold values from 0 to 127, as said below
- first_weight: bfloat16 [9, 256, 69], replicated, may hold values from -0.25 to 0.25
- first_bias: float32 [256], replicated, may hold values from -3 to 3
- second_weight: bfloat16 [9, 256, 256], replicated, may hold values from -0.125 to 0.125
- second_bias: float32 [256], replicated, may hold values from -3 to 3
Outputs:
- features: bfloat16 [256, 512, 1024], P(None, 'lat', 'lon')
- next_tile: bfloat16 [69, 512, 1024], P(None, 'lat', 'lon')
Inputs may be any that keep to these rules, and one draw needn't show every extreme that they name: `reader_slot`: the 69 entries are different slots.
All inputs are finite; a program needn't handle non-finite values.
Results may differ from a plain program's by a relative error of at most 0.0053.
Values may be sent and summed in bfloat16 or wider, within the bound.
No kernel may reach another device: no remote copies, remote signals or barrier semaphores. Data moves between devices by JAX's collectives and lax.ppermute only.
A program may use at most 128 MiB of HBM per device.

v0:
```python
import functools

import jax
import jax.numpy as jnp
from jax import lax
from jax.sharding import Mesh
from jax.sharding import PartitionSpec as P

LAT = ("lat_0", "lat_1", "lat_2")
LON = ("lon_0", "lon_1")
LAT_LON = ("lat_0", "lat_1", "lat_2", "lon_0", "lon_1")


def one_axis_at_a_time(array, axes):
    return functools.reduce(lax.psum, axes, array)


def padded_2(block, sides, width, periodic):
    for axis, dim in sides:
        count = lax.axis_size(axis)
        forward = [(i, i + 1) for i in range(count - 1)]
        if periodic:
            forward.append((count - 1, 0))
        backward = [(target, source) for source, target in forward]
        low = lax.ppermute(
            lax.slice_in_dim(block, block.shape[dim] - width, None, axis=dim), axis, forward
        )
        high = lax.ppermute(lax.slice_in_dim(block, 0, width, axis=dim), axis, backward)
        block = jnp.concatenate([low, block, high], axis=dim)
    return block


def conv_valid(padded, weight, bias):
    rows = padded.shape[1] - 2
    cols = padded.shape[2] - 2
    total = jnp.zeros((weight.shape[1], rows, cols), jnp.float32)
    for tap in range(9):
        shifted = padded[:, tap // 3 : tap // 3 + rows, tap % 3 : tap % 3 + cols]
        total = total + jnp.einsum(
            "ok,khw->ohw", weight[tap], shifted, preferred_element_type=jnp.float32
        )
    return total + bias[:, None, None]


def regrid(next_fields, reader_slot):
    slot_dev, rows_all, cols_all = next_fields.shape
    n_lat = lax.axis_size(LAT)
    n_lon = lax.axis_size(LON)
    lat_rows = rows_all // n_lat
    lon_cols = cols_all // n_lon
    blocks = next_fields.reshape(slot_dev, n_lat, lat_rows, n_lon, lon_cols)
    ordered = blocks.transpose(1, 3, 0, 2, 4).reshape(n_lat * n_lon, slot_dev, lat_rows, lon_cols)
    moved = lax.all_to_all(ordered, LAT_LON, split_axis=0, concat_axis=1, tiled=True)
    moved = moved.reshape(n_lat * n_lon * slot_dev, lat_rows, lon_cols)
    return jnp.take(moved, reader_slot, axis=0)


def encode(current, first_weight, first_bias, second_weight, second_bias):
    values = current.astype(jnp.float32)
    lat_rows = values.shape[1]
    lon_cols = values.shape[2]
    cells = lat_rows * lax.axis_size(LAT) * lon_cols * lax.axis_size(LON)
    total, squares = (
        one_axis_at_a_time(jnp.sum(values, axis=(1, 2)), LAT_LON),
        one_axis_at_a_time(jnp.sum(values * values, axis=(1, 2)), LAT_LON),
    )
    mean = total / cells
    scale = 1.0 / jnp.sqrt(squares / cells - mean * mean + 1e-05)
    normed = ((values - mean[:, None, None]) * scale[:, None, None]).astype(jnp.bfloat16)
    tall = padded_2(normed, ((LAT, 1),), 2, False)
    padded = padded_2(tall, ((LON, 2),), 2, True)
    hidden = jax.nn.gelu(conv_valid(padded, first_weight, first_bias), approximate=True)
    global_row = lax.axis_index(LAT) * lat_rows + jnp.arange(lat_rows + 2, dtype=jnp.int32) - 1
    inside = (global_row >= 0) & (global_row < lat_rows * lax.axis_size(LAT))
    hidden = jnp.where(inside[None, :, None], hidden, 0.0).astype(jnp.bfloat16)
    return conv_valid(hidden, second_weight, second_bias).astype(jnp.bfloat16)


def body(current, next_fields, reader_slot, first_weight, first_bias, second_weight, second_bias):
    features = encode(current, first_weight, first_bias, second_weight, second_bias)
    next_tile = regrid(next_fields, reader_slot)
    return (features, next_tile)


def solution(mesh):
    split = Mesh(mesh.devices.reshape(4, 2, 2, 2, 4), ("lat_0", "lat_1", "lat_2", "lon_0", "lon_1"))
    return jax.shard_map(
        body,
        mesh=split,
        in_specs=(P(None, LAT, LON), P(LAT_LON, None, None), P(), P(), P(), P(), P()),
        out_specs=(P(None, LAT, LON), P(None, LAT, LON)),
        check_vma=False,
    )
```

profile of v0, /device:TPU:4, one launch (start us, length us, event | category | flops | bytes accessed | tf_op | source)
XLA Modules:
  0.0 140.9 jit_solution(8600017276479272520)
XLA Ops:
  0.6 1.9 %copy.16 = bf16[69,32,128]{0,2,1:T(8,128)(2,1)S(1)} copy(bf16[69,32,128]{2,1,0:T(8,128)(2,1)} %param.7) | data formatting | bytes 1130496 | tf_op args[0]
  3.1 8.3 %all-reduce.1 = (f32[69]{0:T(128)S(1)}, f32[69]{0:T(128)S(1)}) all-reduce(f32[69]{0:T(128)S(1)} %get-tuple-element.11, f32[69]{0:T(128)S(1)} %get-tuple-element.10), channel_id=1, replica_groups=mesh['lat_0'=4,'lat_1'=2,'lat_2'=2,'lon_0'=2,'lon_1'=4] {'lat_0'}, use_global_device_ids=true, to_apply=%region_7.0 | all-reduce | flops 138 | bytes 1104 | tf_op jit(solution)/shard_map/psum | solution.py:15
  11.4 4.9 %all-reduce.4 = (f32[69]{0:T(128)S(1)}, f32[69]{0:T(128)S(1)}) all-reduce(f32[69]{0:T(128)S(1)} %get-tuple-element.14, f32[69]{0:T(128)S(1)} %get-tuple-element.15), channel_id=1, replica_groups=mesh['lat_0'=4,'lat_1'=2,'lat_2'=2,'lon_0'=2,'lon_1'=4] {'lat_1'}, use_global_device_ids=true, to_apply=%region_8.0 | all-reduce | flops 138 | bytes 1104 | tf_op jit(solution)/shard_map/psum | solution.py:15
  16.3 2.4 %all-reduce.3 = (f32[69]{0:T(128)S(1)}, f32[69]{0:T(128)S(1)}) all-reduce(f32[69]{0:T(128)S(1)} %get-tuple-element.20, f32[69]{0:T(128)S(1)} %get-tuple-element.21), channel_id=1, replica_groups=mesh['lat_0'=4,'lat_1'=2,'lat_2'=2,'lon_0'=2,'lon_1'=4] {'lat_2'}, use_global_device_ids=true, to_apply=%region_9.0 | all-reduce | flops 138 | bytes 1104 | tf_op jit(solution)/shard_map/psum | solution.py:15
  18.8 6.8 %all-reduce.2 = (f32[69]{0:T(128)S(1)}, f32[69]{0:T(128)S(1)}) all-reduce(f32[69]{0:T(128)S(1)} %get-tuple-element.18, f32[69]{0:T(128)S(1)} %get-tuple-element.19), channel_id=1, replica_groups=mesh['lat_0'=4,'lat_1'=2,'lat_2'=2,'lon_0'=2,'lon_1'=4] {'lon_0'}, use_global_device_ids=true, to_apply=%region_10.0 | all-reduce | flops 138 | bytes 1104 | tf_op jit(solution)/shard_map/psum | solution.py:15
  25.5 10.7 %all-reduce = (f32[69]{0:T(128)S(1)}, f32[69]{0:T(128)S(1)}) all-reduce(f32[69]{0:T(128)S(1)} %get-tuple-element.16, f32[69]{0:T(128)S(1)} %get-tuple-element.17), channel_id=1, replica_groups=mesh['lat_0'=4,'lat_1'=2,'lat_2'=2,'lon_0'=2,'lon_1'=4] {'lon_1'}, use_global_device_ids=true, to_apply=%region_11.0 | all-reduce | flops 138 | bytes 1104 | tf_op jit(solution)/shard_map/psum | solution.py:15
  36.6 1.9 %collective-permute-start = (bf16[69,2,128]{0,2,1:T(8,128)(2,1)S(1)}, bf16[69,2,128]{0,2,1:T(8,128)(2,1)S(1)}, u32[]{:S(2)}, u32[]{:S(2)}) collective-permute-start(bf16[69,2,128]{0,2,1:T(8,128)(2,1)S(1)} %get-tuple-element.24), channel_id=1, source_target_pairs={{0,8},{8,16},{16,24},{24,32},{32,40},{40,48},{48,56},{56,64},{64,7... | collective-permute-start | bytes 105992 | tf_op jit(solution)/shard_map/ppermute | solution.py:25
  38.5 4.5 %collective-permute-start.1 = (bf16[69,2,128]{0,2,1:T(8,128)(2,1)S(1)}, bf16[69,2,128]{0,2,1:T(8,128)(2,1)S(1)}, u32[]{:S(2)}, u32[]{:S(2)}) collective-permute-start(bf16[69,2,128]{0,2,1:T(8,128)(2,1)S(1)} %get-tuple-element.25), channel_id=1, source_target_pairs={{8,0},{16,8},{24,16},{32,24},{40,32},{48,40},{56,48},{64,56},{72,6... | collective-permute-start | bytes 105992 | tf_op jit(solution)/shard_map/ppermute | solution.py:28
  43.3 1.2 copy.17
  44.6 8.1 %all-to-all-start = ((bf16[128,1,32,128]{3,2,1,0:T(8,128)(2,1)}), bf16[128,1,32,128]{3,2,1,0:T(8,128)(2,1)}, u32[]{:S(2)}, u32[]{:S(2)}) async-start(bf16[128,1,32,128]{3,2,1,0:T(8,128)(2,1)} %bitcast.40), calls=%async_computation | async-start | bytes 2097152 | tf_op jit(solution)/shard_map/all_to_all | solution.py:53
  52.8 5.8 %collective-permute-start.3 = (bf16[69,36,2]{0,2,1:T(2,128)(2,1)S(1)}, bf16[69,36,2]{0,2,1:T(2,128)(2,1)S(1)}, u32[]{:S(2)}, u32[]{:S(2)}) collective-permute-start(bf16[69,36,2]{0,2,1:T(2,128)(2,1)S(1)} %get-tuple-element.23), channel_id=1, source_target_pairs={{1,0},{2,1},{3,2},{4,3},{5,4},{6,5},{7,6},{0,7},{9,8},{10,9},{11,1... | collective-permute-start | bytes 29816 | tf_op jit(solution)/shard_map/ppermute | solution.py:28
  58.6 6.9 %collective-permute-done.3 = bf16[69,36,2]{0,2,1:T(2,128)(2,1)S(1)} collective-permute-done((bf16[69,36,2]{0,2,1:T(2,128)(2,1)S(1)}, bf16[69,36,2]{0,2,1:T(2,128)(2,1)S(1)}, u32[]{:S(2)}, u32[]{:S(2)}) %collective-permute-start.3) | collective-permute-done | bytes 9968 | tf_op jit(solution)/shard_map/ppermute | solution.py:28
  65.5 4.4 %collective-permute-done.2 = bf16[69,36,2]{0,2,1:T(2,128)(2,1)S(1)} collective-permute-done((bf16[69,36,2]{0,2,1:T(2,128)(2,1)S(1)}, bf16[69,36,2]{0,2,1:T(2,128)(2,1)S(1)}, u32[]{:S(2)}, u32[]{:S(2)}) %collective-permute-start.2) | collective-permute-done | bytes 9968 | tf_op jit(solution)/shard_map/ppermute | solution.py:25
  71.1 3.0 %fusion.34 = f32[34,130,256]{2,1,0:T(8,128)} fusion(bf16[69,36,132]{0,2,1:T(8,128)(2,1)S(1)} %pad_maximum_fusion, bf16[9,256,69]{1,2,0:T(8,128)(2,1)S(1)} %copy-done.2), kind=kOutput, calls=%fused_computation.41 | convolution fusion | flops 156149760 | bytes 5746688 | tf_op jit(solution)/shard_map/ok,khw->ohw/dot_general | solution.py:39
  74.2 2.9 %fusion.36 = f32[34,130,256]{2,1,0:T(8,128)} fusion(bf16[69,36,132]{0,2,1:T(8,128)(2,1)S(1)} %pad_maximum_fusion, bf16[9,256,69]{1,2,0:T(8,128)(2,1)S(1)} %copy-done.2), kind=kOutput, calls=%fused_computation.43 | convolution fusion | flops 156149760 | bytes 5746688 | tf_op jit(solution)/shard_map/ok,khw->ohw/dot_general | solution.py:39
  77.1 2.9 %fusion.63 = f32[34,130,256]{2,1,0:T(8,128)} fusion(bf16[9,256,69]{1,2,0:T(8,128)(2,1)S(1)} %copy-done.2, bf16[69,36,2]{0,2,1:T(2,128)(2,1)S(1)} %collective-permute-done.3, bf16[69,2,128]{0,2,1:T(8,128)(2,1)S(1)} %collective-permute-done.1, bf16[69,32,128]{0,2,1:T(8,128)(2,1)S(1)} %fusion.10, bf16[69,2,128]{0,2,1:T(8,128)(2,1)S(1)} %collective-permute-done), kind=kOutput, calls=%fused_computation.69 | convolution fusion | flops 158733120 | bytes 5761024 | tf_op jit(solution)/shard_map/ok,khw->ohw/dot_general | solution.py:39
  80.0 2.9 %fusion.66 = f32[34,130,256]{2,1,0:T(8,128)} fusion(bf16[9,256,69]{1,2,0:T(8,128)(2,1)S(1)} %copy-done.2, bf16[69,2,128]{0,2,1:T(8,128)(2,1)S(1)} %collective-permute-done.1, bf16[69,32,128]{0,2,1:T(8,128)(2,1)S(1)} %fusion.10, bf16[69,2,128]{0,2,1:T(8,128)(2,1)S(1)} %collective-permute-done, bf16[69,36,2]{0,2,1:T(2,128)(2,1)S(1)} %collective-permute-done.2), kind=kOutput, calls=%fused_computation.72 | convolution fusion | flops 158733120 | bytes 5761024 | tf_op jit(solution)/shard_map/ok,khw->ohw/dot_general | solution.py:39
  82.9 2.9 %fusion.68 = f32[34,130,256]{2,1,0:T(8,128)} fusion(bf16[9,256,69]{1,2,0:T(8,128)(2,1)S(1)} %copy-done.2, bf16[69,36,2]{0,2,1:T(2,128)(2,1)S(1)} %collective-permute-done.3, bf16[69,2,128]{0,2,1:T(8,128)(2,1)S(1)} %collective-permute-done.1, bf16[69,32,128]{0,2,1:T(8,128)(2,1)S(1)} %fusion.10, bf16[69,2,128]{0,2,1:T(8,128)(2,1)S(1)} %collective-permute-done), kind=kOutput, calls=%fused_computation.74 | convolution fusion | flops 158733120 | bytes 5761024 | tf_op jit(solution)/shard_map/ok,khw->ohw/dot_general | solution.py:39
  85.8 3.0 %fusion.71 = f32[34,130,256]{2,1,0:T(8,128)} fusion(bf16[9,256,69]{1,2,0:T(8,128)(2,1)S(1)} %copy-done.2, bf16[69,2,128]{0,2,1:T(8,128)(2,1)S(1)} %collective-permute-done.1, bf16[69,32,128]{0,2,1:T(8,128)(2,1)S(1)} %fusion.10, bf16[69,2,128]{0,2,1:T(8,128)(2,1)S(1)} %collective-permute-done, bf16[69,36,2]{0,2,1:T(2,128)(2,1)S(1)} %collective-permute-done.2), kind=kOutput, calls=%fused_computation.77 | convolution fusion | flops 158733120 | bytes 5761024 | tf_op jit(solution)/shard_map/ok,khw->ohw/dot_general | solution.py:39
  88.8 2.9 %fusion.61 = f32[34,130,256]{2,1,0:T(8,128)} fusion(bf16[9,256,69]{1,2,0:T(8,128)(2,1)S(1)} %copy-done.2, bf16[69,2,128]{0,2,1:T(8,128)(2,1)S(1)} %collective-permute-done.1, bf16[69,32,128]{0,2,1:T(8,128)(2,1)S(1)} %fusion.10, bf16[69,2,128]{0,2,1:T(8,128)(2,1)S(1)} %collective-permute-done, bf16[69,36,2]{0,2,1:T(2,128)(2,1)S(1)} %collective-permute-done.2), kind=kOutput, calls=%fused_computation.67 | convolution fusion | flops 158733120 | bytes 5761024 | tf_op jit(solution)/shard_map/ok,khw->ohw/dot_general | solution.py:39
  91.7 12.7 %fusion.8 = bf16[256,34,130]{0,2,1:T(8,128)(2,1)S(1)} fusion(f32[34,130,256]{2,1,0:T(8,128)S(1)} %fusion.32, f32[34,130,256]{2,1,0:T(8,128)} %fusion.61, f32[34,130,256]{2,1,0:T(8,128)} %fusion.63, f32[34,130,256]{2,1,0:T(8,128)} %fusion.34, f32[34,130,256]{2,1,0:T(8,128)} %fusion.66, f32[34,130,256]{2,1,0:T(8,128)} %fusion.68, ...), kind=kOutput, calls=%fused_computation.10 | convolution fusion | flops 180232000 | bytes 39917056 | tf_op jit(solution)/shard_map/ok,khw->ohw/dot_general | solution.py:39
  105.2 2.7 %fusion.15 = f32[32,128,256]{2,1,0:T(8,128)} fusion(bf16[256,34,130]{0,2,1:T(8,128)(2,1)S(1)} %fusion.8, bf16[9,256,256]{2,1,0:T(8,128)(2,1)S(1)} %copy-done), kind=kOutput, calls=%fused_computation.21 | convolution fusion | flops 536870912 | bytes 6422528 | tf_op jit(solution)/shard_map/ok,khw->ohw/dot_general | solution.py:39
  107.9 2.7 %fusion.17 = f32[32,128,256]{2,1,0:T(8,128)} fusion(bf16[256,34,130]{0,2,1:T(8,128)(2,1)S(1)} %fusion.8, bf16[9,256,256]{2,1,0:T(8,128)(2,1)S(1)} %copy-done), kind=kOutput, calls=%fused_computation.23 | convolution fusion | flops 536870912 | bytes 6422528 | tf_op jit(solution)/shard_map/ok,khw->ohw/dot_general | solution.py:39
  110.6 2.7 %fusion.19 = f32[32,128,256]{2,1,0:T(8,128)} fusion(bf16[256,34,130]{0,2,1:T(8,128)(2,1)S(1)} %fusion.8, bf16[9,256,256]{2,1,0:T(8,128)(2,1)S(1)} %copy-done), kind=kOutput, calls=%fused_computation.25 | convolution fusion | flops 536870912 | bytes 6422528 | tf_op jit(solution)/shard_map/ok,khw->ohw/dot_general | solution.py:39
  113.3 2.7 %fusion.21 = f32[32,128,256]{2,1,0:T(8,128)} fusion(bf16[256,34,130]{0,2,1:T(8,128)(2,1)S(1)} %fusion.8, bf16[9,256,256]{2,1,0:T(8,128)(2,1)S(1)} %copy-done), kind=kOutput, calls=%fused_computation.27 | convolution fusion | flops 536870912 | bytes 6422528 | tf_op jit(solution)/shard_map/ok,khw->ohw/dot_general | solution.py:39
  116.0 2.7 %fusion.23 = f32[32,128,256]{2,1,0:T(8,128)} fusion(bf16[256,34,130]{0,2,1:T(8,128)(2,1)S(1)} %fusion.8, bf16[9,256,256]{2,1,0:T(8,128)(2,1)S(1)} %copy-done), kind=kOutput, calls=%fused_computation.29 | convolution fusion | flops 536870912 | bytes 6422528 | tf_op jit(solution)/shard_map/ok,khw->ohw/dot_general | solution.py:39
  118.7 2.7 %fusion.25 = f32[32,128,256]{2,1,0:T(8,128)} fusion(bf16[256,34,130]{0,2,1:T(8,128)(2,1)S(1)} %fusion.8, bf16[9,256,256]{2,1,0:T(8,128)(2,1)S(1)} %copy-done), kind=kOutput, calls=%fused_computation.31 | convolution fusion | flops 536870912 | bytes 6422528 | tf_op jit(solution)/shard_map/ok,khw->ohw/dot_general | solution.py:39
  121.5 2.7 %fusion.27 = f32[32,128,256]{2,1,0:T(8,128)} fusion(bf16[256,34,130]{0,2,1:T(8,128)(2,1)S(1)} %fusion.8, bf16[9,256,256]{2,1,0:T(8,128)(2,1)S(1)} %copy-done), kind=kOutput, calls=%fused_computation.33 | convolution fusion | flops 536870912 | bytes 6422528 | tf_op jit(solution)/shard_map/ok,khw->ohw/dot_general | solution.py:39
  124.2 10.8 %fusion.29 = bf16[256,32,128]{0,2,1:T(8,128)(2,1)S(1)} fusion(f32[256]{0:T(256)S(1)} %copy-done.4, bf16[256,34,130]{0,2,1:T(8,128)(2,1)S(1)} %fusion.8, f32[32,128,256]{2,1,0:T(8,128)S(1)} %fusion.13, f32[32,128,256]{2,1,0:T(8,128)} %fusion.15, f32[32,128,256]{2,1,0:T(8,128)} %fusion.17, f32[32,128,256]{2,1,0:T(8,128)} %fusion.19, ...), kind=kOutput, calls=%fused_computation.35 | convolution fusion | flops 547356672 | bytes 37880832 | tf_op jit(solution)/shard_map/ok,khw->ohw/dot_general | solution.py:39
  134.9 3.1 %copy.19 = bf16[256,32,128]{2,1,0:T(8,128)(2,1)} copy(bf16[256,32,128]{0,2,1:T(8,128)(2,1)S(1)} %fusion.29) | data formatting | bytes 4194304
  138.0 1.9 %gather_fusion = bf16[69,32,128]{2,1,0:T(8,128)(2,1)S(1)} fusion(bf16[128,32,128]{2,1,0:T(8,128)(2,1)} %bitcast.41, s32[1024]{0:T(1024)S(1)} %pad_clamp_fusion), kind=kCustom, calls=%fused_computation | custom fusion | bytes 1130772 | tf_op jit(solution)/shard_map/jit(_take)/gather | solution.py:55
  139.9 1.0 broadcast_select_fusion
  (29 shorter events, 3.2 us)
Async XLA Ops:
  0.6 42.4 %copy-start.1 = (bf16[1,512,1024]{2,1,0:T(8,128)(2,1)S(1)}, bf16[1,512,1024]{2,1,0:T(8,128)(2,1)}, u32[]{:S(2)}) copy-start(bf16[1,512,1024]{2,1,0:T(8,128)(2,1)} %param.8) | copy-start | bytes 3145732
  36.6 16.2 %collective-permute-start = (bf16[69,2,128]{0,2,1:T(8,128)(2,1)S(1)}, bf16[69,2,128]{0,2,1:T(8,128)(2,1)S(1)}, u32[]{:S(2)}, u32[]{:S(2)}) collective-permute-start(bf16[69,2,128]{0,2,1:T(8,128)(2,1)S(1)} %get-tuple-element.24), channel_id=1, source_target_pairs={{0,8},{8,16},{16,24},{24,32},{32,40},{40,48},{48,56},{56,64},{64,7... | collective-permute-start | bytes 105992 | tf_op jit(solution)/shard_map/ppermute | solution.py:25
  38.5 14.3 %collective-permute-start.1 = (bf16[69,2,128]{0,2,1:T(8,128)(2,1)S(1)}, bf16[69,2,128]{0,2,1:T(8,128)(2,1)S(1)}, u32[]{:S(2)}, u32[]{:S(2)}) collective-permute-start(bf16[69,2,128]{0,2,1:T(8,128)(2,1)S(1)} %get-tuple-element.25), channel_id=1, source_target_pairs={{8,0},{16,8},{24,16},{32,24},{40,32},{48,40},{56,48},{64,56},{72,6... | collective-permute-start | bytes 105992 | tf_op jit(solution)/shard_map/ppermute | solution.py:28
  43.3 9.4 %copy-start.5 = (s32[69]{0:T(128)S(1)}, s32[69]{0:T(128)}, u32[]{:S(2)}) copy-start(s32[69]{0:T(128)} %param.9) | copy-start | bytes 832
  44.6 25.8 %copy-start.2 = (bf16[9,256,69]{1,2,0:T(8,128)(2,1)S(1)}, bf16[9,256,69]{1,2,0:T(8,128)(2,1)}, u32[]{:S(2)}) copy-start(bf16[9,256,69]{1,2,0:T(8,128)(2,1)} %param.10) | copy-start | bytes 953860
  44.6 93.5 %all-to-all-start = ((bf16[128,1,32,128]{3,2,1,0:T(8,128)(2,1)}), bf16[128,1,32,128]{3,2,1,0:T(8,128)(2,1)}, u32[]{:S(2)}, u32[]{:S(2)}) async-start(bf16[128,1,32,128]{3,2,1,0:T(8,128)(2,1)} %bitcast.40), calls=%async_computation | async-start | bytes 2097152 | tf_op jit(solution)/shard_map/all_to_all | solution.py:53
  52.8 12.7 %collective-permute-start.3 = (bf16[69,36,2]{0,2,1:T(2,128)(2,1)S(1)}, bf16[69,36,2]{0,2,1:T(2,128)(2,1)S(1)}, u32[]{:S(2)}, u32[]{:S(2)}) collective-permute-start(bf16[69,36,2]{0,2,1:T(2,128)(2,1)S(1)} %get-tuple-element.23), channel_id=1, source_target_pairs={{1,0},{2,1},{3,2},{4,3},{5,4},{6,5},{7,6},{0,7},{9,8},{10,9},{11,1... | collective-permute-start | bytes 29816 | tf_op jit(solution)/shard_map/ppermute | solution.py:28
  58.6 11.3 %collective-permute-start.2 = (bf16[69,36,2]{0,2,1:T(2,128)(2,1)S(1)}, bf16[69,36,2]{0,2,1:T(2,128)(2,1)S(1)}, u32[]{:S(2)}, u32[]{:S(2)}) collective-permute-start(bf16[69,36,2]{0,2,1:T(2,128)(2,1)S(1)} %get-tuple-element.22), channel_id=1, source_target_pairs={{0,1},{1,2},{2,3},{3,4},{4,5},{5,6},{6,7},{7,0},{8,9},{9,10},{10,1... | collective-permute-start | bytes 29816 | tf_op jit(solution)/shard_map/ppermute | solution.py:25
  88.8 2.9 %copy-start.3 = (f32[256]{0:T(256)S(1)}, f32[256]{0:T(256)}, u32[]{:S(2)}) copy-start(f32[256]{0:T(256)} %param.11) | copy-start | bytes 3076
  91.7 12.7 %copy-start = (bf16[9,256,256]{2,1,0:T(8,128)(2,1)S(1)}, bf16[9,256,256]{2,1,0:T(8,128)(2,1)}, u32[]{:S(2)}) copy-start(bf16[9,256,256]{2,1,0:T(8,128)(2,1)} %param.12) | copy-start | bytes 3538948
  121.5 2.7 %copy-start.4 = (f32[256]{0:T(256)S(1)}, f32[256]{0:T(256)}, u32[]{:S(2)}) copy-start(f32[256]{0:T(256)} %param.13) | copy-start | bytes 3076
where the time goes:
time: 141 us
  matrix products  64.5 us (46%)
  blocking collectives  33.2 us (24%)
  starting transfers between devices  20.4 us (14%)
  waiting for transfers between devices  11.3 us (8%)
  local copies, waits for them, and re-layouts  8.31 us (6%)
  other arithmetic  2.36 us (2%)
    dot_general x18, matrix products, conv_valid(): jnp.einsum('ok,khw->ohw', weight[tap], shifted, preferred_element_type=jn...  64.5 us
    psum x5, blocking collectives, one_axis_at_a_time(): return functools.reduce(lax.psum, axes, array)  33.2 us
    ppermute x2, starting transfers between devices, padded_2(): lax.ppermute(lax.slice_in_dim(block, 0, width, axis=dim), axis, backward)  10.3 us
    all_to_all x1, starting transfers between devices, regrid(): lax.all_to_all(ordered, LAT_LON, split_axis=0, concat_axis=1, tiled=True)  8.12 us
    ppermute x2, waiting for transfers between devices, padded_2(): lax.ppermute(lax.slice_in_dim(block, 0, width, axis=dim), axis, backward)  6.94 us
    unnamed x15, local copies, waits for them, and re-layouts  5.21 us
    ppermute x2, waiting for transfers between devices, padded_2(): lax.ppermute(lax.slice_in_dim(block, block.shape[dim] - width, None, axis...  4.35 us
  transfers between devices with their start and end apart: 5, of which 2 were waited for; matrix products, arithmetic and copies ran while one was open for 49% of the time, Pallas kernels for 0%

commit v1 on v0

v1 whole, which is shorter than its diff:
```python
import functools

import jax
import jax.numpy as jnp
from jax import lax
from jax.experimental import pallas as pl
from jax.experimental.pallas import tpu as pltpu
from jax.sharding import Mesh
from jax.sharding import PartitionSpec as P

LAT = ("lat_0", "lat_1", "lat_2")
LON = ("lon_0", "lon_1")
LANES = 128
BLOCK = 8
GELU_C = 0.7978845608028654


def gelu(v):
    return (0.5 * v) * (1.0 + jnp.tanh(v * (GELU_C + (GELU_C * 0.044715) * (v * v))))


def conv_kernel(
    channels, rows, cols, hid,
    ends_ref, x_ref, top_ref, bottom_ref, left_ref, right_ref, edge_ref, mean_ref, scale_ref,
    w1_ref, b1_ref, w2_ref, b2_ref, out_ref,
    taps_ref, edge_taps_ref, edge_hid_ref, west_ref, mid_ref, east_ref, turned_ref,
):
    mean = mean_ref[...]
    scale = scale_ref[...]
    first = ends_ref[0] != 0
    last = ends_ref[1] != 0
    lane = lax.broadcasted_iota(jnp.int32, (cols, LANES), 1)
    sub = lax.broadcasted_iota(jnp.int32, (cols, LANES), 0)
    sub_hid = lax.broadcasted_iota(jnp.int32, (cols, hid), 0)
    over = 2 * channels - LANES

    def norm(raw):
        return (raw.astype(jnp.float32) - mean) * scale

    def pack(minus, zero, plus, lanes):
        turned = pltpu.roll(zero, channels, axis=1)
        low = jnp.where(lanes < channels, minus, turned)
        high = jnp.where(lanes < over, turned, pltpu.roll(plus, over, axis=1))
        return low, high

    def build(raw, row, keep):
        main = norm(raw)
        left = norm(left_ref[row])
        right = norm(right_ref[row])
        if keep is not None:
            main = jnp.where(keep, main, 0.0)
            left = jnp.where(keep, left, 0.0)
            right = jnp.where(keep, right, 0.0)
        minus = jnp.where(sub == 0, left[1:2], pltpu.roll(main, 1, axis=0))
        plus = jnp.where(sub == cols - 1, right[0:1], pltpu.roll(main, cols - 1, axis=0))
        low, high = pack(minus, main, plus, lane)
        taps_ref[row, :, 0:LANES] = low.astype(jnp.bfloat16)
        taps_ref[row, :, LANES : 2 * LANES] = high.astype(jnp.bfloat16)

    for r in range(2):
        build(top_ref[r], r, jnp.logical_not(first))
        build(bottom_ref[r], rows + 2 + r, jnp.logical_not(last))

    @pl.loop(0, rows)
    def _(r):
        build(x_ref[r], r + 2, None)

    tall = edge_ref.shape[2]
    edge_row = lax.broadcasted_iota(jnp.int32, (tall, LANES), 0)
    edge_lane = lax.broadcasted_iota(jnp.int32, (tall, LANES), 1)
    outside = jnp.logical_or(
        jnp.logical_and(first, edge_row < 2), jnp.logical_and(last, edge_row >= rows + 2)
    )
    hid_row = lax.broadcasted_iota(jnp.int32, (tall - 8, hid), 0)
    hid_outside = jnp.logical_or(
        jnp.logical_and(first, hid_row < 1), jnp.logical_and(last, hid_row >= rows + 1)
    )
    for side in range(2):
        parts = [jnp.where(outside, 0.0, norm(edge_ref[side, b])) for b in range(3)]
        low, high = pack(*parts, edge_lane)
        edge_taps_ref[:, 0:LANES] = low
        edge_taps_ref[:, LANES : 2 * LANES] = high
        stacked = jnp.concatenate(
            [edge_taps_ref[a : a + tall - 8, :].astype(jnp.bfloat16) for a in range(3)], axis=1
        )
        value = jnp.dot(stacked, w1_ref[...], preferred_element_type=jnp.float32) + b1_ref[...]
        edge_hid_ref[side] = jnp.where(hid_outside, 0.0, gelu(value))

    def hidden(row, count, keep):
        stacked = jnp.concatenate(
            [taps_ref[pl.ds(row + a, count)].reshape(count * cols, 2 * LANES) for a in range(3)], axis=1
        )
        value = jnp.dot(stacked, w1_ref[...], preferred_element_type=jnp.float32) + b1_ref[...]
        value = gelu(value)
        for i in range(count):
            one = value[i * cols : (i + 1) * cols]
            if keep is not None:
                one = jnp.where(keep, one, 0.0)
            west = jnp.where(sub_hid == 0, edge_hid_ref[0, pl.ds(row + i, 1), :], pltpu.roll(one, 1, axis=0))
            east = jnp.where(
                sub_hid == cols - 1, edge_hid_ref[1, pl.ds(row + i, 1), :], pltpu.roll(one, cols - 1, axis=0)
            )
            west_ref[row + i] = west.astype(jnp.bfloat16)
            mid_ref[row + i] = one.astype(jnp.bfloat16)
            east_ref[row + i] = east.astype(jnp.bfloat16)

    hidden(0, 1, jnp.logical_not(first))
    hidden(rows + 1, 1, jnp.logical_not(last))

    @pl.loop(0, rows // 4)
    def _(t):
        hidden(1 + t * 4, 4, None)

    @pl.loop(0, rows // BLOCK)
    def _(t):
        base = t * BLOCK
        stacked = jnp.concatenate(
            [
                ref[pl.ds(base + a, BLOCK)].reshape(BLOCK * cols, hid)
                for a in range(3)
                for ref in (west_ref, mid_ref, east_ref)
            ],
            axis=1,
        )
        value = jnp.dot(stacked, w2_ref[...], preferred_element_type=jnp.float32) + b2_ref[...]
        for i in range(BLOCK):
            turned_ref[pl.ds(i, hid, stride=BLOCK), :] = value[i * cols : (i + 1) * cols].T
        out_ref[:, pl.ds(pl.multiple_of(base, BLOCK), BLOCK), :] = (
            turned_ref[...].reshape(hid, BLOCK, cols).astype(jnp.bfloat16)
        )


def convs(ends, x, top, bottom, left, right, edge, mean, scale, w1, b1, w2, b2):
    rows, cols = x.shape[0], x.shape[1]
    hid = w2.shape[1]
    channels = 69
    tall = edge.shape[2]
    vmem = pl.BlockSpec(memory_space=pltpu.VMEM)
    flops = 2 * hid * (rows * cols * 9 * hid + (rows + 2) * (cols + 2) * 3 * 256)
    return pl.pallas_call(
        functools.partial(conv_kernel, channels, rows, cols, hid),
        out_shape=jax.ShapeDtypeStruct((hid, rows, cols), jnp.bfloat16),
        in_specs=[pl.BlockSpec(memory_space=pltpu.SMEM)] + [vmem] * 12,
        out_specs=vmem,
        scratch_shapes=[
            pltpu.VMEM((rows + 4, cols, 2 * LANES), jnp.bfloat16),
            pltpu.VMEM((tall, 2 * LANES), jnp.float32),
            pltpu.VMEM((2, tall - 8, hid), jnp.float32),
            pltpu.VMEM((rows + 2, cols, hid), jnp.bfloat16),
            pltpu.VMEM((rows + 2, cols, hid), jnp.bfloat16),
            pltpu.VMEM((rows + 2, cols, hid), jnp.bfloat16),
            pltpu.VMEM((hid * BLOCK, cols), jnp.float32),
        ],
        compiler_params=pltpu.CompilerParams(vmem_limit_bytes=48 * 2**20),
        cost_estimate=pl.CostEstimate(flops=flops, bytes_accessed=8 * 2**20, transcendentals=0),
        name="convs",
    )(ends, x, top, bottom, left, right, edge, mean, scale, w1, b1, w2, b2)


def shift_pairs(count, periodic):
    forward = [(i, i + 1) for i in range(count - 1)]
    if periodic:
        forward.append((count - 1, 0))
    return forward, [(b, a) for a, b in forward]


def body(current, next_fields, reader_slot, first_weight, first_bias, second_weight, second_bias):
    channels, rows, cols = current.shape
    hid = first_weight.shape[1]
    n_lat = lax.axis_size(LAT)
    n_lon = lax.axis_size(LON)
    cells = rows * n_lat * cols * n_lon

    values = current.astype(jnp.float32)
    sums = jnp.stack([jnp.sum(values, axis=(1, 2)), jnp.sum(values * values, axis=(1, 2))])
    sums = jnp.pad(sums, ((0, 0), (0, LANES - channels)))
    spread = jnp.broadcast_to(sums[None], (n_lat * n_lon,) + sums.shape)
    gathered = lax.all_to_all(spread, LON + LAT, split_axis=0, concat_axis=0, tiled=True)

    turned = jnp.pad(current.transpose(1, 2, 0), ((0, 0), (0, 0), (0, LANES - channels)))
    forward, backward = shift_pairs(n_lat, False)
    top = lax.ppermute(turned[rows - 2 :], LAT, forward)
    bottom = lax.ppermute(turned[:2], LAT, backward)
    forward, backward = shift_pairs(n_lon, True)

    def tall(low, high):
        return jnp.concatenate([top[:, low:high], turned[:, low:high], bottom[:, low:high]], axis=0)

    first_cols, last_cols = tall(0, 2), tall(cols - 2, cols)
    left = lax.ppermute(last_cols, LON, forward)
    right = lax.ppermute(first_cols, LON, backward)
    edge = jnp.stack([
        jnp.stack([left[:, 0], left[:, 1], first_cols[:, 0]]),
        jnp.stack([last_cols[:, 1], right[:, 0], right[:, 1]]),
    ])
    edge = jnp.pad(edge, ((0, 0), (0, 0), (0, 48 - rows - 4), (0, 0)))

    blocks = next_fields.reshape(rows * n_lat, n_lon, cols).transpose(1, 0, 2)
    blocks = blocks.reshape(n_lon * n_lat, rows, cols)
    moved = lax.all_to_all(blocks, LON + LAT, split_axis=0, concat_axis=0, tiled=True)

    total = jnp.sum(gathered, axis=0)
    mean = total[0] / cells
    scale = 1.0 / jnp.sqrt(total[1] / cells - mean * mean + 1e-05)
    scale = jnp.where(jnp.arange(LANES) < channels, scale, 0.0)

    w1 = first_weight.transpose(0, 2, 1).reshape(3, 3 * channels, hid)
    w1 = jnp.pad(w1, ((0, 0), (0, 2 * LANES - 3 * channels), (0, 0))).reshape(6 * LANES, hid)
    w2 = second_weight.transpose(0, 2, 1).reshape(9 * hid, hid)
    at = lax.axis_index(LAT)
    ends = jnp.stack([at == 0, at == n_lat - 1]).astype(jnp.int32)
    features = convs(
        ends, turned, top, bottom, left, right, edge, mean[None], scale[None],
        w1, first_bias[None], w2, second_bias[None],
    )
    place = (reader_slot % n_lon) * n_lat + reader_slot // n_lon
    next_tile = moved.at[place].get(mode="promise_in_bounds")
    return (features, next_tile)


def solution(mesh):
    split = Mesh(mesh.devices.reshape(4, 2, 2, 2, 4), ("lat_0", "lat_1", "lat_2", "lon_0", "lon_1"))
    return jax.shard_map(
        body,
        mesh=split,
        in_specs=(P(None, LAT, LON), P(LAT + LON, None, None), P(), P(), P(), P(), P()),
        out_specs=(P(None, LAT, LON), P(None, LAT, LON)),
        check_vma=False,
    )
```

time: 141 us -> 71.9 us (0.51)
  the two profiles are of different devices: /device:TPU:4 before, /device:TPU:1 now
where the time goes in v1:
time: 71.9 us; the launch traced here: 71.5 us
  starting transfers between devices  29.6 us (41%)
  Pallas kernels  15.9 us (22%)
  local copies, waits for them, and re-layouts  15.5 us (22%)
  waiting for transfers between devices  8.7 us (12%)
  other arithmetic  0.92 us (1%)
  between operations  0.9 us (1%)
    pallas_call x1, Pallas kernels, convs(): pl.pallas_call(functools.partial(conv_kernel, channels, rows, cols, hid),...  15.9 us
    all_to_all x1, starting transfers between devices, body(): lax.all_to_all(spread, LON + LAT, split_axis=0, concat_axis=0, tiled=True)  10.5 us
    all_to_all x1, starting transfers between devices, body(): lax.all_to_all(blocks, LON + LAT, split_axis=0, concat_axis=0, tiled=True)  6.48 us
    ppermute x1, waiting for transfers between devices, body(): left = lax.ppermute(last_cols, LON, forward)  6.18 us
    ppermute x1, starting transfers between devices, body(): right = lax.ppermute(first_cols, LON, backward)  5.64 us
    unnamed x17, local copies, waits for them, and re-layouts  5.62 us
    ppermute x1, starting transfers between devices, body(): top = lax.ppermute(turned[rows - 2:], LAT, forward)  3.55 us
    ppermute x1, starting transfers between devices, body(): bottom = lax.ppermute(turned[:2], LAT, backward)  3.28 us
  transfers between devices with their start and end apart: 6, of which 2 were waited for; matrix products, arithmetic and copies ran while one was open for 14% of the time, Pallas kernels for 22%

profile of v1, /device:TPU:1, one launch (start us, length us, event | category | flops | bytes accessed | tf_op | source)
XLA Modules:
  0.0 71.5 jit_solution(14971804462900133269)
XLA Ops:
  0.6 2.3 %copy.41 = bf16[69,32,128]{0,1,2:T(8,128)(2,1)S(1)} copy(bf16[69,32,128]{2,1,0:T(8,128)(2,1)} %param.7) | data formatting | bytes 1130496 | tf_op args[0]
  2.9 0.8 %fusion.7 = (bf16[2,128,128]{2,0,1:T(2,128)(2,1)}, bf16[2,128,128]{2,0,1:T(2,128)(2,1)}) fusion(bf16[32,128,69]{2,0,1:T(8,128)(2,1)S(1)} %bitcast.35), kind=kLoop, calls=%fused_computation.32 | loop fusion | bytes 696320 | tf_op jit(solution)/shard_map/slice | solution.py:183
  3.7 3.3 %collective-permute-start.1 = (bf16[2,128,128]{2,0,1:T(2,128)(2,1)}, bf16[2,128,128]{2,0,1:T(2,128)(2,1)S(1)}, u32[]{:S(2)}, u32[]{:S(2)}) collective-permute-start(bf16[2,128,128]{2,0,1:T(2,128)(2,1)} %get-tuple-element.6), channel_id=1, source_target_pairs={{8,0},{16,8},{24,16},{32,24},{40,32},{48,40},{56,48},{64,56},{72,6... | collective-permute-start | bytes 196616 | tf_op jit(solution)/shard_map/ppermute | solution.py:183
  7.0 3.6 %collective-permute-start = (bf16[2,128,128]{2,0,1:T(2,128)(2,1)}, bf16[2,128,128]{2,0,1:T(2,128)(2,1)S(1)}, u32[]{:S(2)}, u32[]{:S(2)}) collective-permute-start(bf16[2,128,128]{2,0,1:T(2,128)(2,1)} %get-tuple-element.7), channel_id=1, source_target_pairs={{0,8},{8,16},{16,24},{24,32},{32,40},{40,48},{48,56},{56,64},{64,7... | collective-permute-start | bytes 196616 | tf_op jit(solution)/shard_map/ppermute | solution.py:182
  10.6 0.6 convert_reduce_fusion
  11.2 0.7 broadcast_in_dim.21
  11.9 10.5 %all-to-all-start = ((f32[128,2,128]{2,1,0:T(2,128)}), f32[128,2,128]{2,1,0:T(2,128)S(1)}, u32[]{:S(2)}, u32[]{:S(2)}) async-start(f32[128,2,128]{2,1,0:T(2,128)} %broadcast_in_dim.21), calls=%async_computation | async-start | bytes 262144 | tf_op jit(solution)/shard_map/all_to_all | solution.py:178
  22.4 0.6 fusion.6
  23.0 0.4 copy.54
  23.4 0.0 copy-start.4
  23.4 1.6 %copy.43 = bf16[9,256,256]{2,1,0:T(8,128)(2,1)S(1)} copy(bf16[9,256,256]{1,2,0:T(8,128)(2,1)} %bitcast.40) | data formatting | bytes 2359296 | tf_op jit(solution)/shard_map/transpose | solution.py:209
  25.1 0.8 %reshape.27 = bf16[3,207,256]{2,1,0:T(8,128)(2,1)} reshape(bf16[9,69,256]{2,1,0:T(8,128)(2,1)S(1)} %bitcast.41) | data formatting | bytes 635904 | tf_op jit(solution)/shard_map/reshape | solution.py:207
  25.9 0.3 pad.16.clone.x_ref
  26.2 0.7 copy-done.3
  26.9 2.3 %copy.49 = bf16[1,512,1024]{1,2,0:T(8,128)(2,1)} copy(bf16[1,512,1024]{2,1,0:T(8,128)(2,1)} %param.8) | data formatting | bytes 2097152 | tf_op args[1]
  29.2 2.3 %copy.50 = bf16[8,512,128]{2,1,0:T(8,128)(2,1)} copy(bf16[8,512,128]{1,2,0:T(8,128)(2,1)} %bitcast.39) | data formatting | bytes 2097152 | tf_op jit(solution)/shard_map/transpose | solution.py:198
  31.5 0.0 copy-done.6
  31.5 0.1 add_convert_fusion.ends_ref
  31.6 0.0 collective-permute-done.1
  31.6 0.0 collective-permute-done
  31.6 5.6 %collective-permute-start.3 = (bf16[36,2,128]{2,0,1:T(8,128)(2,1)S(1)}, bf16[36,2,128]{2,0,1:T(8,128)(2,1)S(1)}, u32[]{:S(2)}, u32[]{:S(2)}) collective-permute-start(bf16[36,2,128]{2,0,1:T(8,128)(2,1)S(1)} %pad_maximum_fusion.1), channel_id=1, source_target_pairs={{1,0},{2,1},{3,2},{4,3},{5,4},{6,5},{7,6},{0,7},{9,8},{10,9},{11,1... | collective-permute-start | bytes 55304 | tf_op jit(solution)/shard_map/ppermute | solution.py:191
  37.3 0.1 collective-permute-start.2
  37.4 6.2 %collective-permute-done.2 = bf16[36,2,128]{2,0,1:T(8,128)(2,1)S(1)} collective-permute-done((bf16[36,2,128]{2,0,1:T(8,128)(2,1)S(1)}, bf16[36,2,128]{2,0,1:T(8,128)(2,1)S(1)}, u32[]{:S(2)}, u32[]{:S(2)}) %collective-permute-start.2) | collective-permute-done | bytes 18464 | tf_op jit(solution)/shard_map/ppermute | solution.py:190
  43.6 0.0 collective-permute-done.3
  43.7 0.0 all-to-all-done
  43.7 0.0 copy-start
  43.7 0.0 copy-start.1
  43.7 6.5 %all-to-all-start.1 = ((bf16[128,32,128]{2,1,0:T(8,128)(2,1)}), bf16[128,32,128]{2,1,0:T(8,128)(2,1)}, u32[]{:S(2)}, u32[]{:S(2)}) async-start(bf16[128,32,128]{2,1,0:T(8,128)(2,1)} %bitcast.38), calls=%async_computation.1 | async-start | bytes 2097152 | tf_op jit(solution)/shard_map/all_to_all | solution.py:200
  50.2 0.1 reduce_sum.29
  50.4 15.9 %convs.1 = bf16[256,32,128]{2,1,0:T(8,128)(2,1)} custom-call(s32[2]{0:T(128)S(1)} %add_convert_fusion.ends_ref, bf16[32,128,128]{2,1,0:T(8,128)(2,1)S(1)} %pad.16.clone.x_ref, bf16[2,128,128]{2,1,0:T(8,128)(2,1)S(1)} %copy.45.top_ref, bf16[2,128,128]{2,1,0:T(8,128)(2,1)S(1)} %copy.46.bottom_ref, bf16[36,2,128]{2,1,0:T(2,128)(2,1)S(1)} %copy.47.left_ref, ...), custom_call_target="tpu_custom_call" | custom-call | flops 6569852928 | bytes 8388608 | tf_op jit(solution)/shard_map/convs/pallas_call | solution.py:140
  66.3 2.5 %all-to-all-done.1 = bf16[128,32,128]{2,1,0:T(8,128)(2,1)} async-done(((bf16[128,32,128]{2,1,0:T(8,128)(2,1)}), bf16[128,32,128]{2,1,0:T(8,128)(2,1)}, u32[]{:S(2)}, u32[]{:S(2)}) %all-to-all-start.1) | async-done | bytes 1048608 | tf_op jit(solution)/shard_map/all_to_all | solution.py:200
  68.8 2.7 %gather_fusion = bf16[69,32,128]{2,1,0:T(8,128)(2,1)} fusion(bf16[128,32,128]{2,1,0:T(8,128)(2,1)} %all-to-all-done.1, s32[1024]{0:T(1024)S(1)} %pad_clamp_fusion), kind=kCustom, calls=%fused_computation | custom fusion | bytes 1130772 | tf_op jit(solution)/shard_map/gather | solution.py:217
  (29 shorter events, 0.2 us)
Async XLA Ops:
  0.6 9.9 %copy-start.2 = (bf16[69,32,128]{2,1,0:T(8,128)(2,1)S(1)}, bf16[69,32,128]{2,1,0:T(8,128)(2,1)}, u32[]{:S(2)}) copy-start(bf16[69,32,128]{2,1,0:T(8,128)(2,1)} %param.7) | copy-start | bytes 1695748
  3.7 27.9 %collective-permute-start.1 = (bf16[2,128,128]{2,0,1:T(2,128)(2,1)}, bf16[2,128,128]{2,0,1:T(2,128)(2,1)S(1)}, u32[]{:S(2)}, u32[]{:S(2)}) collective-permute-start(bf16[2,128,128]{2,0,1:T(2,128)(2,1)} %get-tuple-element.6), channel_id=1, source_target_pairs={{8,0},{16,8},{24,16},{32,24},{40,32},{48,40},{56,48},{64,56},{72,6... | collective-permute-start | bytes 196616 | tf_op jit(solution)/shard_map/ppermute | solution.py:183
  7.0 24.6 %collective-permute-start = (bf16[2,128,128]{2,0,1:T(2,128)(2,1)}, bf16[2,128,128]{2,0,1:T(2,128)(2,1)S(1)}, u32[]{:S(2)}, u32[]{:S(2)}) collective-permute-start(bf16[2,128,128]{2,0,1:T(2,128)(2,1)} %get-tuple-element.7), channel_id=1, source_target_pairs={{0,8},{8,16},{16,24},{24,32},{32,40},{40,48},{48,56},{56,64},{64,7... | collective-permute-start | bytes 196616 | tf_op jit(solution)/shard_map/ppermute | solution.py:182
  11.9 31.8 %all-to-all-start = ((f32[128,2,128]{2,1,0:T(2,128)}), f32[128,2,128]{2,1,0:T(2,128)S(1)}, u32[]{:S(2)}, u32[]{:S(2)}) async-start(f32[128,2,128]{2,1,0:T(2,128)} %broadcast_in_dim.21), calls=%async_computation | async-start | bytes 262144 | tf_op jit(solution)/shard_map/all_to_all | solution.py:178
  23.4 1.6 %copy-start.4 = (bf16[9,256,69]{1,2,0:T(8,128)(2,1)S(1)}, bf16[9,256,69]{1,2,0:T(8,128)(2,1)}, u32[]{:S(2)}) copy-start(bf16[9,256,69]{1,2,0:T(8,128)(2,1)} %param.10) | copy-start | bytes 953860
  25.9 1.0 %copy-start.3 = (bf16[3,207,256]{2,1,0:T(8,128)(2,1)S(1)}, bf16[3,207,256]{2,1,0:T(8,128)(2,1)}, u32[]{:S(2)}) copy-start(bf16[3,207,256]{2,1,0:T(8,128)(2,1)} %reshape.27) | copy-start | bytes 953860
  29.2 2.3 %copy-start.6 = (s32[69]{0:T(128)S(1)}, s32[69]{0:T(128)}, u32[]{:S(2)}) copy-start(s32[69]{0:T(128)} %param.9) | copy-start | bytes 832
  29.2 2.4 %copy-start.5 = (bf16[32,2,128]{2,0,1:T(8,128)(2,1)S(1)}, bf16[32,2,128]{2,0,1:T(8,128)(2,1)}, u32[]{:S(2)}) copy-start(bf16[32,2,128]{2,0,1:T(8,128)(2,1)} %get-tuple-element.4) | copy-start | bytes 49156
  31.6 12.0 %collective-permute-start.3 = (bf16[36,2,128]{2,0,1:T(8,128)(2,1)S(1)}, bf16[36,2,128]{2,0,1:T(8,128)(2,1)S(1)}, u32[]{:S(2)}, u32[]{:S(2)}) collective-permute-start(bf16[36,2,128]{2,0,1:T(8,128)(2,1)S(1)} %pad_maximum_fusion.1), channel_id=1, source_target_pairs={{1,0},{2,1},{3,2},{4,3},{5,4},{6,5},{7,6},{0,7},{9,8},{10,9},{11,1... | collective-permute-start | bytes 55304 | tf_op jit(solution)/shard_map/ppermute | solution.py:191
  37.3 6.3 %collective-permute-start.2 = (bf16[36,2,128]{2,0,1:T(8,128)(2,1)S(1)}, bf16[36,2,128]{2,0,1:T(8,128)(2,1)S(1)}, u32[]{:S(2)}, u32[]{:S(2)}) collective-permute-start(bf16[36,2,128]{2,0,1:T(8,128)(2,1)S(1)} %pad_maximum_fusion), channel_id=1, source_target_pairs={{0,1},{1,2},{2,3},{3,4},{4,5},{5,6},{6,7},{7,0},{8,9},{9,10},{10,1... | collective-permute-start | bytes 55304 | tf_op jit(solution)/shard_map/ppermute | solution.py:190
  43.7 6.7 %copy-start = (f32[256]{0:T(256)S(1)}, f32[256]{0:T(256)}, u32[]{:S(2)}) copy-start(f32[256]{0:T(256)} %param.11) | copy-start | bytes 3076
  43.7 6.7 %copy-start.1 = (f32[256]{0:T(256)S(1)}, f32[256]{0:T(256)}, u32[]{:S(2)}) copy-start(f32[256]{0:T(256)} %param.13) | copy-start | bytes 3076
  43.7 25.1 %all-to-all-start.1 = ((bf16[128,32,128]{2,1,0:T(8,128)(2,1)}), bf16[128,32,128]{2,1,0:T(8,128)(2,1)}, u32[]{:S(2)}, u32[]{:S(2)}) async-start(bf16[128,32,128]{2,1,0:T(8,128)(2,1)} %bitcast.38), calls=%async_computation.1 | async-start | bytes 2097152 | tf_op jit(solution)/shard_map/all_to_all | solution.py:200

commit v2 on v1

v2 whole, which is shorter than its diff:
```python
import functools

import jax
import jax.numpy as jnp
from jax import lax
from jax.experimental import pallas as pl
from jax.experimental.pallas import tpu as pltpu
from jax.sharding import Mesh
from jax.sharding import PartitionSpec as P

LAT = ("lat_0", "lat_1", "lat_2")
LON = ("lon_0", "lon_1")
LANES = 128
BLOCK = 8
GELU_C = 0.7978845608028654


def gelu(v):
    return (0.5 * v) * (1.0 + jnp.tanh(v * (GELU_C + (GELU_C * 0.044715) * (v * v))))


def conv_kernel(
    channels, rows, cols, hid,
    ends_ref, x_ref, top_ref, bottom_ref, left_ref, right_ref, edge_ref, mean_ref, scale_ref,
    w1_raw_ref, b1_ref, w2_raw_ref, b2_ref, out_ref,
    w1_ref, w2_ref, taps_ref, edge_taps_ref, edge_hid_ref, west_ref, mid_ref, east_ref, turned_ref, done_ref, sem,
):
    mean = mean_ref[...]
    scale = scale_ref[...]
    first = ends_ref[0] != 0
    last = ends_ref[1] != 0
    lane = lax.broadcasted_iota(jnp.int32, (cols, LANES), 1)
    sub = lax.broadcasted_iota(jnp.int32, (8, LANES), 0)
    sub_hid = lax.broadcasted_iota(jnp.int32, (8, hid), 0)
    over = 2 * channels - LANES

    def weights():
        group = w1_raw_ref.shape[1]
        for a in range(3):
            for b in range(3):
                w1_ref[a * 2 * LANES + b * group : a * 2 * LANES + (b + 1) * group, :] = w1_raw_ref[3 * a + b]
            w1_ref[a * 2 * LANES + 3 * group : (a + 1) * 2 * LANES, :] = jnp.zeros(
                (2 * LANES - 3 * group, hid), jnp.bfloat16
            )
        for tap in range(9):
            w2_ref[tap * hid : (tap + 1) * hid, :] = w2_raw_ref[tap].T

    def norm(raw):
        return (raw.astype(jnp.float32) - mean) * scale

    def pack(minus, zero, plus, lanes):
        turned = pltpu.roll(zero, channels, axis=1)
        low = jnp.where(lanes < channels, minus, turned)
        high = jnp.where(lanes < over, turned, pltpu.roll(plus, over, axis=1))
        return low, high

    def shifted(main, before, after, sub8):
        minus = pltpu.roll(main, 1, axis=0)
        minus = jnp.concatenate([jnp.where(sub8 == 0, before, minus[:8]), minus[8:]], axis=0)
        plus = pltpu.roll(main, cols - 1, axis=0)
        plus = jnp.concatenate([plus[: cols - 8], jnp.where(sub8 == 7, after, plus[cols - 8 :])], axis=0)
        return minus, plus

    def build(row):
        if row < 2:
            raw, keep = top_ref[row], jnp.logical_not(first)
        elif row >= rows + 2:
            raw, keep = bottom_ref[row - rows - 2], jnp.logical_not(last)
        else:
            raw, keep = x_ref[row - 2], None
        main = norm(raw)
        left = norm(left_ref[row])
        right = norm(right_ref[row])
        if keep is not None:
            main = jnp.where(keep, main, 0.0)
            left = jnp.where(keep, left, 0.0)
            right = jnp.where(keep, right, 0.0)
        minus, plus = shifted(main, left[1:2], right[0:1], sub)
        low, high = pack(minus, main, plus, lane)
        taps_ref[row, :, 0:LANES] = low.astype(jnp.bfloat16)
        taps_ref[row, :, LANES : 2 * LANES] = high.astype(jnp.bfloat16)

    def edges():
        tall = edge_ref.shape[2]
        edge_row = lax.broadcasted_iota(jnp.int32, (tall, LANES), 0)
        edge_lane = lax.broadcasted_iota(jnp.int32, (tall, LANES), 1)
        outside = jnp.logical_or(
            jnp.logical_and(first, edge_row < 2), jnp.logical_and(last, edge_row >= rows + 2)
        )
        hid_row = lax.broadcasted_iota(jnp.int32, (tall - 8, hid), 0)
        hid_outside = jnp.logical_or(
            jnp.logical_and(first, hid_row < 1), jnp.logical_and(last, hid_row >= rows + 1)
        )
        for side in range(2):
            parts = [jnp.where(outside, 0.0, norm(edge_ref[side, b])) for b in range(3)]
            low, high = pack(*parts, edge_lane)
            edge_taps_ref[side, :, 0:LANES] = low
            edge_taps_ref[side, :, LANES : 2 * LANES] = high
            stacked = jnp.concatenate(
                [edge_taps_ref[side, a : a + tall - 8, :].astype(jnp.bfloat16) for a in range(3)], axis=1
            )
            value = jnp.dot(stacked, w1_ref[...], preferred_element_type=jnp.float32) + b1_ref[...]
            edge_hid_ref[side] = jnp.where(hid_outside, 0.0, gelu(value))

    def hidden(row, count):
        stacked = jnp.concatenate(
            [taps_ref[row + a : row + a + count].reshape(count * cols, 2 * LANES) for a in range(3)], axis=1
        )
        value = jnp.dot(stacked, w1_ref[...], preferred_element_type=jnp.float32)
        for i in range(count):
            r = row + i
            one = gelu(value[i * cols : (i + 1) * cols] + b1_ref[...])
            if r == 0:
                one = jnp.where(first, 0.0, one)
            elif r == rows + 1:
                one = jnp.where(last, 0.0, one)
            west, east = shifted(one, edge_hid_ref[0, r : r + 1, :], edge_hid_ref[1, r : r + 1, :], sub_hid)
            west_ref[r] = west.astype(jnp.bfloat16)
            mid_ref[r] = one.astype(jnp.bfloat16)
            east_ref[r] = east.astype(jnp.bfloat16)

    def put(t):
        return pltpu.make_async_copy(
            done_ref.at[t], out_ref.at[:, t * BLOCK : (t + 1) * BLOCK, :], sem.at[t]
        )

    def features(t):
        base = t * BLOCK
        stacked = jnp.concatenate(
            [
                ref[base + a : base + a + BLOCK].reshape(BLOCK * cols, hid)
                for a in range(3)
                for ref in (west_ref, mid_ref, east_ref)
            ],
            axis=1,
        )
        value = jnp.dot(stacked, w2_ref[...], preferred_element_type=jnp.float32) + b2_ref[...]
        for i in range(BLOCK):
            turned_ref[t % 2, pl.ds(i, hid, stride=BLOCK), :] = value[i * cols : (i + 1) * cols].T
        done_ref[t] = turned_ref[t % 2].reshape(hid, BLOCK, cols).astype(jnp.bfloat16)
        put(t).start()

    steps = rows // BLOCK
    weights()
    for r in range(BLOCK + 4):
        build(r)
    edges()
    hidden(0, BLOCK + 2)
    for r in range(BLOCK + 4, 2 * BLOCK + 4):
        build(r)
    for t in range(steps):
        if t + 2 < steps:
            for r in range((t + 2) * BLOCK + 4, (t + 3) * BLOCK + 4):
                build(r)
        if t + 1 < steps:
            hidden((t + 1) * BLOCK + 2, BLOCK)
        features(t)
    for t in range(steps):
        put(t).wait()


def convs(ends, x, top, bottom, left, right, edge, mean, scale, w1, b1, w2, b2):
    rows, cols = x.shape[0], x.shape[1]
    hid = w2.shape[1]
    channels = w1.shape[1]
    tall = edge.shape[2]
    vmem = pl.BlockSpec(memory_space=pltpu.VMEM)
    flops = 2 * hid * (rows * cols * 9 * hid + (rows + 2) * (cols + 2) * 3 * 256)
    return pl.pallas_call(
        functools.partial(conv_kernel, channels, rows, cols, hid),
        out_shape=jax.ShapeDtypeStruct((hid, rows, cols), jnp.bfloat16),
        in_specs=[pl.BlockSpec(memory_space=pltpu.SMEM)] + [vmem] * 12,
        out_specs=pl.BlockSpec(memory_space=pl.ANY),
        scratch_shapes=[
            pltpu.VMEM((6 * LANES, hid), jnp.bfloat16),
            pltpu.VMEM((9 * hid, hid), jnp.bfloat16),
            pltpu.VMEM((rows + 4, cols, 2 * LANES), jnp.bfloat16),
            pltpu.VMEM((2, tall, 2 * LANES), jnp.float32),
            pltpu.VMEM((2, tall - 8, hid), jnp.float32),
            pltpu.VMEM((rows + 2, cols, hid), jnp.bfloat16),
            pltpu.VMEM((rows + 2, cols, hid), jnp.bfloat16),
            pltpu.VMEM((rows + 2, cols, hid), jnp.bfloat16),
            pltpu.VMEM((2, hid * BLOCK, cols), jnp.float32),
            pltpu.VMEM((rows // BLOCK, hid, BLOCK, cols), jnp.bfloat16),
            pltpu.SemaphoreType.DMA((rows // BLOCK,)),
        ],
        compiler_params=pltpu.CompilerParams(vmem_limit_bytes=48 * 2**20),
        cost_estimate=pl.CostEstimate(flops=flops, bytes_accessed=8 * 2**20, transcendentals=0),
        name="convs",
    )(ends, x, top, bottom, left, right, edge, mean, scale, w1, b1, w2, b2)


def prepare_kernel(
    channels, odd_ref, x_ref, fields_ref,
    turned_ref, spread_ref, one_ref, two_ref, west_ref, east_ref, blocks_ref,
    wide_ref, sem,
):
    rows, cols = turned_ref.shape[0], turned_ref.shape[1]
    count = blocks_ref.shape[0]

    def get(j):
        return pltpu.make_async_copy(
            fields_ref.at[0, :, j * cols : (j + 1) * cols], blocks_ref.at[j], sem.at[j]
        )

    for j in range(count):
        get(j).start()
    padded = wide_ref.shape[0] // rows
    wide_ref[0 : channels * rows, :] = x_ref[...].astype(jnp.float32).reshape(channels * rows, cols)
    wide_ref[channels * rows :, :] = jnp.zeros(((padded - channels) * rows, cols), jnp.float32)
    rest = jnp.zeros((LANES - padded, cols), jnp.float32)
    total = jnp.zeros((padded, cols), jnp.float32)
    square = jnp.zeros((padded, cols), jnp.float32)
    for r in range(rows):
        one = wide_ref[pl.ds(r, padded, stride=rows), :]
        total += one
        square += one * one
        turned = jnp.concatenate([one, rest], axis=0).T.astype(jnp.bfloat16)
        turned_ref[r] = turned
        west_ref[r] = turned[:2]
        east_ref[r] = turned[cols - 2 :]
    odd = odd_ref[0] != 0
    low = turned_ref[0:2]
    high = turned_ref[rows - 2 : rows]
    one_ref[...] = jnp.where(odd, low, high)
    two_ref[...] = jnp.where(odd, high, low)

    def sums(value):
        return jnp.sum(jnp.concatenate([value, rest], axis=0).T, axis=0, keepdims=True)

    both = jnp.concatenate([sums(total), sums(square)], axis=0)
    spread_ref[...] = jnp.broadcast_to(both[None], spread_ref.shape)
    for j in range(count):
        get(j).wait()


def prepare(odd, current, next_fields, devices, n_lon):
    channels, rows, cols = current.shape
    vmem = pl.BlockSpec(memory_space=pltpu.VMEM)
    height = next_fields.shape[1]
    padded = (channels + 7) // 8 * 8
    return pl.pallas_call(
        functools.partial(prepare_kernel, channels),
        out_shape=(
            jax.ShapeDtypeStruct((rows, cols, LANES), jnp.bfloat16),
            jax.ShapeDtypeStruct((devices, 2, LANES), jnp.float32),
            jax.ShapeDtypeStruct((2, cols, LANES), jnp.bfloat16),
            jax.ShapeDtypeStruct((2, cols, LANES), jnp.bfloat16),
            jax.ShapeDtypeStruct((rows, 2, LANES), jnp.bfloat16),
            jax.ShapeDtypeStruct((rows, 2, LANES), jnp.bfloat16),
            jax.ShapeDtypeStruct((n_lon, height, cols), jnp.bfloat16),
        ),
        in_specs=[pl.BlockSpec(memory_space=pltpu.SMEM), vmem, pl.BlockSpec(memory_space=pltpu.HBM)],
        out_specs=(vmem,) * 7,
        scratch_shapes=[
            pltpu.VMEM((padded * rows, cols), jnp.float32),
            pltpu.SemaphoreType.DMA((n_lon,)),
        ],
        compiler_params=pltpu.CompilerParams(vmem_limit_bytes=32 * 2**20),
        cost_estimate=pl.CostEstimate(flops=2**24, bytes_accessed=2**22, transcendentals=0),
        name="prepare",
    )(odd, current, next_fields)


def pairs(count, periodic):
    near = [(i, i ^ 1) for i in range(count)]
    far = [(i, i + 1 if i % 2 else i - 1) for i in range(count)]
    if periodic:
        far = [(a, b % count) for a, b in far]
    else:
        far = [(a, b) for a, b in far if 0 <= b < count]
    return near, far


def body(current, next_fields, reader_slot, first_weight, first_bias, second_weight, second_bias):
    channels, rows, cols = current.shape
    n_lat = lax.axis_size(LAT)
    n_lon = lax.axis_size(LON)
    cells = rows * n_lat * cols * n_lon
    at_lat = lax.axis_index(LAT)
    odd_lat = at_lat % 2 == 1
    odd_lon = lax.axis_index(LON) % 2 == 1

    turned, spread, one, two, west, east, blocks = prepare(
        odd_lat.astype(jnp.int32)[None], current, next_fields, n_lat * n_lon, n_lon
    )

    near, far = pairs(n_lat, False)
    one = lax.ppermute(one, LAT, near)
    two = lax.ppermute(two, LAT, far)
    gathered = lax.all_to_all(spread, LON + LAT, split_axis=0, concat_axis=0, tiled=True)
    top = jnp.where(odd_lat, one, two)
    bottom = jnp.where(odd_lat, two, one)
    first_cols = jnp.concatenate([top[:, :2], west, bottom[:, :2]], axis=0)
    last_cols = jnp.concatenate([top[:, cols - 2 :], east, bottom[:, cols - 2 :]], axis=0)
    near, far = pairs(n_lon, True)
    one = lax.ppermute(jnp.where(odd_lon, first_cols, last_cols), LON, near)
    two = lax.ppermute(jnp.where(odd_lon, last_cols, first_cols), LON, far)
    left = jnp.where(odd_lon, one, two)
    right = jnp.where(odd_lon, two, one)
    edge = jnp.stack([
        jnp.stack([left[:, 0], left[:, 1], first_cols[:, 0]]),
        jnp.stack([last_cols[:, 1], right[:, 0], right[:, 1]]),
    ])
    edge = jnp.pad(edge, ((0, 0), (0, 0), (0, 48 - rows - 4), (0, 0)))

    moved = lax.all_to_all(
        blocks.reshape(n_lon * n_lat, rows, cols), LON + LAT, split_axis=0, concat_axis=0, tiled=True
    )

    total = jnp.sum(gathered, axis=0)
    mean = total[0] / cells
    scale = 1.0 / jnp.sqrt(total[1] / cells - mean * mean + 1e-05)
    scale = jnp.where(jnp.arange(LANES) < channels, scale, 0.0)

    w1 = jnp.pad(first_weight.transpose(0, 2, 1), ((0, 0), (0, -channels % 8), (0, 0)))
    ends = jnp.stack([at_lat == 0, at_lat == n_lat - 1]).astype(jnp.int32)
    features = convs(
        ends, turned, top, bottom, left, right, edge, mean[None], scale[None],
        w1, first_bias[None], second_weight, second_bias[None],
    )
    place = (reader_slot % n_lon) * n_lat + reader_slot // n_lon
    next_tile = moved.at[place].get(mode="promise_in_bounds")
    return (features, next_tile)


def solution(mesh):
    split = Mesh(mesh.devices.reshape(4, 2, 2, 2, 4), ("lat_0", "lat_1", "lat_2", "lon_0", "lon_1"))
    return jax.shard_map(
        body,
        mesh=split,
        in_specs=(P(None, LAT, LON), P(LAT + LON, None, None), P(), P(), P(), P(), P()),
        out_specs=(P(None, LAT, LON), P(None, LAT, LON)),
        check_vma=False,
    )
```

time: 71.9 us -> 62.7 us (0.87)
  local copies, waits for them, and re-layouts: 15.5 us -> 5.26 us
  waiting for transfers between devices: 8.7 us -> 13.1 us
  Pallas kernels: 15.9 us -> 12.4 us
  starting transfers between devices: 29.6 us -> 30.4 us
    pallas_call x1, Pallas kernels: 15.9 us -> 10 us  [convs(): pl.pallas_call(functools.partial(conv_kernel, channels, rows, cols, hid),...]
    all_to_all x1, waiting for transfers between devices: 2.51 us -> 8.31 us  [body(): lax.all_to_all(blocks.reshape(n_lon * n_lat, rows, cols), LON + LAT, spli...]
    transpose x2 -> x0, local copies, waits for them, and re-layouts: 3.91 us -> none  [the longest x1 2.29 us: body(): blocks = next_fields.reshape(rows * n_lat, n_lon, cols).transpose(1, 0, 2)]
    ppermute x4, starting transfers between devices: 12.5 us -> 9.1 us  [the longest x1 5.35 us: body(): two = lax.ppermute(jnp.where(odd_lon, last_cols, first_cols), LON, far)]
    all_to_all x1, starting transfers between devices: 6.48 us -> 9.84 us  [body(): lax.all_to_all(blocks.reshape(n_lon * n_lat, rows, cols), LON + LAT, spli...]
    unnamed x17 -> x14, local copies, waits for them, and re-layouts: 5.62 us -> 2.3 us
    pallas_call x0 -> x1, Pallas kernels: none -> 2.33 us  [prepare(): pl.pallas_call(functools.partial(prepare_kernel, channels), out_shape=(ja...]
    ppermute x4, waiting for transfers between devices: 6.19 us -> 4.75 us  [the longest x1 2.15 us: body(): two = lax.ppermute(two, LAT, far)]
  transfers between devices with their start and end apart: 6 -> 6, of which waited for: 2 -> 4; matrix products, arithmetic and copies ran while one was open for 14% -> 1% of each run, Pallas kernels for 22% -> 16%
where the time goes in v2:
time: 62.7 us; the launch traced here: 62.4 us
  starting transfers between devices  30.4 us (48%)
  waiting for transfers between devices  13.1 us (21%)
  Pallas kernels  12.4 us (20%)
  local copies, waits for them, and re-layouts  5.26 us (8%)
  between operations  0.95 us (2%)
    all_to_all x1, starting transfers between devices, body(): lax.all_to_all(spread, LON + LAT, split_axis=0, concat_axis=0, tiled=True)  11.5 us
    pallas_call x1, Pallas kernels, convs(): pl.pallas_call(functools.partial(conv_kernel, channels, rows, cols, hid),...  10 us
    all_to_all x1, starting transfers between devices, body(): lax.all_to_all(blocks.reshape(n_lon * n_lat, rows, cols), LON + LAT, spli...  9.84 us
    all_to_all x1, waiting for transfers between devices, body(): lax.all_to_all(blocks.reshape(n_lon * n_lat, rows, cols), LON + LAT, spli...  8.31 us
    ppermute x1, starting transfers between devices, body(): two = lax.ppermute(jnp.where(odd_lon, last_cols, first_cols), LON, far)  5.35 us
    ppermute x1, starting transfers between devices, body(): two = lax.ppermute(two, LAT, far)  3.66 us
    gather x1, local copies, waits for them, and re-layouts, body(): next_tile = moved.at[place].get(mode='promise_in_bounds')  2.7 us
    pallas_call x1, Pallas kernels, prepare(): pl.pallas_call(functools.partial(prepare_kernel, channels), out_shape=(ja...  2.33 us
  transfers between devices with their start and end apart: 6, of which 4 were waited for; matrix products, arithmetic and copies ran while one was open for 1% of the time, Pallas kernels for 16%

profile of v2, /device:TPU:1, one launch (start us, length us, event | category | flops | bytes accessed | tf_op | source)
XLA Modules:
  0.0 62.4 jit_solution(5890660751844651548)
XLA Ops:
  0.6 0.0 copy-start.6
  0.7 0.0 copy-start
  0.7 1.2 %copy-done = bf16[1,512,1024]{2,1,0:T(8,128)(2,1)S(1)} copy-done((bf16[1,512,1024]{2,1,0:T(8,128)(2,1)S(1)}, bf16[1,512,1024]{2,1,0:T(8,128)(2,1)}, u32[]{:S(2)}) %copy-start) | copy-done | bytes 1048600
  1.9 1.1 %copy-done.1 = bf16[69,32,128]{2,1,0:T(8,128)(2,1)S(1)} copy-done((bf16[69,32,128]{2,1,0:T(8,128)(2,1)S(1)}, bf16[69,32,128]{2,1,0:T(8,128)(2,1)}, u32[]{:S(2)}) %copy-start.1) | copy-done | bytes 565272
  2.9 0.0 copy-start.5
  2.9 2.3 %prepare.1 = (bf16[32,128,128]{2,1,0:T(8,128)(2,1)S(1)}, f32[128,2,128]{2,1,0:T(2,128)}, bf16[2,128,128]{2,1,0:T(8,128)(2,1)S(1)}, bf16[2,128,128]{2,1,0:T(8,128...) custom-call(s32[1]{0:T(128)} %bitcast.2.odd_ref, ...), custom_call_target="tpu_custom_call" | custom-call | flops 16777216 | bytes 4194304 | tf_op jit(solution)/shard_map/prepare/pallas_call | solution.py:242
  5.3 11.5 %all-to-all-start = ((f32[128,2,128]{2,1,0:T(2,128)}), f32[128,2,128]{2,1,0:T(2,128)S(1)}, u32[]{:S(2)}, u32[]{:S(2)}) async-start(f32[128,2,128]{2,1,0:T(2,128)} %get-tuple-element.14), calls=%async_computation | async-start | bytes 262144 | tf_op jit(solution)/shard_map/all_to_all | solution.py:291
  16.8 0.1 copy.18
  16.9 3.7 %collective-permute-start.1 = (bf16[2,128,128]{2,0,1:T(2,128)(2,1)S(1)}, bf16[2,128,128]{2,0,1:T(2,128)(2,1)S(1)}, u32[]{:S(2)}, u32[]{:S(2)}) collective-permute-start(bf16[2,128,128]{2,0,1:T(2,128)(2,1)S(1)} %copy.18), channel_id=1, source_target_pairs={{8,16},{16,8},{24,32},{32,24},{40,48},{48,40},{56,64},{64,56},{72,... | collective-permute-start | bytes 196616 | tf_op jit(solution)/shard_map/ppermute | solution.py:290
  20.5 0.1 copy.17
  20.6 0.1 collective-permute-start
  20.7 0.0 copy-done.6
  20.8 0.0 copy-start.2
  20.8 0.0 copy-start.3
  20.8 0.0 copy-start.4
  20.8 0.0 copy-done.5
  20.9 0.1 add_convert_fusion.ends_ref
  20.9 2.2 %collective-permute-done.1 = bf16[2,128,128]{2,0,1:T(2,128)(2,1)S(1)} collective-permute-done((bf16[2,128,128]{2,0,1:T(2,128)(2,1)S(1)}, bf16[2,128,128]{2,0,1:T(2,128)(2,1)S(1)}, u32[]{:S(2)}, u32[]{:S(2)}) %collective-permute-start.1) | collective-permute-done | bytes 65568 | tf_op jit(solution)/shard_map/ppermute | solution.py:290
  23.1 0.0 collective-permute-done
  23.2 5.3 %collective-permute-start.3 = (bf16[36,2,128]{2,0,1:T(8,128)(2,1)S(1)}, bf16[36,2,128]{2,0,1:T(8,128)(2,1)S(1)}, u32[]{:S(2)}, u32[]{:S(2)}) collective-permute-start(bf16[36,2,128]{2,0,1:T(8,128)(2,1)S(1)} %get-tuple-element.24), channel_id=1, source_target_pairs={{0,7},{1,2},{2,1},{3,4},{4,3},{5,6},{6,5},{7,0},{8,15},{9,10},{10,... | collective-permute-start | bytes 55304 | tf_op jit(solution)/shard_map/ppermute | solution.py:298
  28.5 0.0 collective-permute-start.2
  28.6 1.1 %collective-permute-done.3 = bf16[36,2,128]{2,0,1:T(8,128)(2,1)S(1)} collective-permute-done((bf16[36,2,128]{2,0,1:T(8,128)(2,1)S(1)}, bf16[36,2,128]{2,0,1:T(8,128)(2,1)S(1)}, u32[]{:S(2)}, u32[]{:S(2)}) %collective-permute-start.3) | collective-permute-done | bytes 18464 | tf_op jit(solution)/shard_map/ppermute | solution.py:298
  29.7 1.5 %collective-permute-done.2 = bf16[36,2,128]{2,0,1:T(8,128)(2,1)S(1)} collective-permute-done((bf16[36,2,128]{2,0,1:T(8,128)(2,1)S(1)}, bf16[36,2,128]{2,0,1:T(8,128)(2,1)S(1)}, u32[]{:S(2)}, u32[]{:S(2)}) %collective-permute-start.2) | collective-permute-done | bytes 18464 | tf_op jit(solution)/shard_map/ppermute | solution.py:297
  31.3 0.0 all-to-all-done
  31.3 9.8 %all-to-all-start.1 = ((bf16[128,32,128]{2,1,0:T(8,128)(2,1)}), bf16[128,32,128]{2,1,0:T(8,128)(2,1)}, u32[]{:S(2)}, u32[]{:S(2)}) async-start(bf16[128,32,128]{2,1,0:T(8,128)(2,1)} %bitcast.14), calls=%async_computation.1 | async-start | bytes 2097152 | tf_op jit(solution)/shard_map/all_to_all | solution.py:307
  41.2 0.1 reduce_sum.9
  41.3 0.0 copy-done.2
  41.3 0.0 copy-done.3
  41.3 0.0 copy-done.4
  41.3 10.0 %convs.1 = bf16[256,32,128]{2,1,0:T(8,128)(2,1)} custom-call(s32[2]{0:T(128)S(1)} %add_convert_fusion.ends_ref, bf16[32,128,128]{2,1,0:T(8,128)(2,1)S(1)} %get-tuple-element.9.x_ref, bf16[2,128,128]{2,1,0:T(8,128)(2,1)S(1)} %copy.21.top_ref, bf16[2,128,128]{2,1,0:T(8,128)(2,1)S(1)} %copy.22.bottom_ref, bf16[36,2,128]{2,1,0:T(2,128)(2,1)S(1)} %copy.23.left_ref, ...), custom_call_target="tpu_custom_call" | custom-call | flops 6569852928 | bytes 8388608 | tf_op jit(solution)/shard_map/convs/pallas_call | solution.py:169
  51.4 8.3 %all-to-all-done.1 = bf16[128,32,128]{2,1,0:T(8,128)(2,1)} async-done(((bf16[128,32,128]{2,1,0:T(8,128)(2,1)}), bf16[128,32,128]{2,1,0:T(8,128)(2,1)}, u32[]{:S(2)}, u32[]{:S(2)}) %all-to-all-start.1) | async-done | bytes 1048608 | tf_op jit(solution)/shard_map/all_to_all | solution.py:307
  59.7 2.7 %gather_fusion = bf16[69,32,128]{2,1,0:T(8,128)(2,1)} fusion(bf16[128,32,128]{2,1,0:T(8,128)(2,1)} %all-to-all-done.1, s32[1024]{0:T(1024)S(1)} %pad_clamp_fusion), kind=kCustom, calls=%fused_computation | custom fusion | bytes 1130772 | tf_op jit(solution)/shard_map/gather | solution.py:323
  (22 shorter events, 0.2 us)
Async XLA Ops:
  0.6 20.1 %copy-start.6 = (s32[69]{0:T(128)S(1)}, s32[69]{0:T(128)}, u32[]{:S(2)}) copy-start(s32[69]{0:T(128)} %param.9) | copy-start | bytes 832
  0.7 1.2 %copy-start = (bf16[1,512,1024]{2,1,0:T(8,128)(2,1)S(1)}, bf16[1,512,1024]{2,1,0:T(8,128)(2,1)}, u32[]{:S(2)}) copy-start(bf16[1,512,1024]{2,1,0:T(8,128)(2,1)} %fields_ref.1) | copy-start | bytes 3145732
  1.9 1.1 %copy-start.1 = (bf16[69,32,128]{2,1,0:T(8,128)(2,1)S(1)}, bf16[69,32,128]{2,1,0:T(8,128)(2,1)}, u32[]{:S(2)}) copy-start(bf16[69,32,128]{2,1,0:T(8,128)(2,1)} %x_ref.1) | copy-start | bytes 1695748
  2.9 17.9 %copy-start.5 = (bf16[9,256,69]{1,2,0:T(8,128)(2,1)S(1)}, bf16[9,256,69]{1,2,0:T(8,128)(2,1)}, u32[]{:S(2)}) copy-start(bf16[9,256,69]{1,2,0:T(8,128)(2,1)} %param.10) | copy-start | bytes 953860
  5.3 26.0 %all-to-all-start = ((f32[128,2,128]{2,1,0:T(2,128)}), f32[128,2,128]{2,1,0:T(2,128)S(1)}, u32[]{:S(2)}, u32[]{:S(2)}) async-start(f32[128,2,128]{2,1,0:T(2,128)} %get-tuple-element.14), calls=%async_computation | async-start | bytes 262144 | tf_op jit(solution)/shard_map/all_to_all | solution.py:291
  16.9 6.2 %collective-permute-start.1 = (bf16[2,128,128]{2,0,1:T(2,128)(2,1)S(1)}, bf16[2,128,128]{2,0,1:T(2,128)(2,1)S(1)}, u32[]{:S(2)}, u32[]{:S(2)}) collective-permute-start(bf16[2,128,128]{2,0,1:T(2,128)(2,1)S(1)} %copy.18), channel_id=1, source_target_pairs={{8,16},{16,8},{24,32},{32,24},{40,48},{48,40},{56,64},{64,56},{72,... | collective-permute-start | bytes 196616 | tf_op jit(solution)/shard_map/ppermute | solution.py:290
  20.6 2.5 %collective-permute-start = (bf16[2,128,128]{2,0,1:T(2,128)(2,1)S(1)}, bf16[2,128,128]{2,0,1:T(2,128)(2,1)S(1)}, u32[]{:S(2)}, u32[]{:S(2)}) collective-permute-start(bf16[2,128,128]{2,0,1:T(2,128)(2,1)S(1)} %copy.17), channel_id=1, source_target_pairs={{0,8},{8,0},{16,24},{24,16},{32,40},{40,32},{48,56},{56,48},{64,72... | collective-permute-start | bytes 196616 | tf_op jit(solution)/shard_map/ppermute | solution.py:289
  20.8 20.5 %copy-start.2 = (bf16[9,256,256]{2,1,0:T(8,128)(2,1)S(1)}, bf16[9,256,256]{2,1,0:T(8,128)(2,1)}, u32[]{:S(2)}) copy-start(bf16[9,256,256]{2,1,0:T(8,128)(2,1)} %w2_raw_ref.1) | copy-start | bytes 3538948
  20.8 20.5 %copy-start.3 = (f32[256]{0:T(256)S(1)}, f32[256]{0:T(256)}, u32[]{:S(2)}) copy-start(f32[256]{0:T(256)} %param.11) | copy-start | bytes 3076
  20.8 20.5 %copy-start.4 = (f32[256]{0:T(256)S(1)}, f32[256]{0:T(256)}, u32[]{:S(2)}) copy-start(f32[256]{0:T(256)} %param.13) | copy-start | bytes 3076
  23.2 6.5 %collective-permute-start.3 = (bf16[36,2,128]{2,0,1:T(8,128)(2,1)S(1)}, bf16[36,2,128]{2,0,1:T(8,128)(2,1)S(1)}, u32[]{:S(2)}, u32[]{:S(2)}) collective-permute-start(bf16[36,2,128]{2,0,1:T(8,128)(2,1)S(1)} %get-tuple-element.24), channel_id=1, source_target_pairs={{0,7},{1,2},{2,1},{3,4},{4,3},{5,6},{6,5},{7,0},{8,15},{9,10},{10,... | collective-permute-start | bytes 55304 | tf_op jit(solution)/shard_map/ppermute | solution.py:298
  28.5 2.6 %collective-permute-start.2 = (bf16[36,2,128]{2,0,1:T(8,128)(2,1)S(1)}, bf16[36,2,128]{2,0,1:T(8,128)(2,1)S(1)}, u32[]{:S(2)}, u32[]{:S(2)}) collective-permute-start(bf16[36,2,128]{2,0,1:T(8,128)(2,1)S(1)} %get-tuple-element.25), channel_id=1, source_target_pairs={{0,1},{1,0},{2,3},{3,2},{4,5},{5,4},{6,7},{7,6},{8,9},{9,8},{10,11... | collective-permute-start | bytes 55304 | tf_op jit(solution)/shard_map/ppermute | solution.py:297
  31.3 28.4 %all-to-all-start.1 = ((bf16[128,32,128]{2,1,0:T(8,128)(2,1)}), bf16[128,32,128]{2,1,0:T(8,128)(2,1)}, u32[]{:S(2)}, u32[]{:S(2)}) async-start(bf16[128,32,128]{2,1,0:T(8,128)(2,1)} %bitcast.14), calls=%async_computation.1 | async-start | bytes 2097152 | tf_op jit(solution)/shard_map/all_to_all | solution.py:307

commit v3 on v2

--- a/solution.py
+++ b/solution.py
@@ -12,6 +12,7 @@
 LON = ("lon_0", "lon_1")
 LANES = 128
 BLOCK = 8
+EXTRA = 8
 GELU_C = 0.7978845608028654
 
 
@@ -21,12 +22,12 @@
 
 def conv_kernel(
     channels, rows, cols, hid,
-    ends_ref, x_ref, top_ref, bottom_ref, left_ref, right_ref, edge_ref, mean_ref, scale_ref,
-    w1_raw_ref, b1_ref, w2_raw_ref, b2_ref, out_ref,
+    ends_ref, place_ref, x_ref, top_ref, bottom_ref, left_ref, right_ref, edge_ref,
+    w1_raw_ref, b1_ref, w2_raw_ref, b2_ref, moved_ref, out_ref, tile_ref,
     w1_ref, w2_ref, taps_ref, edge_taps_ref, edge_hid_ref, west_ref, mid_ref, east_ref, turned_ref, done_ref, sem,
+    held_ref, sums_ref, take_sem,
 ):
-    mean = mean_ref[...]
-    scale = scale_ref[...]
+    cells = rows * cols * moved_ref.shape[0]
     first = ends_ref[0] != 0
     last = ends_ref[1] != 0
     lane = lax.broadcasted_iota(jnp.int32, (cols, LANES), 1)
@@ -141,7 +142,21 @@
         put(t).start()
 
     steps = rows // BLOCK
+    taken = held_ref.shape[0]
+    load_sums = pltpu.make_async_copy(moved_ref.at[:, rows : rows + EXTRA, :], sums_ref, take_sem.at[2])
+    load_sums.start()
+
+    @pl.loop(0, taken)
+    def _(c):
+        pltpu.make_async_copy(moved_ref.at[place_ref[c], 0:rows, :], held_ref.at[c], take_sem.at[0]).start()
+
     weights()
+    load_sums.wait()
+    sums = jnp.sum(sums_ref[...].astype(jnp.float32), axis=0)
+    mean = (sums[0:1] + sums[1:2] + sums[2:3]) / cells
+    square = (sums[3:4] + sums[4:5] + sums[5:6]) / cells
+    scale = 1.0 / jnp.sqrt(square - mean * mean + 1e-05)
+    scale = jnp.where(lax.broadcasted_iota(jnp.int32, (1, LANES), 1) < channels, scale, 0.0)
     for r in range(BLOCK + 4):
         build(r)
     edges()
@@ -155,22 +170,31 @@
         if t + 1 < steps:
             hidden((t + 1) * BLOCK + 2, BLOCK)
         features(t)
+        if t == 1:
+            pltpu.make_async_copy(moved_ref.at[0:taken, 0:rows, :], held_ref, take_sem.at[0]).wait()
+            pltpu.make_async_copy(held_ref, tile_ref, take_sem.at[1]).start()
+    pltpu.make_async_copy(held_ref, tile_ref, take_sem.at[1]).wait()
     for t in range(steps):
         put(t).wait()
 
 
-def convs(ends, x, top, bottom, left, right, edge, mean, scale, w1, b1, w2, b2):
+def convs(ends, place, x, top, bottom, left, right, edge, w1, b1, w2, b2, moved):
     rows, cols = x.shape[0], x.shape[1]
     hid = w2.shape[1]
     channels = w1.shape[1]
+    taken = place.shape[0]
     tall = edge.shape[2]
     vmem = pl.BlockSpec(memory_space=pltpu.VMEM)
+    smem = pl.BlockSpec(memory_space=pltpu.SMEM)
     flops = 2 * hid * (rows * cols * 9 * hid + (rows + 2) * (cols + 2) * 3 * 256)
     return pl.pallas_call(
         functools.partial(conv_kernel, channels, rows, cols, hid),
-        out_shape=jax.ShapeDtypeStruct((hid, rows, cols), jnp.bfloat16),
-        in_specs=[pl.BlockSpec(memory_space=pltpu.SMEM)] + [vmem] * 12,
-        out_specs=pl.BlockSpec(memory_space=pl.ANY),
+        out_shape=(
+            jax.ShapeDtypeStruct((hid, rows, cols), jnp.bfloat16),
+            jax.ShapeDtypeStruct((taken, rows, cols), jnp.bfloat16),
+        ),
+        in_specs=[smem, smem] + [vmem] * 10 + [pl.BlockSpec(memory_space=pl.ANY)],
+        out_specs=(pl.BlockSpec(memory_space=pl.ANY),) * 2,
         scratch_shapes=[
             pltpu.VMEM((6 * LANES, hid), jnp.bfloat16),
             pltpu.VMEM((9 * hid, hid), jnp.bfloat16),
@@ -183,34 +207,46 @@
             pltpu.VMEM((2, hid * BLOCK, cols), jnp.float32),
             pltpu.VMEM((rows // BLOCK, hid, BLOCK, cols), jnp.bfloat16),
             pltpu.SemaphoreType.DMA((rows // BLOCK,)),
+            pltpu.VMEM((taken, rows, cols), jnp.bfloat16),
+            pltpu.VMEM((moved.shape[0], EXTRA, cols), jnp.bfloat16),
+            pltpu.SemaphoreType.DMA((3,)),
         ],
         compiler_params=pltpu.CompilerParams(vmem_limit_bytes=48 * 2**20),
         cost_estimate=pl.CostEstimate(flops=flops, bytes_accessed=8 * 2**20, transcendentals=0),
         name="convs",
-    )(ends, x, top, bottom, left, right, edge, mean, scale, w1, b1, w2, b2)
+    )(ends, place, x, top, bottom, left, right, edge, w1, b1, w2, b2, moved)
 
 
 def prepare_kernel(
     channels, odd_ref, x_ref, fields_ref,
-    turned_ref, spread_ref, one_ref, two_ref, west_ref, east_ref, blocks_ref,
-    wide_ref, sem,
+    turned_ref, one_ref, two_ref, west_ref, east_ref, blocks_ref,
+    raw_ref, wide_ref, held_ref, sums_ref, x_sem, in_sem, out_sem, sums_sem,
 ):
     rows, cols = turned_ref.shape[0], turned_ref.shape[1]
-    count = blocks_ref.shape[0]
+    count = held_ref.shape[0]
 
     def get(j):
+        return pltpu.make_async_copy(fields_ref.at[0, :, j * cols : (j + 1) * cols], held_ref.at[j], in_sem.at[j])
+
+    def put(j):
         return pltpu.make_async_copy(
-            fields_ref.at[0, :, j * cols : (j + 1) * cols], blocks_ref.at[j], sem.at[j]
-        )
-
+            held_ref.at[j].reshape(held_ref.shape[1] // rows, rows, cols), blocks_ref.at[j, :, 0:rows, :], out_sem.at[j]
+        )
+
+    def put_sums(j):
+        return pltpu.make_async_copy(sums_ref, blocks_ref.at[j, :, rows : rows + EXTRA, :], sums_sem.at[j])
+
+    load = pltpu.make_async_copy(x_ref, raw_ref, x_sem)
+    load.start()
     for j in range(count):
         get(j).start()
     padded = wide_ref.shape[0] // rows
-    wide_ref[0 : channels * rows, :] = x_ref[...].astype(jnp.float32).reshape(channels * rows, cols)
     wide_ref[channels * rows :, :] = jnp.zeros(((padded - channels) * rows, cols), jnp.float32)
     rest = jnp.zeros((LANES - padded, cols), jnp.float32)
     total = jnp.zeros((padded, cols), jnp.float32)
     square = jnp.zeros((padded, cols), jnp.float32)
+    load.wait()
+    wide_ref[0 : channels * rows, :] = raw_ref[...].astype(jnp.float32).reshape(channels * rows, cols)
     for r in range(rows):
         one = wide_ref[pl.ds(r, padded, stride=rows), :]
         total += one
@@ -219,44 +255,62 @@
         turned_ref[r] = turned
         west_ref[r] = turned[:2]
         east_ref[r] = turned[cols - 2 :]
+        if r % 4 == 3:
+            get(r // 4).wait()
+            put(r // 4).start()
     odd = odd_ref[0] != 0
     low = turned_ref[0:2]
     high = turned_ref[rows - 2 : rows]
     one_ref[...] = jnp.where(odd, low, high)
     two_ref[...] = jnp.where(odd, high, low)
 
-    def sums(value):
-        return jnp.sum(jnp.concatenate([value, rest], axis=0).T, axis=0, keepdims=True)
-
-    both = jnp.concatenate([sums(total), sums(square)], axis=0)
-    spread_ref[...] = jnp.broadcast_to(both[None], spread_ref.shape)
+    def parts(value):
+        value = jnp.sum(jnp.concatenate([value, rest], axis=0).T, axis=0, keepdims=True)
+        high = value.astype(jnp.bfloat16)
+        value = value - high.astype(jnp.float32)
+        middle = value.astype(jnp.bfloat16)
+        value = value - middle.astype(jnp.float32)
+        return [high.astype(jnp.float32), middle.astype(jnp.float32), value]
+
+    both = parts(total) + parts(square) + [jnp.zeros((EXTRA - 6, cols), jnp.float32)]
+    both = jnp.concatenate(both, axis=0).astype(jnp.bfloat16)
+    sums_ref[...] = jnp.broadcast_to(both[None], sums_ref.shape)
     for j in range(count):
-        get(j).wait()
-
-
-def prepare(odd, current, next_fields, devices, n_lon):
+        put_sums(j).start()
+    for j in range(count):
+        put(j).wait()
+        put_sums(j).wait()
+
+
+def prepare(odd, current, next_fields, n_lon):
     channels, rows, cols = current.shape
     vmem = pl.BlockSpec(memory_space=pltpu.VMEM)
+    hbm = pl.BlockSpec(memory_space=pl.ANY)
     height = next_fields.shape[1]
     padded = (channels + 7) // 8 * 8
     return pl.pallas_call(
         functools.partial(prepare_kernel, channels),
         out_shape=(
             jax.ShapeDtypeStruct((rows, cols, LANES), jnp.bfloat16),
-            jax.ShapeDtypeStruct((devices, 2, LANES), jnp.float32),
             jax.ShapeDtypeStruct((2, cols, LANES), jnp.bfloat16),
             jax.ShapeDtypeStruct((2, cols, LANES), jnp.bfloat16),
             jax.ShapeDtypeStruct((rows, 2, LANES), jnp.bfloat16),
             jax.ShapeDtypeStruct((rows, 2, LANES), jnp.bfloat16),
-            jax.ShapeDtypeStruct((n_lon, height, cols), jnp.bfloat16),
+            jax.ShapeDtypeStruct((n_lon, height // rows, rows + EXTRA, cols), jnp.bfloat16),
         ),
-        in_specs=[pl.BlockSpec(memory_space=pltpu.SMEM), vmem, pl.BlockSpec(memory_space=pltpu.HBM)],
-        out_specs=(vmem,) * 7,
+        in_specs=[pl.BlockSpec(memory_space=pltpu.SMEM), hbm, hbm],
+        out_specs=(vmem,) * 5 + (hbm,),
         scratch_shapes=[
+            pltpu.VMEM((channels, rows, cols), jnp.bfloat16),
             pltpu.VMEM((padded * rows, cols), jnp.float32),
+            pltpu.VMEM((n_lon, height, cols), jnp.bfloat16),
+            pltpu.VMEM((height // rows, EXTRA, cols), jnp.bfloat16),
+            pltpu.SemaphoreType.DMA,
+            pltpu.SemaphoreType.DMA((n_lon,)),
+            pltpu.SemaphoreType.DMA((n_lon,)),
             pltpu.SemaphoreType.DMA((n_lon,)),
         ],
-        compiler_params=pltpu.CompilerParams(vmem_limit_bytes=32 * 2**20),
+        compiler_params=pltpu.CompilerParams(vmem_limit_bytes=60 * 2**20),
         cost_estimate=pl.CostEstimate(flops=2**24, bytes_accessed=2**22, transcendentals=0),
         name="prepare",
     )(odd, current, next_fields)
@@ -266,29 +320,27 @@
     near = [(i, i ^ 1) for i in range(count)]
     far = [(i, i + 1 if i % 2 else i - 1) for i in range(count)]
     if periodic:
-        far = [(a, b % count) for a, b in far]
-    else:
-        far = [(a, b) for a, b in far if 0 <= b < count]
-    return near, far
+        return near, [(a, b % count) for a, b in far]
+    return near, [(a, b) for a, b in far if 0 <= b < count]
 
 
 def body(current, next_fields, reader_slot, first_weight, first_bias, second_weight, second_bias):
     channels, rows, cols = current.shape
     n_lat = lax.axis_size(LAT)
     n_lon = lax.axis_size(LON)
-    cells = rows * n_lat * cols * n_lon
     at_lat = lax.axis_index(LAT)
     odd_lat = at_lat % 2 == 1
     odd_lon = lax.axis_index(LON) % 2 == 1
 
-    turned, spread, one, two, west, east, blocks = prepare(
-        odd_lat.astype(jnp.int32)[None], current, next_fields, n_lat * n_lon, n_lon
+    turned, one, two, west, east, blocks = prepare(
+        odd_lat.astype(jnp.int32)[None], current, next_fields, n_lon
     )
-
     near, far = pairs(n_lat, False)
     one = lax.ppermute(one, LAT, near)
     two = lax.ppermute(two, LAT, far)
-    gathered = lax.all_to_all(spread, LON + LAT, split_axis=0, concat_axis=0, tiled=True)
+    moved = lax.all_to_all(
+        blocks.reshape(n_lon * n_lat, rows + EXTRA, cols), LON + LAT, split_axis=0, concat_axis=0, tiled=True
+    )
     top = jnp.where(odd_lat, one, two)
     bottom = jnp.where(odd_lat, two, one)
     first_cols = jnp.concatenate([top[:, :2], west, bottom[:, :2]], axis=0)
@@ -304,24 +356,13 @@
     ])
     edge = jnp.pad(edge, ((0, 0), (0, 0), (0, 48 - rows - 4), (0, 0)))
 
-    moved = lax.all_to_all(
-        blocks.reshape(n_lon * n_lat, rows, cols), LON + LAT, split_axis=0, concat_axis=0, tiled=True
-    )
-
-    total = jnp.sum(gathered, axis=0)
-    mean = total[0] / cells
-    scale = 1.0 / jnp.sqrt(total[1] / cells - mean * mean + 1e-05)
-    scale = jnp.where(jnp.arange(LANES) < channels, scale, 0.0)
-
     w1 = jnp.pad(first_weight.transpose(0, 2, 1), ((0, 0), (0, -channels % 8), (0, 0)))
     ends = jnp.stack([at_lat == 0, at_lat == n_lat - 1]).astype(jnp.int32)
-    features = convs(
-        ends, turned, top, bottom, left, right, edge, mean[None], scale[None],
-        w1, first_bias[None], second_weight, second_bias[None],
+    place = (reader_slot % n_lon) * n_lat + reader_slot // n_lon
+    return convs(
+        ends, place, turned, top, bottom, left, right, edge,
+        w1, first_bias[None], second_weight, second_bias[None], moved,
     )
-    place = (reader_slot % n_lon) * n_lat + reader_slot // n_lon
-    next_tile = moved.at[place].get(mode="promise_in_bounds")
-    return (features, next_tile)
 
 
 def solution(mesh):

time: 62.7 us -> 57.5 us (0.917)
  the two profiles are of different devices: /device:TPU:1 before, /device:TPU:2 now
where the time goes in v3:
time: 57.5 us; the launch traced here: 57.2 us
  starting transfers between devices  19.9 us (35%)
  Pallas kernels  17.5 us (30%)
  waiting for transfers between devices  17.1 us (30%)
  local copies, waits for them, and re-layouts  1.52 us (3%)
  between operations  0.96 us (2%)
    ppermute x1, waiting for transfers between devices, body(): two = lax.ppermute(two, LAT, far)  13.4 us
    pallas_call x1, Pallas kernels, convs(): pl.pallas_call(functools.partial(conv_kernel, channels, rows, cols, hid),...  12.6 us
    all_to_all x1, starting transfers between devices, body(): lax.all_to_all(blocks.reshape(n_lon * n_lat, rows + EXTRA, cols), LON + L...  10.5 us
    ppermute x1, starting transfers between devices, body(): two = lax.ppermute(jnp.where(odd_lon, last_cols, first_cols), LON, far)  5.51 us
    pallas_call x1, Pallas kernels, prepare(): pl.pallas_call(functools.partial(prepare_kernel, channels), out_shape=(ja...  4.97 us
    ppermute x1, starting transfers between devices, body(): two = lax.ppermute(two, LAT, far)  3.35 us
    ppermute x1, waiting for transfers between devices, body(): two = lax.ppermute(jnp.where(odd_lon, last_cols, first_cols), LON, far)  1.92 us
    ppermute x1, waiting for transfers between devices, body(): one = lax.ppermute(jnp.where(odd_lon, first_cols, last_cols), LON, near)  1.82 us
  transfers between devices with their start and end apart: 5, of which 3 were waited for; matrix products, arithmetic and copies ran while one was open for 1% of the time, Pallas kernels for 0%

profile of v3, /device:TPU:2, one launch (start us, length us, event | category | flops | bytes accessed | tf_op | source)
XLA Modules:
  0.0 57.2 jit_solution(2636679124894500024)
XLA Ops:
  0.6 5.0 %prepare.1 = (bf16[32,128,128]{2,1,0:T(8,128)(2,1)}, bf16[2,128,128]{2,1,0:T(8,128)(2,1)}, bf16[2,128,128]{2,1,0:T(8,128)(2,1)}, bf16[32,2,128]{2,1,0:T(2,128)(2...) custom-call(s32[1]{0:T(128)} %bitcast.2.odd_ref, bf16[69,32,128]{2,1,0:T(8,128)(2,1)} %x_ref.1, ...), custom_call_target="tpu_custom_call" | custom-call | flops 16777216 | bytes 4194304 | tf_op jit(solution)/shard_map/prepare/pallas_call | solution.py:291
  5.6 0.0 copy-start.6
  5.6 0.0 copy-start.5
  5.6 0.0 copy-start.9
  5.7 0.0 copy-start.8
  5.7 0.0 copy-start.7
  5.7 0.0 copy-start.4
  5.7 10.5 %all-to-all-start = ((bf16[128,40,128]{2,1,0:T(8,128)(2,1)}), bf16[128,40,128]{2,1,0:T(8,128)(2,1)S(1)}, u32[]{:S(2)}, u32[]{:S(2)}) async-start(bf16[128,40,128]{2,1,0:T(8,128)(2,1)} %bitcast.29), calls=%async_computation | async-start | bytes 2621440 | tf_op jit(solution)/shard_map/all_to_all | solution.py:341
  16.2 0.0 copy-start
  16.2 0.0 copy-start.2
  16.3 0.0 copy-start.3
  16.3 0.0 copy-done.6
  16.3 0.1 copy.10
  16.4 3.4 %collective-permute-start.1 = (bf16[2,128,128]{2,0,1:T(2,128)(2,1)S(1)}, bf16[2,128,128]{2,0,1:T(2,128)(2,1)S(1)}, u32[]{:S(2)}, u32[]{:S(2)}) collective-permute-start(bf16[2,128,128]{2,0,1:T(2,128)(2,1)S(1)} %copy.10), channel_id=1, source_target_pairs={{8,16},{16,8},{24,32},{32,24},{40,48},{48,40},{56,64},{64,56},{72,... | collective-permute-start | bytes 196616 | tf_op jit(solution)/shard_map/ppermute | solution.py:340
  19.7 0.0 copy-done.5
  19.7 0.1 copy.9
  19.8 0.5 collective-permute-start
  20.3 0.0 copy-done.9
  20.3 0.0 copy-done.8
  20.3 0.0 copy-done.7
  20.4 0.0 copy-done.4
  20.4 0.1 add_convert_fusion.ends_ref
  20.5 13.4 %collective-permute-done.1 = bf16[2,128,128]{2,0,1:T(2,128)(2,1)S(1)} collective-permute-done((bf16[2,128,128]{2,0,1:T(2,128)(2,1)S(1)}, bf16[2,128,128]{2,0,1:T(2,128)(2,1)S(1)}, u32[]{:S(2)}, u32[]{:S(2)}) %collective-permute-start.1) | collective-permute-done | bytes 65568 | tf_op jit(solution)/shard_map/ppermute | solution.py:340
  33.9 0.0 collective-permute-done
  33.9 5.5 %collective-permute-start.3 = (bf16[36,2,128]{2,0,1:T(8,128)(2,1)S(1)}, bf16[36,2,128]{2,0,1:T(8,128)(2,1)S(1)}, u32[]{:S(2)}, u32[]{:S(2)}) collective-permute-start(bf16[36,2,128]{2,0,1:T(8,128)(2,1)S(1)} %get-tuple-element.22), channel_id=1, source_target_pairs={{0,7},{1,2},{2,1},{3,4},{4,3},{5,6},{6,5},{7,0},{8,15},{9,10},{10,... | collective-permute-start | bytes 55304 | tf_op jit(solution)/shard_map/ppermute | solution.py:350
  39.5 0.0 collective-permute-start.2
  39.5 1.9 %collective-permute-done.3 = bf16[36,2,128]{2,0,1:T(8,128)(2,1)S(1)} collective-permute-done((bf16[36,2,128]{2,0,1:T(8,128)(2,1)S(1)}, bf16[36,2,128]{2,0,1:T(8,128)(2,1)S(1)}, u32[]{:S(2)}, u32[]{:S(2)}) %collective-permute-start.3) | collective-permute-done | bytes 18464 | tf_op jit(solution)/shard_map/ppermute | solution.py:350
  41.4 1.8 %collective-permute-done.2 = bf16[36,2,128]{2,0,1:T(8,128)(2,1)S(1)} collective-permute-done((bf16[36,2,128]{2,0,1:T(8,128)(2,1)S(1)}, bf16[36,2,128]{2,0,1:T(8,128)(2,1)S(1)}, u32[]{:S(2)}, u32[]{:S(2)}) %collective-permute-start.2) | collective-permute-done | bytes 18464 | tf_op jit(solution)/shard_map/ppermute | solution.py:349
  43.4 0.0 all-to-all-done.moved_ref
  43.4 0.0 copy-done
  43.4 1.2 %copy-done.1 = bf16[32,128,128]{2,1,0:T(8,128)(2,1)S(1)} copy-done((bf16[32,128,128]{2,1,0:T(8,128)(2,1)S(1)}, bf16[32,128,128]{2,1,0:T(8,128)(2,1)}, u32[]{:S(2)}) %copy-start.1) | copy-done | bytes 1048600
  44.6 12.6 %convs.1 = (bf16[256,32,128]{2,1,0:T(8,128)(2,1)}, bf16[69,32,128]{2,1,0:T(8,128)(2,1)}) custom-call(s32[2]{0:T(128)S(1)} %add_convert_fusion.ends_ref, s32[69]{0:T(128)S(1)} %fusion.4.place_ref, bf16[32,128,128]{2,1,0:T(8,128)(2,1)S(1)} %copy-done.1, bf16[2,128,128]{2,1,0:T(8,128)(2,1)S(1)} %copy.13.top_ref, bf16[2,128,128]{2,1,0:T(8,128)(2,1)S(1)} %copy.14.bottom_ref, ...), custom_call_target="tpu_custom_call" | custom-call | flops 6569852928 | bytes 8388608 | tf_op jit(solution)/shard_map/convs/pallas_call | solution.py:190
  (22 shorter events, 0.2 us)
Async XLA Ops:
  5.6 10.6 %copy-start.6 = (bf16[2,128,128]{2,1,0:T(8,128)(2,1)S(1)}, bf16[2,128,128]{2,1,0:T(8,128)(2,1)}, u32[]{:S(2)}) copy-start(bf16[2,128,128]{2,1,0:T(8,128)(2,1)} %get-tuple-element.10) | copy-start | bytes 196612
  5.6 14.1 %copy-start.5 = (bf16[2,128,128]{2,1,0:T(8,128)(2,1)S(1)}, bf16[2,128,128]{2,1,0:T(8,128)(2,1)}, u32[]{:S(2)}) copy-start(bf16[2,128,128]{2,1,0:T(8,128)(2,1)} %get-tuple-element.9) | copy-start | bytes 196612
  5.6 14.6 %copy-start.9 = (s32[69]{0:T(128)S(1)}, s32[69]{0:T(128)}, u32[]{:S(2)}) copy-start(s32[69]{0:T(128)} %param.9) | copy-start | bytes 832
  5.7 14.6 %copy-start.8 = (bf16[32,2,128]{2,1,0:T(2,128)(2,1)S(1)}, bf16[32,2,128]{2,1,0:T(2,128)(2,1)}, u32[]{:S(2)}) copy-start(bf16[32,2,128]{2,1,0:T(2,128)(2,1)} %get-tuple-element.11) | copy-start | bytes 49156
  5.7 14.7 %copy-start.7 = (bf16[32,2,128]{2,1,0:T(2,128)(2,1)S(1)}, bf16[32,2,128]{2,1,0:T(2,128)(2,1)}, u32[]{:S(2)}) copy-start(bf16[32,2,128]{2,1,0:T(2,128)(2,1)} %get-tuple-element.12) | copy-start | bytes 49156
  5.7 14.7 %copy-start.4 = (bf16[9,256,69]{1,2,0:T(8,128)(2,1)S(1)}, bf16[9,256,69]{1,2,0:T(8,128)(2,1)}, u32[]{:S(2)}) copy-start(bf16[9,256,69]{1,2,0:T(8,128)(2,1)} %param.10) | copy-start | bytes 953860
  5.7 37.7 %all-to-all-start = ((bf16[128,40,128]{2,1,0:T(8,128)(2,1)}), bf16[128,40,128]{2,1,0:T(8,128)(2,1)S(1)}, u32[]{:S(2)}, u32[]{:S(2)}) async-start(bf16[128,40,128]{2,1,0:T(8,128)(2,1)} %bitcast.29), calls=%async_computation | async-start | bytes 2621440 | tf_op jit(solution)/shard_map/all_to_all | solution.py:341
  16.2 27.2 %copy-start = (bf16[9,256,256]{2,1,0:T(8,128)(2,1)S(1)}, bf16[9,256,256]{2,1,0:T(8,128)(2,1)}, u32[]{:S(2)}) copy-start(bf16[9,256,256]{2,1,0:T(8,128)(2,1)} %w2_raw_ref.1) | copy-start | bytes 3538948
  16.2 27.2 %copy-start.2 = (f32[256]{0:T(256)S(1)}, f32[256]{0:T(256)}, u32[]{:S(2)}) copy-start(f32[256]{0:T(256)} %param.11) | copy-start | bytes 3076
  16.3 27.1 %copy-start.3 = (f32[256]{0:T(256)S(1)}, f32[256]{0:T(256)}, u32[]{:S(2)}) copy-start(f32[256]{0:T(256)} %param.13) | copy-start | bytes 3076
  16.4 17.5 %collective-permute-start.1 = (bf16[2,128,128]{2,0,1:T(2,128)(2,1)S(1)}, bf16[2,128,128]{2,0,1:T(2,128)(2,1)S(1)}, u32[]{:S(2)}, u32[]{:S(2)}) collective-permute-start(bf16[2,128,128]{2,0,1:T(2,128)(2,1)S(1)} %copy.10), channel_id=1, source_target_pairs={{8,16},{16,8},{24,32},{32,24},{40,48},{48,40},{56,64},{64,56},{72,... | collective-permute-start | bytes 196616 | tf_op jit(solution)/shard_map/ppermute | solution.py:340
  19.8 14.1 %collective-permute-start = (bf16[2,128,128]{2,0,1:T(2,128)(2,1)S(1)}, bf16[2,128,128]{2,0,1:T(2,128)(2,1)S(1)}, u32[]{:S(2)}, u32[]{:S(2)}) collective-permute-start(bf16[2,128,128]{2,0,1:T(2,128)(2,1)S(1)} %copy.9), channel_id=1, source_target_pairs={{0,8},{8,0},{16,24},{24,16},{32,40},{40,32},{48,56},{56,48},{64,72... | collective-permute-start | bytes 196616 | tf_op jit(solution)/shard_map/ppermute | solution.py:339
  33.9 7.5 %collective-permute-start.3 = (bf16[36,2,128]{2,0,1:T(8,128)(2,1)S(1)}, bf16[36,2,128]{2,0,1:T(8,128)(2,1)S(1)}, u32[]{:S(2)}, u32[]{:S(2)}) collective-permute-start(bf16[36,2,128]{2,0,1:T(8,128)(2,1)S(1)} %get-tuple-element.22), channel_id=1, source_target_pairs={{0,7},{1,2},{2,1},{3,4},{4,3},{5,6},{6,5},{7,0},{8,15},{9,10},{10,... | collective-permute-start | bytes 55304 | tf_op jit(solution)/shard_map/ppermute | solution.py:350
  39.5 3.8 %collective-permute-start.2 = (bf16[36,2,128]{2,0,1:T(8,128)(2,1)S(1)}, bf16[36,2,128]{2,0,1:T(8,128)(2,1)S(1)}, u32[]{:S(2)}, u32[]{:S(2)}) collective-permute-start(bf16[36,2,128]{2,0,1:T(8,128)(2,1)S(1)} %get-tuple-element.23), channel_id=1, source_target_pairs={{0,1},{1,0},{2,3},{3,2},{4,5},{5,4},{6,7},{7,6},{8,9},{9,8},{10,11... | collective-permute-start | bytes 55304 | tf_op jit(solution)/shard_map/ppermute | solution.py:349
  43.4 1.2 %copy-start.1 = (bf16[32,128,128]{2,1,0:T(8,128)(2,1)S(1)}, bf16[32,128,128]{2,1,0:T(8,128)(2,1)}, u32[]{:S(2)}) copy-start(bf16[32,128,128]{2,1,0:T(8,128)(2,1)} %get-tuple-element.8.x_ref) | copy-start | bytes 3145732

commit v4 on v3

v4 whole, which is shorter than its diff:
```python
import functools

import jax
import jax.numpy as jnp
from jax import lax
from jax.experimental import pallas as pl
from jax.experimental.pallas import tpu as pltpu
from jax.sharding import Mesh
from jax.sharding import PartitionSpec as P

LAT = ("lat_0", "lat_1", "lat_2")
LON = ("lon_0", "lon_1")
LANES = 128
BLOCK = 8
EXTRA = 8
X_PART = 24
SPILL = 13
LAT_COUNT = 16
PREPARE_VMEM = 60 * 2**20
GELU_C = 0.7978845608028654


def gelu(v):
    return (0.5 * v) * (1.0 + jnp.tanh(v * (GELU_C + (GELU_C * 0.044715) * (v * v))))


def conv_kernel(
    channels, rows, cols, hid,
    at_ref, place_ref, x_ref, lat_one_ref, lat_two_ref, sent_one_ref, sent_two_ref, lon_one_ref, lon_two_ref,
    w1_raw_ref, b1_ref, w2_raw_ref, b2_ref, moved_ref, out_ref, tile_ref,
    w1_ref, w2_ref, taps_ref, edge_ref, edge_taps_ref, edge_hid_ref, west_ref, mid_ref, east_ref,
    turned_ref, done_ref, sem, take_sem,
):
    n_lat, n_lon = LAT_COUNT, moved_ref.shape[0] // LAT_COUNT
    cells = rows * cols * moved_ref.shape[0]
    lat, lon = at_ref[0], at_ref[1]
    first = lat == 0
    last = lat == n_lat - 1
    odd_lat = lat % 2 == 1
    odd_lon = lon % 2 == 1
    lane = lax.broadcasted_iota(jnp.int32, (cols, LANES), 1)
    sub = lax.broadcasted_iota(jnp.int32, (8, LANES), 0)
    sub_hid = lax.broadcasted_iota(jnp.int32, (8, hid), 0)
    group = w1_raw_ref.shape[1]
    over = 2 * group - LANES

    def weights():
        for a in range(3):
            for b in range(3):
                w1_ref[a * 2 * LANES + b * group : a * 2 * LANES + (b + 1) * group, :] = w1_raw_ref[3 * a + b]
            w1_ref[a * 2 * LANES + 3 * group : (a + 1) * 2 * LANES, :] = jnp.zeros(
                (2 * LANES - 3 * group, hid), jnp.bfloat16
            )
        for tap in range(9):
            w2_ref[tap * hid : (tap + 1) * hid, :] = w2_raw_ref[tap].T

    def norm(raw):
        return (raw.astype(jnp.float32) - mean) * scale

    def pack(minus, zero, plus, lanes):
        turned = pltpu.roll(zero, group, axis=1)
        low = jnp.where(lanes < group, minus, turned)
        high = jnp.where(lanes < over, turned, pltpu.roll(plus, over, axis=1))
        return low, high

    def shifted(main, before, after, sub8):
        minus = pltpu.roll(main, 1, axis=0)
        minus = jnp.concatenate([jnp.where(sub8 == 0, before, minus[:8]), minus[8:]], axis=0)
        plus = pltpu.roll(main, cols - 1, axis=0)
        plus = jnp.concatenate([plus[: cols - 8], jnp.where(sub8 == 7, after, plus[cols - 8 :])], axis=0)
        return minus, plus

    def lat_row(row):
        if row < 2:
            return jnp.where(odd_lat, lat_one_ref[row], lat_two_ref[row]), jnp.logical_not(first)
        if row >= rows + 2:
            row = row - rows - 2
            return jnp.where(odd_lat, lat_two_ref[row], lat_one_ref[row]), jnp.logical_not(last)
        return x_ref[row - 2], None

    def build(row):
        raw, keep = lat_row(row)
        main = norm(raw)
        if keep is not None:
            main = jnp.where(keep, main, 0.0)
        minus, plus = shifted(main, edge_ref[0, 1, row : row + 1, :], edge_ref[1, 1, row : row + 1, :], sub)
        low, high = pack(minus, main, plus, lane)
        taps_ref[row, :, 0:LANES] = low.astype(jnp.bfloat16)
        taps_ref[row, :, LANES : 2 * LANES] = high.astype(jnp.bfloat16)

    def corner(down, right):
        there = ((lon + right) % n_lon) * n_lat + (lat + down) % n_lat
        block = moved_ref[there, rows : rows + EXTRA, :].astype(jnp.float32)
        line = lax.broadcasted_iota(jnp.int32, (1, LANES), 1)
        split = LANES - channels
        cells = []
        for j in range(2):
            cells.append(block[6 + j : 7 + j])
        for j in range(2):
            head = pltpu.roll(block[6 + j : 7 + j], LANES - channels, axis=1)
            tail = pltpu.roll(block[j : j + 1], LANES - SPILL, axis=1)
            cells.append(jnp.where(line < split, head, tail))
        return cells

    def edges():
        sides = (
            (odd_lon, lon_one_ref, lon_two_ref, sent_one_ref, sent_two_ref),
            (odd_lon, lon_two_ref, lon_one_ref, sent_two_ref, sent_one_ref),
        )
        keep_top = jnp.logical_not(first)
        keep_bottom = jnp.logical_not(last)
        for side, (odd, one_ref, two_ref, own_one_ref, own_two_ref) in enumerate(sides):
            own_part = 2 if side == 0 else 0
            own = jnp.where(odd, own_one_ref[side], own_two_ref[side])
            edge_ref[side, own_part, 2 : rows + 2, :] = norm(own)
            for row in (0, 1, rows + 2, rows + 3):
                raw, keep = lat_row(row)
                value = norm(raw[0:16] if side == 0 else raw[cols - 16 : cols])
                value = value[0:1] if side == 0 else value[15:16]
                edge_ref[side, own_part, row : row + 1, :] = jnp.where(keep, value, 0.0)
            right = 1 if side == 1 else -1
            top = corner(-1, right)
            bottom = corner(1, right)
            for j in range(2):
                part = j + side
                edge_ref[side, part, 2 : rows + 2, :] = norm(jnp.where(odd, one_ref[j], two_ref[j]))
                for i in range(2):
                    edge_ref[side, part, i : i + 1, :] = jnp.where(keep_top, norm(top[2 * i + j]), 0.0)
                    edge_ref[side, part, rows + 2 + i : rows + 3 + i, :] = jnp.where(
                        keep_bottom, norm(bottom[2 * i + j]), 0.0
                    )
        tall = edge_ref.shape[2]
        for side in range(2):
            for part in range(3):
                edge_ref[side, part, rows + 4 : tall, :] = jnp.zeros((tall - rows - 4, LANES), jnp.float32)
        edge_lane = lax.broadcasted_iota(jnp.int32, (tall, LANES), 1)
        hid_row = lax.broadcasted_iota(jnp.int32, (tall - 8, hid), 0)
        hid_outside = jnp.logical_or(
            jnp.logical_and(first, hid_row < 1), jnp.logical_and(last, hid_row >= rows + 1)
        )
        for side in range(2):
            low, high = pack(edge_ref[side, 0], edge_ref[side, 1], edge_ref[side, 2], edge_lane)
            edge_taps_ref[side, :, 0:LANES] = low
            edge_taps_ref[side, :, LANES : 2 * LANES] = high
            stacked = jnp.concatenate(
                [edge_taps_ref[side, a : a + tall - 8, :].astype(jnp.bfloat16) for a in range(3)], axis=1
            )
            value = jnp.dot(stacked, w1_ref[...], preferred_element_type=jnp.float32) + b1_ref[...]
            edge_hid_ref[side] = jnp.where(hid_outside, 0.0, gelu(value))

    def hidden(row, count):
        stacked = jnp.concatenate(
            [taps_ref[row + a : row + a + count].reshape(count * cols, 2 * LANES) for a in range(3)], axis=1
        )
        value = jnp.dot(stacked, w1_ref[...], preferred_element_type=jnp.float32)
        for i in range(count):
            r = row + i
            one = gelu(value[i * cols : (i + 1) * cols] + b1_ref[...])
            if r == 0:
                one = jnp.where(first, 0.0, one)
            elif r == rows + 1:
                one = jnp.where(last, 0.0, one)
            west, east = shifted(one, edge_hid_ref[0, r : r + 1, :], edge_hid_ref[1, r : r + 1, :], sub_hid)
            west_ref[r] = west.astype(jnp.bfloat16)
            mid_ref[r] = one.astype(jnp.bfloat16)
            east_ref[r] = east.astype(jnp.bfloat16)

    def put(t):
        return pltpu.make_async_copy(
            done_ref.at[t], out_ref.at[:, t * BLOCK : (t + 1) * BLOCK, :], sem.at[t]
        )

    def features(t):
        base = t * BLOCK
        stacked = jnp.concatenate(
            [
                ref[base + a : base + a + BLOCK].reshape(BLOCK * cols, hid)
                for a in range(3)
                for ref in (west_ref, mid_ref, east_ref)
            ],
            axis=1,
        )
        value = jnp.dot(stacked, w2_ref[...], preferred_element_type=jnp.float32) + b2_ref[...]
        for i in range(BLOCK):
            turned_ref[t % 2, pl.ds(i, hid, stride=BLOCK), :] = value[i * cols : (i + 1) * cols].T
        done_ref[t] = turned_ref[t % 2].reshape(hid, BLOCK, cols).astype(jnp.bfloat16)
        put(t).start()

    steps = rows // BLOCK
    taken = tile_ref.shape[0]

    @pl.loop(0, taken)
    def _(c):
        pltpu.make_async_copy(moved_ref.at[place_ref[c], 0:rows, :], tile_ref.at[c], take_sem).start()

    weights()
    sums = jnp.sum(moved_ref[:, rows : rows + EXTRA, :].astype(jnp.float32), axis=0)
    line = lax.broadcasted_iota(jnp.int32, (1, LANES), 1)
    mean = (sums[0:1] + sums[1:2] + sums[2:3]) / cells
    square = (sums[3:4] + sums[4:5] + sums[5:6]) / cells
    mean = jnp.where(line < channels, mean, 0.0)
    square = jnp.where(line < channels, square, 0.0)
    scale = 1.0 / jnp.sqrt(square - mean * mean + 1e-05)
    scale = jnp.where(line < channels, scale, 0.0)
    edges()
    for r in range(BLOCK + 4):
        build(r)
    hidden(0, BLOCK + 2)
    for r in range(BLOCK + 4, 2 * BLOCK + 4):
        build(r)
    for t in range(steps):
        if t + 2 < steps:
            for r in range((t + 2) * BLOCK + 4, (t + 3) * BLOCK + 4):
                build(r)
        if t + 1 < steps:
            hidden((t + 1) * BLOCK + 2, BLOCK)
        features(t)
    pltpu.make_async_copy(moved_ref.at[0:taken, 0:rows, :], tile_ref, take_sem).wait()
    for t in range(steps):
        put(t).wait()


def convs(channels, at, place, x, lat_one, lat_two, sent_one, sent_two, lon_one, lon_two, w1, b1, w2, b2, moved):
    rows, cols = x.shape[0], x.shape[1]
    hid = w2.shape[1]
    taken = place.shape[0]
    tall = (rows + 4 + 7) // 8 * 8 + 8
    vmem = pl.BlockSpec(memory_space=pltpu.VMEM)
    smem = pl.BlockSpec(memory_space=pltpu.SMEM)
    hbm = pl.BlockSpec(memory_space=pl.ANY)
    flops = 2 * hid * (rows * cols * 9 * hid + (rows + 2) * (cols + 2) * 3 * 256)
    return pl.pallas_call(
        functools.partial(conv_kernel, channels, rows, cols, hid),
        out_shape=(
            jax.ShapeDtypeStruct((hid, rows, cols), jnp.bfloat16),
            jax.ShapeDtypeStruct((taken, rows, cols), jnp.bfloat16),
        ),
        in_specs=[smem, smem] + [vmem] * 12,
        out_specs=(hbm, hbm),
        scratch_shapes=[
            pltpu.VMEM((6 * LANES, hid), jnp.bfloat16),
            pltpu.VMEM((9 * hid, hid), jnp.bfloat16),
            pltpu.VMEM((rows + 4, cols, 2 * LANES), jnp.bfloat16),
            pltpu.VMEM((2, 3, tall, LANES), jnp.float32),
            pltpu.VMEM((2, tall, 2 * LANES), jnp.float32),
            pltpu.VMEM((2, tall - 8, hid), jnp.float32),
            pltpu.VMEM((rows + 2, cols, hid), jnp.bfloat16),
            pltpu.VMEM((rows + 2, cols, hid), jnp.bfloat16),
            pltpu.VMEM((rows + 2, cols, hid), jnp.bfloat16),
            pltpu.VMEM((2, hid * BLOCK, cols), jnp.float32),
            pltpu.VMEM((rows // BLOCK, hid, BLOCK, cols), jnp.bfloat16),
            pltpu.SemaphoreType.DMA((rows // BLOCK,)),
            pltpu.SemaphoreType.DMA,
        ],
        compiler_params=pltpu.CompilerParams(vmem_limit_bytes=40 * 2**20),
        cost_estimate=pl.CostEstimate(flops=flops, bytes_accessed=8 * 2**20, transcendentals=0),
        name="convs",
    )(at, place, x, lat_one, lat_two, sent_one, sent_two, lon_one, lon_two, w1, b1, w2, b2, moved)


def prepare_kernel(
    channels, at_ref, x_ref, fields_ref,
    turned_ref, lat_one_ref, lat_two_ref, lon_one_ref, lon_two_ref, blocks_ref,
    raw_ref, wide_ref, held_ref, extra_ref, first_ref, last_ref, x_sem, in_sem, out_sem, extra_sem,
):
    rows, cols = turned_ref.shape[0], turned_ref.shape[1]
    n_lon, n_lat = blocks_ref.shape[0], blocks_ref.shape[1]
    lat, lon = at_ref[0], at_ref[1]

    def load(j):
        part = pl.ds(j * X_PART, min(X_PART, channels - j * X_PART))
        return pltpu.make_async_copy(x_ref.at[part], raw_ref.at[part], x_sem.at[j])

    def get(j):
        return pltpu.make_async_copy(fields_ref.at[0, :, j * cols : (j + 1) * cols], held_ref.at[j], in_sem.at[j])

    def put(j):
        return pltpu.make_async_copy(
            held_ref.at[j].reshape(n_lat, rows, cols), blocks_ref.at[j, :, 0:rows, :], out_sem.at[j]
        )

    def put_extra(j):
        return pltpu.make_async_copy(extra_ref.at[j], blocks_ref.at[j, :, rows : rows + EXTRA, :], extra_sem.at[j])

    loads = (channels + X_PART - 1) // X_PART
    for j in range(loads):
        load(j).start()
    for j in range(n_lon):
        get(j).start()
    padded = wide_ref.shape[0] // rows
    wide_ref[channels * rows :, :] = jnp.zeros(((padded - channels) * rows, cols), jnp.float32)
    for j in range(loads):
        load(j).wait()
        low, high = j * X_PART, min((j + 1) * X_PART, channels)
        wide_ref[low * rows : high * rows, :] = (
            raw_ref[low:high].astype(jnp.float32).reshape((high - low) * rows, cols)
        )
    rest = jnp.zeros((LANES - padded, cols), jnp.float32)
    total = jnp.zeros((padded, cols), jnp.float32)
    square = jnp.zeros((padded, cols), jnp.float32)
    for r in range(rows):
        one = wide_ref[pl.ds(r, padded, stride=rows), :]
        total += one
        square += one * one
        turned = jnp.concatenate([one, rest], axis=0).T
        turned_ref[r] = turned.astype(jnp.bfloat16)
        for j in range(2):
            first_ref[j, r : r + 1, :] = turned[j : j + 1]
            last_ref[j, r : r + 1, :] = turned[cols - 2 + j : cols - 1 + j]
        if r % 4 == 3:
            get(r // 4).wait()
            put(r // 4).start()

    def parts(value):
        value = jnp.sum(jnp.concatenate([value, rest], axis=0).T, axis=0, keepdims=True)
        high = value.astype(jnp.bfloat16).astype(jnp.float32)
        value = value - high
        middle = value.astype(jnp.bfloat16).astype(jnp.float32)
        return [high, middle, value - middle]

    sums = parts(total) + parts(square)
    line = lax.broadcasted_iota(jnp.int32, (1, LANES), 1)

    def extra(down, right):
        cols_ref = last_ref if right > 0 else first_ref
        row = rows - 2 if down > 0 else 0
        near = [cols_ref[j, row : row + 1, :] for j in range(2)]
        far = [cols_ref[j, row + 1 : row + 2, :] for j in range(2)]
        spill = [
            jnp.where(
                jnp.logical_and(line >= SPILL + LANES - channels, line < SPILL + channels),
                pltpu.roll(far[j], SPILL, axis=1), sums[j],
            )
            for j in range(2)
        ]
        both = [jnp.where(line < channels, near[j], pltpu.roll(far[j], channels, axis=1)) for j in range(2)]
        return jnp.concatenate(spill + sums[2:] + both, axis=0).astype(jnp.bfloat16)

    extra_ref[...] = jnp.broadcast_to(extra(1, 1)[None, None], extra_ref.shape)
    for down, right in ((1, -1), (-1, 1), (-1, -1)):
        extra_ref[(lon + n_lon + right) % n_lon, (lat + n_lat + down) % n_lat] = extra(down, right)
    for j in range(n_lon):
        put_extra(j).start()
    odd_lat = lat % 2 == 1
    odd_lon = lon % 2 == 1
    low = turned_ref[0:2]
    high = turned_ref[rows - 2 : rows]
    lat_one_ref[...] = jnp.where(odd_lat, low, high)
    lat_two_ref[...] = jnp.where(odd_lat, high, low)
    low = first_ref[...].astype(jnp.bfloat16)
    high = last_ref[...].astype(jnp.bfloat16)
    lon_one_ref[...] = jnp.where(odd_lon, low, high)
    lon_two_ref[...] = jnp.where(odd_lon, high, low)
    for j in range(n_lon):
        put(j).wait()
        put_extra(j).wait()


def prepare(at, current, next_fields, n_lon):
    channels, rows, cols = current.shape
    vmem = pl.BlockSpec(memory_space=pltpu.VMEM)
    hbm = pl.BlockSpec(memory_space=pl.ANY)
    height = next_fields.shape[1]
    padded = (channels + 7) // 8 * 8
    lat_row = jax.ShapeDtypeStruct((2, cols, LANES), jnp.bfloat16)
    lon_row = jax.ShapeDtypeStruct((2, rows, LANES), jnp.bfloat16)
    return pl.pallas_call(
        functools.partial(prepare_kernel, channels),
        out_shape=(
            jax.ShapeDtypeStruct((rows, cols, LANES), jnp.bfloat16),
            lat_row, lat_row, lon_row, lon_row,
            jax.ShapeDtypeStruct((n_lon, height // rows, rows + EXTRA, cols), jnp.bfloat16),
        ),
        in_specs=[pl.BlockSpec(memory_space=pltpu.SMEM), hbm, hbm],
        out_specs=(vmem,) * 5 + (hbm,),
        scratch_shapes=[
            pltpu.VMEM((channels, rows, cols), jnp.bfloat16),
            pltpu.VMEM((padded * rows, cols), jnp.float32),
            pltpu.VMEM((n_lon, height, cols), jnp.bfloat16),
            pltpu.VMEM((n_lon, height // rows, EXTRA, cols), jnp.bfloat16),
            pltpu.VMEM((2, rows, LANES), jnp.float32),
            pltpu.VMEM((2, rows, LANES), jnp.float32),
            pltpu.SemaphoreType.DMA(((channels + X_PART - 1) // X_PART,)),
            pltpu.SemaphoreType.DMA((n_lon,)),
            pltpu.SemaphoreType.DMA((n_lon,)),
            pltpu.SemaphoreType.DMA((n_lon,)),
        ],
        compiler_params=pltpu.CompilerParams(vmem_limit_bytes=PREPARE_VMEM),
        cost_estimate=pl.CostEstimate(flops=2**24, bytes_accessed=2**22, transcendentals=0),
        name="prepare",
    )(at, current, next_fields)


def pairs(count, periodic):
    near = [(i, i ^ 1) for i in range(count)]
    far = [(i, i + 1 if i % 2 else i - 1) for i in range(count)]
    if periodic:
        return near, [(a, b % count) for a, b in far]
    return near, [(a, b) for a, b in far if 0 <= b < count]


def body(current, next_fields, reader_slot, first_weight, first_bias, second_weight, second_bias):
    channels, rows, cols = current.shape
    n_lat = lax.axis_size(LAT)
    n_lon = lax.axis_size(LON)
    at = jnp.stack([lax.axis_index(LAT), lax.axis_index(LON)]).astype(jnp.int32)
    turned, lat_one, lat_two, sent_one, sent_two, blocks = prepare(at, current, next_fields, n_lon)
    moved = lax.all_to_all(
        blocks.reshape(n_lon * n_lat, rows + EXTRA, cols), LON + LAT, split_axis=0, concat_axis=0, tiled=True
    )
    near, far = pairs(n_lat, False)
    lat_one = lax.ppermute(lat_one, LAT, near)
    lat_two = lax.ppermute(lat_two, LAT, far)
    near, far = pairs(n_lon, True)
    lon_one = lax.ppermute(sent_one, LON, near)
    lon_two = lax.ppermute(sent_two, LON, far)
    w1 = jnp.pad(first_weight.transpose(0, 2, 1), ((0, 0), (0, -channels % 8), (0, 0)))
    place = (reader_slot % n_lon) * n_lat + reader_slot // n_lon
    return convs(
        channels, at, place, turned, lat_one, lat_two, sent_one, sent_two, lon_one, lon_two,
        w1, first_bias[None], second_weight, second_bias[None], moved,
    )


def solution(mesh):
    split = Mesh(mesh.devices.reshape(4, 2, 2, 2, 4), ("lat_0", "lat_1", "lat_2", "lon_0", "lon_1"))
    return jax.shard_map(
        body,
        mesh=split,
        in_specs=(P(None, LAT, LON), P(LAT + LON, None, None), P(), P(), P(), P(), P()),
        out_specs=(P(None, LAT, LON), P(None, LAT, LON)),
        check_vma=False,
    )
```

time: 57.5 us -> 51.8 us (0.901)
  the two profiles are of different devices: /device:TPU:2 before, /device:TPU:1 now
where the time goes in v4:
time: 51.8 us; the launch traced here: 51.6 us
  starting transfers between devices  20.9 us (40%)
  Pallas kernels  16.2 us (31%)
  waiting for transfers between devices  11.7 us (23%)
  local copies, waits for them, and re-layouts  1.3 us (3%)
  between operations  0.81 us (2%)
  other arithmetic  0.62 us (1%)
    all_to_all x1, starting transfers between devices, body(): lax.all_to_all(blocks.reshape(n_lon * n_lat, rows + EXTRA, cols), LON + L...  11.5 us
    pallas_call x1, Pallas kernels, convs(): pl.pallas_call(functools.partial(conv_kernel, channels, rows, cols, hid),...  10.6 us
    pallas_call x1, Pallas kernels, prepare(): pl.pallas_call(functools.partial(prepare_kernel, channels), out_shape=(ja...  5.55 us
    ppermute x1, starting transfers between devices, body(): lon_two = lax.ppermute(sent_two, LON, far)  4.72 us
    ppermute x1, waiting for transfers between devices, body(): lat_two = lax.ppermute(lat_two, LAT, far)  4.65 us
    all_to_all x1, waiting for transfers between devices, body(): lax.all_to_all(blocks.reshape(n_lon * n_lat, rows + EXTRA, cols), LON + L...  3.61 us
    ppermute x1, waiting for transfers between devices, body(): lon_two = lax.ppermute(sent_two, LON, far)  3.44 us
    ppermute x1, starting transfers between devices, body(): lat_two = lax.ppermute(lat_two, LAT, far)  2.35 us
  transfers between devices with their start and end apart: 5, of which 3 were waited for; matrix products, arithmetic and copies ran while one was open for 0% of the time, Pallas kernels for 0%

profile of v4, /device:TPU:1, one launch (start us, length us, event | category | flops | bytes accessed | tf_op | source)
XLA Modules:
  0.0 51.6 jit_solution(9371234536973939795)
XLA Ops:
  0.6 0.6 %pad_add_fusion.at_ref = s32[2]{0:T(128)} fusion(s32[1]{0:T(128)} %bitcast.1, s32[1]{0:T(128)} %bitcast), kind=kLoop, calls=%fused_computation.7 | loop fusion | flops 2 | bytes 16 | tf_op jit(solution)/shard_map/stack | solution.py:406
  1.2 5.5 %prepare.1 = (bf16[32,128,128]{2,1,0:T(8,128)(2,1)}, bf16[2,128,128]{2,1,0:T(8,128)(2,1)}, bf16[2,128,128]{2,1,0:T(8,128)(2,1)}, bf16[2,32,128]{2,1,0:T(8,128)(2...) custom-call(s32[2]{0:T(128)} %pad_add_fusion.at_ref, bf16[69,32,128]{2,1,0:T(8,128)(2,1)} %x_ref.1, ...), custom_call_target="tpu_custom_call" | custom-call | flops 16777216 | bytes 4194304 | tf_op jit(solution)/shard_map/prepare/pallas_call | solution.py:367
  6.8 0.0 copy-start.3
  6.8 0.0 copy-start.4
  6.8 0.0 copy-start.9
  6.8 0.0 copy-start.8
  6.8 0.0 copy-start.10
  6.9 0.0 copy-start.7
  6.9 0.0 copy-start
  6.9 0.0 copy-start.1
  6.9 0.0 copy-start.5
  6.9 0.0 copy-start.6
  6.9 11.5 %all-to-all-start = ((bf16[128,40,128]{2,1,0:T(8,128)(2,1)}), bf16[128,40,128]{2,1,0:T(8,128)(2,1)S(1)}, u32[]{:S(2)}, u32[]{:S(2)}) async-start(bf16[128,40,128]{2,1,0:T(8,128)(2,1)} %bitcast.8), calls=%async_computation | async-start | bytes 2621440 | tf_op jit(solution)/shard_map/all_to_all | solution.py:408
  18.4 0.0 copy-done.3
  18.4 1.4 %collective-permute-start.2 = (bf16[2,32,128]{2,1,0:T(8,128)(2,1)S(1)}, bf16[2,32,128]{2,1,0:T(8,128)(2,1)S(1)}, u32[]{:S(2)}, u32[]{:S(2)}) collective-permute-start(bf16[2,32,128]{2,1,0:T(8,128)(2,1)S(1)} %copy-done.3), channel_id=1, source_target_pairs={{0,1},{1,0},{2,3},{3,2},{4,5},{5,4},{6,7},{7,6},{8,9},{9,8},{10,11... | collective-permute-start | bytes 49160 | tf_op jit(solution)/shard_map/ppermute | solution.py:415
  19.9 0.0 copy-done.4
  19.9 4.7 %collective-permute-start.3 = (bf16[2,32,128]{2,1,0:T(8,128)(2,1)S(1)}, bf16[2,32,128]{2,1,0:T(8,128)(2,1)S(1)}, u32[]{:S(2)}, u32[]{:S(2)}) collective-permute-start(bf16[2,32,128]{2,1,0:T(8,128)(2,1)S(1)} %copy-done.4), channel_id=1, source_target_pairs={{0,7},{1,2},{2,1},{3,4},{4,3},{5,6},{6,5},{7,0},{8,15},{9,10},{10,... | collective-permute-start | bytes 49160 | tf_op jit(solution)/shard_map/ppermute | solution.py:416
  24.6 0.0 copy-done.9
  24.6 0.9 %collective-permute-start = (bf16[2,128,128]{2,1,0:T(8,128)(2,1)S(1)}, bf16[2,128,128]{2,1,0:T(8,128)(2,1)S(1)}, u32[]{:S(2)}, u32[]{:S(2)}) collective-permute-start(bf16[2,128,128]{2,1,0:T(8,128)(2,1)S(1)} %copy-done.9), channel_id=1, source_target_pairs={{0,8},{8,0},{16,24},{24,16},{32,40},{40,32},{48,56},{56,48},{64,72... | collective-permute-start | bytes 196616 | tf_op jit(solution)/shard_map/ppermute | solution.py:412
  25.5 0.0 copy-done.8
  25.5 2.4 %collective-permute-start.1 = (bf16[2,128,128]{2,1,0:T(8,128)(2,1)S(1)}, bf16[2,128,128]{2,1,0:T(8,128)(2,1)S(1)}, u32[]{:S(2)}, u32[]{:S(2)}) collective-permute-start(bf16[2,128,128]{2,1,0:T(8,128)(2,1)S(1)} %copy-done.8), channel_id=1, source_target_pairs={{8,16},{16,8},{24,32},{32,24},{40,48},{48,40},{56,64},{64,56},{72,... | collective-permute-start | bytes 196616 | tf_op jit(solution)/shard_map/ppermute | solution.py:413
  27.9 0.0 copy-done.10
  27.9 0.0 copy-done.7
  28.0 0.0 collective-permute-done.2.lon_one_ref
  28.0 3.4 %collective-permute-done.3.lon_two_ref = bf16[2,32,128]{2,1,0:T(8,128)(2,1)S(1)} collective-permute-done((bf16[2,32,128]{2,1,0:T(8,128)(2,1)S(1)}, bf16[2,32,128]{2,1,0:T(8,128)(2,1)S(1)}, u32[]{:S(2)}, u32[]{:S(2)}) %collective-permute-start.3) | collective-permute-done | bytes 16416 | tf_op jit(solution)/shard_map/ppermute | solution.py:416
  31.4 0.0 collective-permute-done.lat_one_ref
  31.4 4.6 %collective-permute-done.1.lat_two_ref = bf16[2,128,128]{2,1,0:T(8,128)(2,1)S(1)} collective-permute-done((bf16[2,128,128]{2,1,0:T(8,128)(2,1)S(1)}, bf16[2,128,128]{2,1,0:T(8,128)(2,1)S(1)}, u32[]{:S(2)}, u32[]{:S(2)}) %collective-permute-start.1) | collective-permute-done | bytes 65568 | tf_op jit(solution)/shard_map/ppermute | solution.py:413
  36.1 3.6 %all-to-all-done.moved_ref = bf16[128,40,128]{2,1,0:T(8,128)(2,1)S(1)} async-done(((bf16[128,40,128]{2,1,0:T(8,128)(2,1)}), bf16[128,40,128]{2,1,0:T(8,128)(2,1)S(1)}, u32[]{:S(2)}, u32[]{:S(2)}) %all-to-all-start) | async-done | bytes 1310752 | tf_op jit(solution)/shard_map/all_to_all | solution.py:408
  39.7 0.0 copy-done
  39.7 0.0 copy-done.1
  39.7 1.2 %copy-done.2 = bf16[32,128,128]{2,1,0:T(8,128)(2,1)S(1)} copy-done((bf16[32,128,128]{2,1,0:T(8,128)(2,1)S(1)}, bf16[32,128,128]{2,1,0:T(8,128)(2,1)}, u32[]{:S(2)}) %copy-start.2) | copy-done | bytes 1048600
  40.9 10.6 %convs.1 = (bf16[256,32,128]{2,1,0:T(8,128)(2,1)}, bf16[69,32,128]{2,1,0:T(8,128)(2,1)}) custom-call(s32[2]{0:T(128)S(1)} %copy-done, s32[69]{0:T(128)S(1)} %fusion.1.place_ref, bf16[32,128,128]{2,1,0:T(8,128)(2,1)S(1)} %copy-done.2, bf16[2,128,128]{2,1,0:T(8,128)(2,1)S(1)} %collective-permute-done.lat_one_ref, ...), custom_call_target="tpu_custom_call" | custom-call | flops 6569852928 | bytes 8388608 | tf_op jit(solution)/shard_map/convs/pallas_call | solution.py:232
  (5 shorter events, 0.0 us)
Async XLA Ops:
  6.8 11.6 %copy-start.3 = (bf16[2,32,128]{2,1,0:T(8,128)(2,1)S(1)}, bf16[2,32,128]{2,1,0:T(8,128)(2,1)}, u32[]{:S(2)}) copy-start(bf16[2,32,128]{2,1,0:T(8,128)(2,1)} %get-tuple-element.11.sent_one_ref) | copy-start | bytes 49156
  6.8 13.0 %copy-start.4 = (bf16[2,32,128]{2,1,0:T(8,128)(2,1)S(1)}, bf16[2,32,128]{2,1,0:T(8,128)(2,1)}, u32[]{:S(2)}) copy-start(bf16[2,32,128]{2,1,0:T(8,128)(2,1)} %get-tuple-element.12.sent_two_ref) | copy-start | bytes 49156
  6.8 17.8 %copy-start.9 = (bf16[2,128,128]{2,1,0:T(8,128)(2,1)S(1)}, bf16[2,128,128]{2,1,0:T(8,128)(2,1)}, u32[]{:S(2)}) copy-start(bf16[2,128,128]{2,1,0:T(8,128)(2,1)} %get-tuple-element.9) | copy-start | bytes 196612
  6.8 18.7 %copy-start.8 = (bf16[2,128,128]{2,1,0:T(8,128)(2,1)S(1)}, bf16[2,128,128]{2,1,0:T(8,128)(2,1)}, u32[]{:S(2)}) copy-start(bf16[2,128,128]{2,1,0:T(8,128)(2,1)} %get-tuple-element.10) | copy-start | bytes 196612
  6.8 21.1 %copy-start.10 = (s32[69]{0:T(128)S(1)}, s32[69]{0:T(128)}, u32[]{:S(2)}) copy-start(s32[69]{0:T(128)} %param.9) | copy-start | bytes 832
  6.9 21.1 %copy-start.7 = (bf16[9,256,69]{1,2,0:T(8,128)(2,1)S(1)}, bf16[9,256,69]{1,2,0:T(8,128)(2,1)}, u32[]{:S(2)}) copy-start(bf16[9,256,69]{1,2,0:T(8,128)(2,1)} %param.10) | copy-start | bytes 953860
  6.9 32.8 %copy-start = (s32[2]{0:T(128)S(1)}, s32[2]{0:T(128)}, u32[]{:S(2)}) copy-start(s32[2]{0:T(128)} %pad_add_fusion.at_ref) | copy-start | bytes 28
  6.9 32.8 %copy-start.1 = (bf16[9,256,256]{2,1,0:T(8,128)(2,1)S(1)}, bf16[9,256,256]{2,1,0:T(8,128)(2,1)}, u32[]{:S(2)}) copy-start(bf16[9,256,256]{2,1,0:T(8,128)(2,1)} %w2_raw_ref.1) | copy-start | bytes 3538948
  6.9 32.8 %copy-start.5 = (f32[256]{0:T(256)S(1)}, f32[256]{0:T(256)}, u32[]{:S(2)}) copy-start(f32[256]{0:T(256)} %param.11) | copy-start | bytes 3076
  6.9 32.8 %copy-start.6 = (f32[256]{0:T(256)S(1)}, f32[256]{0:T(256)}, u32[]{:S(2)}) copy-start(f32[256]{0:T(256)} %param.13) | copy-start | bytes 3076
  6.9 32.8 %all-to-all-start = ((bf16[128,40,128]{2,1,0:T(8,128)(2,1)}), bf16[128,40,128]{2,1,0:T(8,128)(2,1)S(1)}, u32[]{:S(2)}, u32[]{:S(2)}) async-start(bf16[128,40,128]{2,1,0:T(8,128)(2,1)} %bitcast.8), calls=%async_computation | async-start | bytes 2621440 | tf_op jit(solution)/shard_map/all_to_all | solution.py:408
  18.4 9.5 %collective-permute-start.2 = (bf16[2,32,128]{2,1,0:T(8,128)(2,1)S(1)}, bf16[2,32,128]{2,1,0:T(8,128)(2,1)S(1)}, u32[]{:S(2)}, u32[]{:S(2)}) collective-permute-start(bf16[2,32,128]{2,1,0:T(8,128)(2,1)S(1)} %copy-done.3), channel_id=1, source_target_pairs={{0,1},{1,0},{2,3},{3,2},{4,5},{5,4},{6,7},{7,6},{8,9},{9,8},{10,11... | collective-permute-start | bytes 49160 | tf_op jit(solution)/shard_map/ppermute | solution.py:415
  19.9 11.6 %collective-permute-start.3 = (bf16[2,32,128]{2,1,0:T(8,128)(2,1)S(1)}, bf16[2,32,128]{2,1,0:T(8,128)(2,1)S(1)}, u32[]{:S(2)}, u32[]{:S(2)}) collective-permute-start(bf16[2,32,128]{2,1,0:T(8,128)(2,1)S(1)} %copy-done.4), channel_id=1, source_target_pairs={{0,7},{1,2},{2,1},{3,4},{4,3},{5,6},{6,5},{7,0},{8,15},{9,10},{10,... | collective-permute-start | bytes 49160 | tf_op jit(solution)/shard_map/ppermute | solution.py:416
  24.6 6.8 %collective-permute-start = (bf16[2,128,128]{2,1,0:T(8,128)(2,1)S(1)}, bf16[2,128,128]{2,1,0:T(8,128)(2,1)S(1)}, u32[]{:S(2)}, u32[]{:S(2)}) collective-permute-start(bf16[2,128,128]{2,1,0:T(8,128)(2,1)S(1)} %copy-done.9), channel_id=1, source_target_pairs={{0,8},{8,0},{16,24},{24,16},{32,40},{40,32},{48,56},{56,48},{64,72... | collective-permute-start | bytes 196616 | tf_op jit(solution)/shard_map/ppermute | solution.py:412
  25.5 10.5 %collective-permute-start.1 = (bf16[2,128,128]{2,1,0:T(8,128)(2,1)S(1)}, bf16[2,128,128]{2,1,0:T(8,128)(2,1)S(1)}, u32[]{:S(2)}, u32[]{:S(2)}) collective-permute-start(bf16[2,128,128]{2,1,0:T(8,128)(2,1)S(1)} %copy-done.8), channel_id=1, source_target_pairs={{8,16},{16,8},{24,32},{32,24},{40,48},{48,40},{56,64},{64,56},{72,... | collective-permute-start | bytes 196616 | tf_op jit(solution)/shard_map/ppermute | solution.py:413
  39.7 1.2 %copy-start.2 = (bf16[32,128,128]{2,1,0:T(8,128)(2,1)S(1)}, bf16[32,128,128]{2,1,0:T(8,128)(2,1)}, u32[]{:S(2)}) copy-start(bf16[32,128,128]{2,1,0:T(8,128)(2,1)} %get-tuple-element.8.x_ref) | copy-start | bytes 3145732

commit v5 on v4

--- a/solution.py
+++ b/solution.py
@@ -15,8 +15,9 @@
 EXTRA = 8
 X_PART = 24
 SPILL = 13
-LAT_COUNT = 16
+GROUP = 72
 PREPARE_VMEM = 60 * 2**20
+CONVS_VMEM = 40 * 2**20
 GELU_C = 0.7978845608028654
 
 
@@ -24,67 +25,70 @@
     return (0.5 * v) * (1.0 + jnp.tanh(v * (GELU_C + (GELU_C * 0.044715) * (v * v))))
 
 
+def pack(minus, zero, plus, lanes):
+    over = 2 * GROUP - LANES
+    turned = pltpu.roll(zero, GROUP, axis=1)
+    low = jnp.where(lanes < GROUP, minus, turned)
+    high = jnp.where(lanes < over, turned, pltpu.roll(plus, over, axis=1))
+    return low, high
+
+
+def shifted(main, before, after, sub8):
+    cols = main.shape[0]
+    minus = pltpu.roll(main, 1, axis=0)
+    minus = jnp.concatenate([jnp.where(sub8 == 0, before, minus[:8]), minus[8:]], axis=0)
+    plus = pltpu.roll(main, cols - 1, axis=0)
+    plus = jnp.concatenate([plus[: cols - 8], jnp.where(sub8 == 7, after, plus[cols - 8 :])], axis=0)
+    return minus, plus
+
+
 def conv_kernel(
     channels, rows, cols, hid,
-    at_ref, place_ref, x_ref, lat_one_ref, lat_two_ref, sent_one_ref, sent_two_ref, lon_one_ref, lon_two_ref,
-    w1_raw_ref, b1_ref, w2_raw_ref, b2_ref, moved_ref, out_ref, tile_ref,
-    w1_ref, w2_ref, taps_ref, edge_ref, edge_taps_ref, edge_hid_ref, west_ref, mid_ref, east_ref,
-    turned_ref, done_ref, sem, take_sem,
+    place_ref, taps_hbm_ref, lat_one_ref, lat_two_ref, sent_one_ref, sent_two_ref, lon_one_ref, lon_two_ref,
+    w1_hbm_ref, b1_ref, w2_hbm_ref, b2_ref, moved_ref, out_ref, tile_ref,
+    raw_taps_ref, w1_ref, w2_ref, taps_ref, edge_ref, edge_taps_ref, edge_hid_ref, west_ref, mid_ref, east_ref,
+    turned_ref, done_ref, sem, take_sem, load_sem,
 ):
-    n_lat, n_lon = LAT_COUNT, moved_ref.shape[0] // LAT_COUNT
+    n_lat, n_lon = lax.axis_size(LAT), lax.axis_size(LON)
     cells = rows * cols * moved_ref.shape[0]
-    lat, lon = at_ref[0], at_ref[1]
+    lat, lon = lax.axis_index(LAT), lax.axis_index(LON)
     first = lat == 0
     last = lat == n_lat - 1
     odd_lat = lat % 2 == 1
     odd_lon = lon % 2 == 1
     lane = lax.broadcasted_iota(jnp.int32, (cols, LANES), 1)
     sub = lax.broadcasted_iota(jnp.int32, (8, LANES), 0)
+    lane8 = lax.broadcasted_iota(jnp.int32, (8, LANES), 1)
     sub_hid = lax.broadcasted_iota(jnp.int32, (8, hid), 0)
-    group = w1_raw_ref.shape[1]
+    group = GROUP
     over = 2 * group - LANES
-
-    def weights():
-        for a in range(3):
-            for b in range(3):
-                w1_ref[a * 2 * LANES + b * group : a * 2 * LANES + (b + 1) * group, :] = w1_raw_ref[3 * a + b]
-            w1_ref[a * 2 * LANES + 3 * group : (a + 1) * 2 * LANES, :] = jnp.zeros(
-                (2 * LANES - 3 * group, hid), jnp.bfloat16
-            )
-        for tap in range(9):
-            w2_ref[tap * hid : (tap + 1) * hid, :] = w2_raw_ref[tap].T
 
     def norm(raw):
         return (raw.astype(jnp.float32) - mean) * scale
-
-    def pack(minus, zero, plus, lanes):
-        turned = pltpu.roll(zero, group, axis=1)
-        low = jnp.where(lanes < group, minus, turned)
-        high = jnp.where(lanes < over, turned, pltpu.roll(plus, over, axis=1))
-        return low, high
-
-    def shifted(main, before, after, sub8):
-        minus = pltpu.roll(main, 1, axis=0)
-        minus = jnp.concatenate([jnp.where(sub8 == 0, before, minus[:8]), minus[8:]], axis=0)
-        plus = pltpu.roll(main, cols - 1, axis=0)
-        plus = jnp.concatenate([plus[: cols - 8], jnp.where(sub8 == 7, after, plus[cols - 8 :])], axis=0)
-        return minus, plus
 
     def lat_row(row):
         if row < 2:
             return jnp.where(odd_lat, lat_one_ref[row], lat_two_ref[row]), jnp.logical_not(first)
-        if row >= rows + 2:
-            row = row - rows - 2
-            return jnp.where(odd_lat, lat_two_ref[row], lat_one_ref[row]), jnp.logical_not(last)
-        return x_ref[row - 2], None
+        row = row - rows - 2
+        return jnp.where(odd_lat, lat_two_ref[row], lat_one_ref[row]), jnp.logical_not(last)
 
     def build(row):
-        raw, keep = lat_row(row)
-        main = norm(raw)
-        if keep is not None:
-            main = jnp.where(keep, main, 0.0)
-        minus, plus = shifted(main, edge_ref[0, 1, row : row + 1, :], edge_ref[1, 1, row : row + 1, :], sub)
-        low, high = pack(minus, main, plus, lane)
+        before, after = edge_ref[0, 1, row : row + 1, :], edge_ref[1, 1, row : row + 1, :]
+        if 2 <= row < rows + 2:
+            raw = raw_taps_ref[row - 2].astype(jnp.float32)
+            low = (raw[:, 0:LANES] - mean_low) * scale_low
+            high = (raw[:, LANES : 2 * LANES] - mean_high) * scale_high
+            head = jnp.where(jnp.logical_and(sub == 0, lane8 < group), before, low[:8])
+            tail = jnp.where(
+                jnp.logical_and(sub == 7, lane8 >= over), pltpu.roll(after, over, axis=1), high[cols - 8 :]
+            )
+            low = jnp.concatenate([head, low[8:]], axis=0)
+            high = jnp.concatenate([high[: cols - 8], tail], axis=0)
+        else:
+            raw, keep = lat_row(row)
+            main = jnp.where(keep, norm(raw), 0.0)
+            minus, plus = shifted(main, before, after, sub)
+            low, high = pack(minus, main, plus, lane)
         taps_ref[row, :, 0:LANES] = low.astype(jnp.bfloat16)
         taps_ref[row, :, LANES : 2 * LANES] = high.astype(jnp.bfloat16)
 
@@ -189,11 +193,23 @@
     steps = rows // BLOCK
     taken = tile_ref.shape[0]
 
+    def load_taps(t):
+        low = 0 if t == 0 else t * BLOCK + 2
+        part = pl.ds(low, min((t + 1) * BLOCK + 2, rows) - low)
+        return pltpu.make_async_copy(taps_hbm_ref.at[part], raw_taps_ref.at[part], load_sem.at[t])
+
+    load_weights = pltpu.make_async_copy(w2_hbm_ref, w2_ref, load_sem.at[steps])
+    load_first = pltpu.make_async_copy(w1_hbm_ref, w1_ref, load_sem.at[steps + 1])
+    load_first.start()
+    load_taps(0).start()
+    load_weights.start()
+    for t in range(1, steps):
+        load_taps(t).start()
+
     @pl.loop(0, taken)
     def _(c):
         pltpu.make_async_copy(moved_ref.at[place_ref[c], 0:rows, :], tile_ref.at[c], take_sem).start()
 
-    weights()
     sums = jnp.sum(moved_ref[:, rows : rows + EXTRA, :].astype(jnp.float32), axis=0)
     line = lax.broadcasted_iota(jnp.int32, (1, LANES), 1)
     mean = (sums[0:1] + sums[1:2] + sums[2:3]) / cells
@@ -202,10 +218,17 @@
     square = jnp.where(line < channels, square, 0.0)
     scale = 1.0 / jnp.sqrt(square - mean * mean + 1e-05)
     scale = jnp.where(line < channels, scale, 0.0)
+    mean_low, mean_high = pack(mean, mean, mean, line)
+    scale_low, scale_high = pack(scale, scale, scale, line)
+    load_first.wait()
     edges()
+    load_taps(0).wait()
     for r in range(BLOCK + 4):
         build(r)
     hidden(0, BLOCK + 2)
+    for t in range(1, steps):
+        load_taps(t).wait()
+    load_weights.wait()
     for r in range(BLOCK + 4, 2 * BLOCK + 4):
         build(r)
     for t in range(steps):
@@ -220,8 +243,8 @@
         put(t).wait()
 
 
-def convs(channels, at, place, x, lat_one, lat_two, sent_one, sent_two, lon_one, lon_two, w1, b1, w2, b2, moved):
-    rows, cols = x.shape[0], x.shape[1]
+def convs(channels, place, taps, lat_one, lat_two, sent_one, sent_two, lon_one, lon_two, w1, b1, w2, b2, moved):
+    rows, cols = taps.shape[0], taps.shape[1]
     hid = w2.shape[1]
     taken = place.shape[0]
     tall = (rows + 4 + 7) // 8 * 8 + 8
@@ -235,9 +258,10 @@
             jax.ShapeDtypeStruct((hid, rows, cols), jnp.bfloat16),
             jax.ShapeDtypeStruct((taken, rows, cols), jnp.bfloat16),
         ),
-        in_specs=[smem, smem] + [vmem] * 12,
+        in_specs=[smem, hbm] + [vmem] * 6 + [hbm, vmem, hbm, vmem, vmem],
         out_specs=(hbm, hbm),
         scratch_shapes=[
+            pltpu.VMEM((rows, cols, 2 * LANES), jnp.bfloat16),
             pltpu.VMEM((6 * LANES, hid), jnp.bfloat16),
             pltpu.VMEM((9 * hid, hid), jnp.bfloat16),
             pltpu.VMEM((rows + 4, cols, 2 * LANES), jnp.bfloat16),
@@ -251,21 +275,70 @@
             pltpu.VMEM((rows // BLOCK, hid, BLOCK, cols), jnp.bfloat16),
             pltpu.SemaphoreType.DMA((rows // BLOCK,)),
             pltpu.SemaphoreType.DMA,
+            pltpu.SemaphoreType.DMA((rows // BLOCK + 2,)),
         ],
-        compiler_params=pltpu.CompilerParams(vmem_limit_bytes=40 * 2**20),
+        compiler_params=pltpu.CompilerParams(vmem_limit_bytes=CONVS_VMEM),
         cost_estimate=pl.CostEstimate(flops=flops, bytes_accessed=8 * 2**20, transcendentals=0),
         name="convs",
-    )(at, place, x, lat_one, lat_two, sent_one, sent_two, lon_one, lon_two, w1, b1, w2, b2, moved)
+    )(place, taps, lat_one, lat_two, sent_one, sent_two, lon_one, lon_two, w1, b1, w2, b2, moved)
+
+
+def stage_kernel(x_ref, w1_raw_ref, w2_raw_ref, taps_ref, w1_ref, w2_ref, wide_ref):
+    channels, rows, cols = x_ref.shape
+    hid = w2_ref.shape[1]
+    padded = wide_ref.shape[0] // rows
+    wide_ref[channels * rows :, :] = jnp.zeros(((padded - channels) * rows, cols), jnp.float32)
+    wide_ref[0 : channels * rows, :] = x_ref[...].astype(jnp.float32).reshape(channels * rows, cols)
+    rest = jnp.zeros((LANES - padded, cols), jnp.float32)
+    lane = lax.broadcasted_iota(jnp.int32, (cols, LANES), 1)
+    sub = lax.broadcasted_iota(jnp.int32, (8, LANES), 0)
+    for r in range(rows):
+        one = wide_ref[pl.ds(r, padded, stride=rows), :]
+        main = jnp.concatenate([one, rest], axis=0).T
+        minus, plus = shifted(main, 0.0, 0.0, sub)
+        low, high = pack(minus, main, plus, lane)
+        taps_ref[r, :, 0:LANES] = low.astype(jnp.bfloat16)
+        taps_ref[r, :, LANES : 2 * LANES] = high.astype(jnp.bfloat16)
+    group = w1_raw_ref.shape[1]
+    for a in range(3):
+        for b in range(3):
+            w1_ref[a * 2 * LANES + b * group : a * 2 * LANES + (b + 1) * group, :] = w1_raw_ref[3 * a + b]
+        w1_ref[a * 2 * LANES + 3 * group : (a + 1) * 2 * LANES, :] = jnp.zeros(
+            (2 * LANES - 3 * group, hid), jnp.bfloat16
+        )
+    for tap in range(9):
+        w2_ref[tap * hid : (tap + 1) * hid, :] = w2_raw_ref[tap].T
+
+
+def stage(current, w1, w2):
+    _, rows, cols = current.shape
+    hid = w2.shape[1]
+    vmem = pl.BlockSpec(memory_space=pltpu.VMEM)
+    return pl.pallas_call(
+        stage_kernel,
+        out_shape=(
+            jax.ShapeDtypeStruct((rows, cols, 2 * LANES), jnp.bfloat16),
+            jax.ShapeDtypeStruct((6 * LANES, hid), jnp.bfloat16),
+            jax.ShapeDtypeStruct((9 * hid, hid), jnp.bfloat16),
+        ),
+        in_specs=[vmem] * 3,
+        out_specs=(vmem,) * 3,
+        scratch_shapes=[pltpu.VMEM((GROUP * rows, cols), jnp.float32)],
+        compiler_params=pltpu.CompilerParams(vmem_limit_bytes=16 * 2**20),
+        cost_estimate=pl.CostEstimate(flops=2**25, bytes_accessed=2**22, transcendentals=0),
+        name="stage",
+    )(current, w1, w2)
 
 
 def prepare_kernel(
-    channels, at_ref, x_ref, fields_ref,
-    turned_ref, lat_one_ref, lat_two_ref, lon_one_ref, lon_two_ref, blocks_ref,
-    raw_ref, wide_ref, held_ref, extra_ref, first_ref, last_ref, x_sem, in_sem, out_sem, extra_sem,
+    channels, x_ref, fields_ref,
+    lat_one_ref, lat_two_ref, lon_one_ref, lon_two_ref, blocks_ref,
+    raw_ref, wide_ref, gather_ref, partial_ref, held_ref, extra_ref, lat_ref, lon_ref, first_ref, last_ref,
+    x_sem, in_sem, out_sem, extra_sem, halo_sem,
 ):
-    rows, cols = turned_ref.shape[0], turned_ref.shape[1]
+    rows, cols = raw_ref.shape[1], raw_ref.shape[2]
     n_lon, n_lat = blocks_ref.shape[0], blocks_ref.shape[1]
-    lat, lon = at_ref[0], at_ref[1]
+    lat, lon = lax.axis_index(LAT), lax.axis_index(LON)
 
     def load(j):
         part = pl.ds(j * X_PART, min(X_PART, channels - j * X_PART))
@@ -282,6 +355,12 @@
     def put_extra(j):
         return pltpu.make_async_copy(extra_ref.at[j], blocks_ref.at[j, :, rows : rows + EXTRA, :], extra_sem.at[j])
 
+    halos = [
+        pltpu.make_async_copy(lat_ref.at[0], lat_one_ref, halo_sem.at[0]),
+        pltpu.make_async_copy(lat_ref.at[1], lat_two_ref, halo_sem.at[1]),
+        pltpu.make_async_copy(lon_ref.at[0], lon_one_ref, halo_sem.at[2]),
+        pltpu.make_async_copy(lon_ref.at[1], lon_two_ref, halo_sem.at[3]),
+    ]
     loads = (channels + X_PART - 1) // X_PART
     for j in range(loads):
         load(j).start()
@@ -289,36 +368,54 @@
         get(j).start()
     padded = wide_ref.shape[0] // rows
     wide_ref[channels * rows :, :] = jnp.zeros(((padded - channels) * rows, cols), jnp.float32)
+    partial_ref[:, channels * 8 :, :] = jnp.zeros((2, (padded - channels) * 8, cols), jnp.float32)
     for j in range(loads):
         load(j).wait()
         low, high = j * X_PART, min((j + 1) * X_PART, channels)
-        wide_ref[low * rows : high * rows, :] = (
-            raw_ref[low:high].astype(jnp.float32).reshape((high - low) * rows, cols)
-        )
+        count = high - low
+        value = raw_ref[low:high].astype(jnp.float32)
+        wide_ref[low * rows : high * rows, :] = value.reshape(count * rows, cols)
+        value = value.reshape(count, rows // 8, 8, cols)
+        partial_ref[0, low * 8 : high * 8, :] = jnp.sum(value, axis=1).reshape(count * 8, cols)
+        partial_ref[1, low * 8 : high * 8, :] = jnp.sum(value * value, axis=1).reshape(count * 8, cols)
     rest = jnp.zeros((LANES - padded, cols), jnp.float32)
-    total = jnp.zeros((padded, cols), jnp.float32)
-    square = jnp.zeros((padded, cols), jnp.float32)
+    odd_lat = lat % 2 == 1
+    odd_lon = lon % 2 == 1
+    lane = lax.broadcasted_iota(jnp.int32, (padded, cols), 1)
+    columns = jnp.zeros((padded, cols), jnp.float32)
+    kept = {}
     for r in range(rows):
         one = wide_ref[pl.ds(r, padded, stride=rows), :]
-        total += one
-        square += one * one
-        turned = jnp.concatenate([one, rest], axis=0).T
-        turned_ref[r] = turned.astype(jnp.bfloat16)
-        for j in range(2):
-            first_ref[j, r : r + 1, :] = turned[j : j + 1]
-            last_ref[j, r : r + 1, :] = turned[cols - 2 + j : cols - 1 + j]
-        if r % 4 == 3:
-            get(r // 4).wait()
-            put(r // 4).start()
-
-    def parts(value):
+        columns = jnp.where(lane // 4 == r, pltpu.roll(one, (2 + 4 * r) % cols, axis=1), columns)
+        if r in (0, 1, rows - 2, rows - 1):
+            kept[r] = jnp.concatenate([one, rest], axis=0).T
+    for j in range(2):
+        low, high = kept[j], kept[rows - 2 + j]
+        lat_ref[0, j] = jnp.where(odd_lat, low, high).astype(jnp.bfloat16)
+        lat_ref[1, j] = jnp.where(odd_lat, high, low).astype(jnp.bfloat16)
+    halos[0].start()
+    halos[1].start()
+    gather_ref[...] = jnp.concatenate([columns, rest], axis=0).T
+    for j in range(2):
+        last_ref[j] = gather_ref[pl.ds(j, rows, stride=4), :]
+        first_ref[j] = gather_ref[pl.ds(2 + j, rows, stride=4), :]
+    low, high = first_ref[...], last_ref[...]
+    lon_ref[0] = jnp.where(odd_lon, low, high).astype(jnp.bfloat16)
+    lon_ref[1] = jnp.where(odd_lon, high, low).astype(jnp.bfloat16)
+    halos[2].start()
+    halos[3].start()
+
+    def parts(which):
+        value = partial_ref[which, pl.ds(0, padded, stride=8), :]
+        for i in range(1, 8):
+            value = value + partial_ref[which, pl.ds(i, padded, stride=8), :]
         value = jnp.sum(jnp.concatenate([value, rest], axis=0).T, axis=0, keepdims=True)
         high = value.astype(jnp.bfloat16).astype(jnp.float32)
         value = value - high
         middle = value.astype(jnp.bfloat16).astype(jnp.float32)
         return [high, middle, value - middle]
 
-    sums = parts(total) + parts(square)
+    sums = parts(0) + parts(1)
     line = lax.broadcasted_iota(jnp.int32, (1, LANES), 1)
 
     def extra(down, right):
@@ -341,54 +438,55 @@
         extra_ref[(lon + n_lon + right) % n_lon, (lat + n_lat + down) % n_lat] = extra(down, right)
     for j in range(n_lon):
         put_extra(j).start()
-    odd_lat = lat % 2 == 1
-    odd_lon = lon % 2 == 1
-    low = turned_ref[0:2]
-    high = turned_ref[rows - 2 : rows]
-    lat_one_ref[...] = jnp.where(odd_lat, low, high)
-    lat_two_ref[...] = jnp.where(odd_lat, high, low)
-    low = first_ref[...].astype(jnp.bfloat16)
-    high = last_ref[...].astype(jnp.bfloat16)
-    lon_one_ref[...] = jnp.where(odd_lon, low, high)
-    lon_two_ref[...] = jnp.where(odd_lon, high, low)
+    for j in range(n_lon):
+        get(j).wait()
+        put(j).start()
     for j in range(n_lon):
         put(j).wait()
         put_extra(j).wait()
-
-
-def prepare(at, current, next_fields, n_lon):
+    for halo in halos:
+        halo.wait()
+
+
+def prepare(current, next_fields, n_lon):
     channels, rows, cols = current.shape
-    vmem = pl.BlockSpec(memory_space=pltpu.VMEM)
     hbm = pl.BlockSpec(memory_space=pl.ANY)
     height = next_fields.shape[1]
-    padded = (channels + 7) // 8 * 8
     lat_row = jax.ShapeDtypeStruct((2, cols, LANES), jnp.bfloat16)
     lon_row = jax.ShapeDtypeStruct((2, rows, LANES), jnp.bfloat16)
     return pl.pallas_call(
         functools.partial(prepare_kernel, channels),
         out_shape=(
-            jax.ShapeDtypeStruct((rows, cols, LANES), jnp.bfloat16),
             lat_row, lat_row, lon_row, lon_row,
             jax.ShapeDtypeStruct((n_lon, height // rows, rows + EXTRA, cols), jnp.bfloat16),
         ),
-        in_specs=[pl.BlockSpec(memory_space=pltpu.SMEM), hbm, hbm],
-        out_specs=(vmem,) * 5 + (hbm,),
+        in_specs=[hbm, hbm],
+        out_specs=(hbm,) * 5,
         scratch_shapes=[
             pltpu.VMEM((channels, rows, cols), jnp.bfloat16),
-            pltpu.VMEM((padded * rows, cols), jnp.float32),
+            pltpu.VMEM((GROUP * rows, cols), jnp.float32),
+            pltpu.VMEM((cols, LANES), jnp.float32),
+            pltpu.VMEM((2, GROUP * 8, cols), jnp.float32),
             pltpu.VMEM((n_lon, height, cols), jnp.bfloat16),
             pltpu.VMEM((n_lon, height // rows, EXTRA, cols), jnp.bfloat16),
+            pltpu.VMEM((2, 2, cols, LANES), jnp.bfloat16),
+            pltpu.VMEM((2, 2, rows, LANES), jnp.bfloat16),
             pltpu.VMEM((2, rows, LANES), jnp.float32),
             pltpu.VMEM((2, rows, LANES), jnp.float32),
             pltpu.SemaphoreType.DMA(((channels + X_PART - 1) // X_PART,)),
             pltpu.SemaphoreType.DMA((n_lon,)),
             pltpu.SemaphoreType.DMA((n_lon,)),
             pltpu.SemaphoreType.DMA((n_lon,)),
+            pltpu.SemaphoreType.DMA((4,)),
         ],
         compiler_params=pltpu.CompilerParams(vmem_limit_bytes=PREPARE_VMEM),
         cost_estimate=pl.CostEstimate(flops=2**24, bytes_accessed=2**22, transcendentals=0),
         name="prepare",
-    )(at, current, next_fields)
+    )(current, next_fields)
+
+
+def in_hbm(array):
+    return pltpu.with_memory_space_constraint(array, pltpu.HBM)
 
 
 def pairs(count, periodic):
@@ -403,8 +501,7 @@
     channels, rows, cols = current.shape
     n_lat = lax.axis_size(LAT)
     n_lon = lax.axis_size(LON)
-    at = jnp.stack([lax.axis_index(LAT), lax.axis_index(LON)]).astype(jnp.int32)
-    turned, lat_one, lat_two, sent_one, sent_two, blocks = prepare(at, current, next_fields, n_lon)
+    lat_one, lat_two, sent_one, sent_two, blocks = prepare(current, next_fields, n_lon)
     moved = lax.all_to_all(
         blocks.reshape(n_lon * n_lat, rows + EXTRA, cols), LON + LAT, split_axis=0, concat_axis=0, tiled=True
     )
@@ -414,11 +511,13 @@
     near, far = pairs(n_lon, True)
     lon_one = lax.ppermute(sent_one, LON, near)
     lon_two = lax.ppermute(sent_two, LON, far)
-    w1 = jnp.pad(first_weight.transpose(0, 2, 1), ((0, 0), (0, -channels % 8), (0, 0)))
+    w1 = jnp.pad(first_weight.transpose(0, 2, 1), ((0, 0), (0, GROUP - channels), (0, 0)))
+    taps, w1, w2 = stage(current, w1, second_weight)
     place = (reader_slot % n_lon) * n_lat + reader_slot // n_lon
+    taps, w1, w2 = in_hbm(taps), in_hbm(w1), in_hbm(w2)
     return convs(
-        channels, at, place, turned, lat_one, lat_two, sent_one, sent_two, lon_one, lon_two,
-        w1, first_bias[None], second_weight, second_bias[None], moved,
+        channels, place, taps, lat_one, lat_two, sent_one, sent_two, lon_one, lon_two,
+        w1, first_bias[None], w2, second_bias[None], moved,
     )
 
 

time: 51.8 us -> 49.7 us (0.959)
  waiting for transfers between devices: 11.7 us -> 5.31 us
  local copies, waits for them, and re-layouts: 1.3 us -> 4.17 us
  Pallas kernels: 16.2 us -> 17.9 us
  other arithmetic: 0.62 us -> 0.01 us
    ppermute x1, waiting for transfers between devices: 3.44 us -> 0.01 us  [body(): lon_two = lax.ppermute(sent_two, LON, far)]
    ppermute x1, waiting for transfers between devices: 4.65 us -> 1.69 us  [body(): lat_two = lax.ppermute(lat_two, LAT, far)]
    unnamed x22 -> x24, local copies, waits for them, and re-layouts: 1.27 us -> 3.16 us
    pallas_call x1, Pallas kernels: 10.6 us -> 12.1 us  [convs(): pl.pallas_call(functools.partial(conv_kernel, channels, rows, cols, hid),...]
    pad x1, local copies, waits for them, and re-layouts: 0.03 us -> 1.01 us  [body(): jnp.pad(first_weight.transpose(0, 2, 1), ((0, 0), (0, GROUP - channels),...]
    another operation x1 -> x0, other arithmetic: 0.61 us -> none  [body(): at = jnp.stack([lax.axis_index(LAT), lax.axis_index(LON)]).astype(jnp.int32)]
    pallas_call x1 -> x2, Pallas kernels: 5.55 us -> 5.85 us  [the longest x1 3.78 us: prepare(): pl.pallas_call(functools.partial(prepare_kernel, channels), out_shape=(la...]
  transfers between devices with their start and end apart: 5 -> 5, of which waited for: 3 -> 2; matrix products, arithmetic and copies ran while one was open for 0% -> 2% of each run, Pallas kernels for 0% -> 4%
where the time goes in v5:
time: 49.7 us; the launch traced here: 49.5 us
  starting transfers between devices  21.1 us (42%)
  Pallas kernels  17.9 us (36%)
  waiting for transfers between devices  5.31 us (11%)
  local copies, waits for them, and re-layouts  4.17 us (8%)
  between operations  0.95 us (2%)
    pallas_call x1, Pallas kernels, convs(): pl.pallas_call(functools.partial(conv_kernel, channels, rows, cols, hid),...  12.1 us
    all_to_all x1, starting transfers between devices, body(): lax.all_to_all(blocks.reshape(n_lon * n_lat, rows + EXTRA, cols), LON + L...  11.5 us
    ppermute x1, starting transfers between devices, body(): lon_two = lax.ppermute(sent_two, LON, far)  4.72 us
    pallas_call x1, Pallas kernels, prepare(): pl.pallas_call(functools.partial(prepare_kernel, channels), out_shape=(la...  3.78 us
    all_to_all x1, waiting for transfers between devices, body(): lax.all_to_all(blocks.reshape(n_lon * n_lat, rows + EXTRA, cols), LON + L...  3.61 us
    unnamed x24, local copies, waits for them, and re-layouts  3.16 us
    ppermute x1, starting transfers between devices, body(): lat_two = lax.ppermute(lat_two, LAT, far)  2.53 us
    pallas_call x1, Pallas kernels, stage(): pl.pallas_call(stage_kernel, out_shape=(jax.ShapeDtypeStruct((rows, cols,...  2.08 us
  transfers between devices with their start and end apart: 5, of which 2 were waited for; matrix products, arithmetic and copies ran while one was open for 2% of the time, Pallas kernels for 4%

profile of v5, /device:TPU:1, one launch (start us, length us, event | category | flops | bytes accessed | tf_op | source)
XLA Modules:
  0.0 49.5 jit_solution(8096921198356977079)
XLA Ops:
  0.6 3.8 %prepare.1 = (bf16[2,128,128]{2,1,0:T(8,128)(2,1)}, bf16[2,128,128]{2,1,0:T(8,128)(2,1)}, bf16[2,32,128]{2,1,0:T(8,128)(2,1)}, bf16[2,32,128]{2,1,0:T(8,128)(2,1)}, bf16[8,16,40,128]{3,2,1,0:T(8,128)(2,1)}) custom-call(bf16[69,32,128]{2,1,0:T(8,128)(2,1)} %x_ref.3, bf16[1,512,1024]{2,1,0:T(8,128)(2,1)} %fields_ref.1), custom_call_target="tpu_custom_call" | custom-call | flops 16777216 | bytes 4194304 | tf_op jit(solution)/shard_map/prepare/pallas_call | solution.py:457
  4.4 0.0 copy-start.5
  4.4 0.0 copy-start.6
  4.4 0.0 copy-start.10
  4.4 0.0 copy-start.9
  4.5 0.0 copy-start.11
  4.5 0.0 copy-start
  4.5 0.0 copy-start.1
  4.5 11.5 %all-to-all-start = ((bf16[128,40,128]{2,1,0:T(8,128)(2,1)}), bf16[128,40,128]{2,1,0:T(8,128)(2,1)S(1)}, u32[]{:S(2)}, u32[]{:S(2)}) async-start(bf16[128,40,128]{2,1,0:T(8,128)(2,1)} %bitcast.6), calls=%async_computation | async-start | bytes 2621440 | tf_op jit(solution)/shard_map/all_to_all | solution.py:505
  16.0 0.0 copy-done.5
  16.0 1.4 %collective-permute-start.2 = (bf16[2,32,128]{2,1,0:T(8,128)(2,1)S(1)}, bf16[2,32,128]{2,1,0:T(8,128)(2,1)S(1)}, u32[]{:S(2)}, u32[]{:S(2)}) collective-permute-start(bf16[2,32,128]{2,1,0:T(8,128)(2,1)S(1)} %copy-done.5), channel_id=1, source_target_pairs={{0,1},{1,0},{2,3},{3,2},{4,5},{5,4},{6,7},{7,6},{8,9},{9,8},{10,11... | collective-permute-start | bytes 49160 | tf_op jit(solution)/shard_map/ppermute | solution.py:512
  17.4 0.0 copy-done.6
  17.4 4.7 %collective-permute-start.3 = (bf16[2,32,128]{2,1,0:T(8,128)(2,1)S(1)}, bf16[2,32,128]{2,1,0:T(8,128)(2,1)S(1)}, u32[]{:S(2)}, u32[]{:S(2)}) collective-permute-start(bf16[2,32,128]{2,1,0:T(8,128)(2,1)S(1)} %copy-done.6), channel_id=1, source_target_pairs={{0,7},{1,2},{2,1},{3,4},{4,3},{5,6},{6,5},{7,0},{8,15},{9,10},{10,... | collective-permute-start | bytes 49160 | tf_op jit(solution)/shard_map/ppermute | solution.py:513
  22.2 0.0 copy-done.10
  22.2 0.9 %collective-permute-start = (bf16[2,128,128]{2,1,0:T(8,128)(2,1)S(1)}, bf16[2,128,128]{2,1,0:T(8,128)(2,1)S(1)}, u32[]{:S(2)}, u32[]{:S(2)}) collective-permute-start(bf16[2,128,128]{2,1,0:T(8,128)(2,1)S(1)} %copy-done.10), channel_id=1, source_target_pairs={{0,8},{8,0},{16,24},{24,16},{32,40},{40,32},{48,56},{56,48},{64,72... | collective-permute-start | bytes 196616 | tf_op jit(solution)/shard_map/ppermute | solution.py:509
  23.1 0.0 copy-done.9
  23.1 2.5 %collective-permute-start.1 = (bf16[2,128,128]{2,1,0:T(8,128)(2,1)S(1)}, bf16[2,128,128]{2,1,0:T(8,128)(2,1)S(1)}, u32[]{:S(2)}, u32[]{:S(2)}) collective-permute-start(bf16[2,128,128]{2,1,0:T(8,128)(2,1)S(1)} %copy-done.9), channel_id=1, source_target_pairs={{8,16},{16,8},{24,32},{32,24},{40,48},{48,40},{56,64},{64,56},{72,... | collective-permute-start | bytes 196616 | tf_op jit(solution)/shard_map/ppermute | solution.py:510
  25.7 0.0 copy-done.11
  25.7 0.0 copy-start.7
  25.7 0.0 copy-start.8
  25.7 1.0 %pad.4.w1_raw_ref = bf16[9,72,256]{2,1,0:T(8,128)(2,1)S(1)} pad(bf16[9,69,256]{2,1,0:T(8,128)(2,1)} %bitcast.7, bf16[]{:T(256)} %constant.32.clone.1), padding=0_0x0_3x0_0 | pad | bytes 649730 | tf_op jit(solution)/shard_map/jit(_pad)/pad | solution.py:514
  26.7 0.0 copy-done
  26.7 2.1 %stage.1 = (bf16[32,128,256]{2,1,0:T(8,128)(2,1)S(1)}, bf16[768,256]{1,0:T(8,128)(2,1)S(1)}, bf16[2304,256]{1,0:T(8,128)(2,1)S(1)}) custom-call(bf16[69,32,128]{2,1,0:T(8,128)(2,1)S(1)} %copy-done, bf16[9,72,256]{2,1,0:T(8,128)(2,1)S(1)} %pad.4.w1_raw_ref, bf16[9,256,256]{2,1,0:T(8,128)(2,1)S(1)} %copy-done.1), custom_call_target="tpu_custom_call" | custom-call | flops 33554432 | bytes 4194304 | tf_op jit(solution)/shard_map/stage/pallas_call | solution.py:317
  28.8 1.3 %copy-done.2 = bf16[32,128,256]{2,1,0:T(8,128)(2,1)} copy-done((bf16[32,128,256]{2,1,0:T(8,128)(2,1)}, bf16[32,128,256]{2,1,0:T(8,128)(2,1)S(1)}, u32[]{:S(2)}) %copy-start.2) | copy-done | bytes 2097176
  30.2 1.0 %copy-done.3 = bf16[2304,256]{1,0:T(8,128)(2,1)} copy-done((bf16[2304,256]{1,0:T(8,128)(2,1)}, bf16[2304,256]{1,0:T(8,128)(2,1)S(1)}, u32[]{:S(2)}) %copy-start.3) | copy-done | bytes 1179672
  31.2 0.7 %copy-done.4 = bf16[768,256]{1,0:T(8,128)(2,1)} copy-done((bf16[768,256]{1,0:T(8,128)(2,1)}, bf16[768,256]{1,0:T(8,128)(2,1)S(1)}, u32[]{:S(2)}) %copy-start.4) | copy-done | bytes 393240
  31.9 0.0 collective-permute-done.2.lon_one_ref
  31.9 0.0 collective-permute-done.3.lon_two_ref
  31.9 0.0 collective-permute-done.lat_one_ref
  32.0 1.7 %collective-permute-done.1.lat_two_ref = bf16[2,128,128]{2,1,0:T(8,128)(2,1)S(1)} collective-permute-done((bf16[2,128,128]{2,1,0:T(8,128)(2,1)S(1)}, bf16[2,128,128]{2,1,0:T(8,128)(2,1)S(1)}, u32[]{:S(2)}, u32[]{:S(2)}) %collective-permute-start.1) | collective-permute-done | bytes 65568 | tf_op jit(solution)/shard_map/ppermute | solution.py:510
  33.6 3.6 %all-to-all-done.moved_ref = bf16[128,40,128]{2,1,0:T(8,128)(2,1)S(1)} async-done(((bf16[128,40,128]{2,1,0:T(8,128)(2,1)}), bf16[128,40,128]{2,1,0:T(8,128)(2,1)S(1)}, u32[]{:S(2)}, u32[]{:S(2)}) %all-to-all-start) | async-done | bytes 1310752 | tf_op jit(solution)/shard_map/all_to_all | solution.py:505
  37.3 12.1 %convs.1 = (bf16[256,32,128]{2,1,0:T(8,128)(2,1)}, bf16[69,32,128]{2,1,0:T(8,128)(2,1)}) custom-call(s32[69]{0:T(128)S(1)} %fusion.1.place_ref, bf16[32,128,256]{2,1,0:T(8,128)(2,1)} %copy-done.2, bf16[2,128,128]{2,1,0:T(8,128)(2,1)S(1)} %collective-permute-done.lat_one_ref, bf16[2,128,128]{2,1,0:T(8,128)(2,1)S(1)} %collective-permute-done.1.lat_two_ref, ...), custom_call_target="tpu_custom_call" | custom-call | flops 6569852928 | bytes 8388608 | tf_op jit(solution)/shard_map/convs/pallas_call | solution.py:255
  (7 shorter events, 0.0 us)
Async XLA Ops:
  4.4 11.6 %copy-start.5 = (bf16[2,32,128]{2,1,0:T(8,128)(2,1)S(1)}, bf16[2,32,128]{2,1,0:T(8,128)(2,1)}, u32[]{:S(2)}) copy-start(bf16[2,32,128]{2,1,0:T(8,128)(2,1)} %get-tuple-element.13.sent_one_ref) | copy-start | bytes 49156
  4.4 13.0 %copy-start.6 = (bf16[2,32,128]{2,1,0:T(8,128)(2,1)S(1)}, bf16[2,32,128]{2,1,0:T(8,128)(2,1)}, u32[]{:S(2)}) copy-start(bf16[2,32,128]{2,1,0:T(8,128)(2,1)} %get-tuple-element.14.sent_two_ref) | copy-start | bytes 49156
  4.4 17.7 %copy-start.10 = (bf16[2,128,128]{2,1,0:T(8,128)(2,1)S(1)}, bf16[2,128,128]{2,1,0:T(8,128)(2,1)}, u32[]{:S(2)}) copy-start(bf16[2,128,128]{2,1,0:T(8,128)(2,1)} %get-tuple-element.11) | copy-start | bytes 196612
  4.4 18.7 %copy-start.9 = (bf16[2,128,128]{2,1,0:T(8,128)(2,1)S(1)}, bf16[2,128,128]{2,1,0:T(8,128)(2,1)}, u32[]{:S(2)}) copy-start(bf16[2,128,128]{2,1,0:T(8,128)(2,1)} %get-tuple-element.12) | copy-start | bytes 196612
  4.5 21.2 %copy-start.11 = (s32[69]{0:T(128)S(1)}, s32[69]{0:T(128)}, u32[]{:S(2)}) copy-start(s32[69]{0:T(128)} %param.9) | copy-start | bytes 832
  4.5 22.3 %copy-start = (bf16[69,32,128]{2,1,0:T(8,128)(2,1)S(1)}, bf16[69,32,128]{2,1,0:T(8,128)(2,1)}, u32[]{:S(2)}) copy-start(bf16[69,32,128]{2,1,0:T(8,128)(2,1)} %x_ref.3) | copy-start | bytes 1695748
  4.5 22.2 %copy-start.1 = (bf16[9,256,256]{2,1,0:T(8,128)(2,1)S(1)}, bf16[9,256,256]{2,1,0:T(8,128)(2,1)}, u32[]{:S(2)}) copy-start(bf16[9,256,256]{2,1,0:T(8,128)(2,1)} %w2_raw_ref.1) | copy-start | bytes 3538948
  4.5 32.8 %all-to-all-start = ((bf16[128,40,128]{2,1,0:T(8,128)(2,1)}), bf16[128,40,128]{2,1,0:T(8,128)(2,1)S(1)}, u32[]{:S(2)}, u32[]{:S(2)}) async-start(bf16[128,40,128]{2,1,0:T(8,128)(2,1)} %bitcast.6), calls=%async_computation | async-start | bytes 2621440 | tf_op jit(solution)/shard_map/all_to_all | solution.py:505
  16.0 15.9 %collective-permute-start.2 = (bf16[2,32,128]{2,1,0:T(8,128)(2,1)S(1)}, bf16[2,32,128]{2,1,0:T(8,128)(2,1)S(1)}, u32[]{:S(2)}, u32[]{:S(2)}) collective-permute-start(bf16[2,32,128]{2,1,0:T(8,128)(2,1)S(1)} %copy-done.5), channel_id=1, source_target_pairs={{0,1},{1,0},{2,3},{3,2},{4,5},{5,4},{6,7},{7,6},{8,9},{9,8},{10,11... | collective-permute-start | bytes 49160 | tf_op jit(solution)/shard_map/ppermute | solution.py:512
  17.4 14.5 %collective-permute-start.3 = (bf16[2,32,128]{2,1,0:T(8,128)(2,1)S(1)}, bf16[2,32,128]{2,1,0:T(8,128)(2,1)S(1)}, u32[]{:S(2)}, u32[]{:S(2)}) collective-permute-start(bf16[2,32,128]{2,1,0:T(8,128)(2,1)S(1)} %copy-done.6), channel_id=1, source_target_pairs={{0,7},{1,2},{2,1},{3,4},{4,3},{5,6},{6,5},{7,0},{8,15},{9,10},{10,... | collective-permute-start | bytes 49160 | tf_op jit(solution)/shard_map/ppermute | solution.py:513
  22.2 9.8 %collective-permute-start = (bf16[2,128,128]{2,1,0:T(8,128)(2,1)S(1)}, bf16[2,128,128]{2,1,0:T(8,128)(2,1)S(1)}, u32[]{:S(2)}, u32[]{:S(2)}) collective-permute-start(bf16[2,128,128]{2,1,0:T(8,128)(2,1)S(1)} %copy-done.10), channel_id=1, source_target_pairs={{0,8},{8,0},{16,24},{24,16},{32,40},{40,32},{48,56},{56,48},{64,72... | collective-permute-start | bytes 196616 | tf_op jit(solution)/shard_map/ppermute | solution.py:509
  23.1 10.5 %collective-permute-start.1 = (bf16[2,128,128]{2,1,0:T(8,128)(2,1)S(1)}, bf16[2,128,128]{2,1,0:T(8,128)(2,1)S(1)}, u32[]{:S(2)}, u32[]{:S(2)}) collective-permute-start(bf16[2,128,128]{2,1,0:T(8,128)(2,1)S(1)} %copy-done.9), channel_id=1, source_target_pairs={{8,16},{16,8},{24,32},{32,24},{40,48},{48,40},{56,64},{64,56},{72,... | collective-permute-start | bytes 196616 | tf_op jit(solution)/shard_map/ppermute | solution.py:510
  25.7 11.6 %copy-start.7 = (f32[256]{0:T(256)S(1)}, f32[256]{0:T(256)}, u32[]{:S(2)}) copy-start(f32[256]{0:T(256)} %param.11) | copy-start | bytes 3076
  25.7 11.6 %copy-start.8 = (f32[256]{0:T(256)S(1)}, f32[256]{0:T(256)}, u32[]{:S(2)}) copy-start(f32[256]{0:T(256)} %param.13) | copy-start | bytes 3076
  28.8 1.3 %copy-start.2 = (bf16[32,128,256]{2,1,0:T(8,128)(2,1)}, bf16[32,128,256]{2,1,0:T(8,128)(2,1)S(1)}, u32[]{:S(2)}) copy-start(bf16[32,128,256]{2,1,0:T(8,128)(2,1)S(1)} %get-tuple-element.10.taps_hbm_ref) | copy-start | bytes 6291460
  30.2 1.0 %copy-start.3 = (bf16[2304,256]{1,0:T(8,128)(2,1)}, bf16[2304,256]{1,0:T(8,128)(2,1)S(1)}, u32[]{:S(2)}) copy-start(bf16[2304,256]{1,0:T(8,128)(2,1)S(1)} %get-tuple-element.16.w2_hbm_ref) | copy-start | bytes 3538948
  31.2 0.7 %copy-start.4 = (bf16[768,256]{1,0:T(8,128)(2,1)}, bf16[768,256]{1,0:T(8,128)(2,1)S(1)}, u32[]{:S(2)}) copy-start(bf16[768,256]{1,0:T(8,128)(2,1)S(1)} %get-tuple-element.15.w1_hbm_ref) | copy-start | bytes 1179652

commit v6 on v5

--- a/solution.py
+++ b/solution.py
@@ -12,6 +12,7 @@
 LON = ("lon_0", "lon_1")
 LANES = 128
 BLOCK = 8
+UNIT = 2
 EXTRA = 8
 X_PART = 24
 SPILL = 13
@@ -137,6 +138,9 @@
         for side in range(2):
             for part in range(3):
                 edge_ref[side, part, rows + 4 : tall, :] = jnp.zeros((tall - rows - 4, LANES), jnp.float32)
+
+    def edges_hidden():
+        tall = edge_ref.shape[2]
         edge_lane = lax.broadcasted_iota(jnp.int32, (tall, LANES), 1)
         hid_row = lax.broadcasted_iota(jnp.int32, (tall - 8, hid), 0)
         hid_outside = jnp.logical_or(
@@ -174,21 +178,23 @@
             done_ref.at[t], out_ref.at[:, t * BLOCK : (t + 1) * BLOCK, :], sem.at[t]
         )
 
-    def features(t):
-        base = t * BLOCK
+    def features(u):
+        base = u * UNIT
         stacked = jnp.concatenate(
             [
-                ref[base + a : base + a + BLOCK].reshape(BLOCK * cols, hid)
+                ref[base + a : base + a + UNIT].reshape(UNIT * cols, hid)
                 for a in range(3)
                 for ref in (west_ref, mid_ref, east_ref)
             ],
             axis=1,
         )
         value = jnp.dot(stacked, w2_ref[...], preferred_element_type=jnp.float32) + b2_ref[...]
-        for i in range(BLOCK):
-            turned_ref[t % 2, pl.ds(i, hid, stride=BLOCK), :] = value[i * cols : (i + 1) * cols].T
-        done_ref[t] = turned_ref[t % 2].reshape(hid, BLOCK, cols).astype(jnp.bfloat16)
-        put(t).start()
+        t, at = base // BLOCK, base % BLOCK
+        for i in range(UNIT):
+            turned_ref[t % 2, pl.ds(at + i, hid, stride=BLOCK), :] = value[i * cols : (i + 1) * cols].T
+        if at + UNIT == BLOCK:
+            done_ref[t] = turned_ref[t % 2].reshape(hid, BLOCK, cols).astype(jnp.bfloat16)
+            put(t).start()
 
     steps = rows // BLOCK
     taken = tile_ref.shape[0]
@@ -200,15 +206,11 @@
 
     load_weights = pltpu.make_async_copy(w2_hbm_ref, w2_ref, load_sem.at[steps])
     load_first = pltpu.make_async_copy(w1_hbm_ref, w1_ref, load_sem.at[steps + 1])
+    load_taps(0).start()
     load_first.start()
-    load_taps(0).start()
     load_weights.start()
     for t in range(1, steps):
         load_taps(t).start()
-
-    @pl.loop(0, taken)
-    def _(c):
-        pltpu.make_async_copy(moved_ref.at[place_ref[c], 0:rows, :], tile_ref.at[c], take_sem).start()
 
     sums = jnp.sum(moved_ref[:, rows : rows + EXTRA, :].astype(jnp.float32), axis=0)
     line = lax.broadcasted_iota(jnp.int32, (1, LANES), 1)
@@ -220,24 +222,31 @@
     scale = jnp.where(line < channels, scale, 0.0)
     mean_low, mean_high = pack(mean, mean, mean, line)
     scale_low, scale_high = pack(scale, scale, scale, line)
-    load_first.wait()
     edges()
     load_taps(0).wait()
-    for r in range(BLOCK + 4):
+    for r in range(UNIT + 4):
         build(r)
-    hidden(0, BLOCK + 2)
+    load_first.wait()
+    edges_hidden()
+    hidden(0, UNIT + 2)
+    for c in range(taken):
+        pltpu.make_async_copy(moved_ref.at[place_ref[c], 0:rows, :], tile_ref.at[c], take_sem).start()
     for t in range(1, steps):
         load_taps(t).wait()
     load_weights.wait()
-    for r in range(BLOCK + 4, 2 * BLOCK + 4):
-        build(r)
-    for t in range(steps):
-        if t + 2 < steps:
-            for r in range((t + 2) * BLOCK + 4, (t + 3) * BLOCK + 4):
+    units = rows // UNIT
+
+    def more(u):
+        if u < units:
+            for r in range(u * UNIT + 4, (u + 1) * UNIT + 4):
                 build(r)
-        if t + 1 < steps:
-            hidden((t + 1) * BLOCK + 2, BLOCK)
-        features(t)
+
+    more(1)
+    for u in range(units):
+        more(u + 2)
+        if u + 1 < units:
+            hidden((u + 1) * UNIT + 2, UNIT)
+        features(u)
     pltpu.make_async_copy(moved_ref.at[0:taken, 0:rows, :], tile_ref, take_sem).wait()
     for t in range(steps):
         put(t).wait()
@@ -286,14 +295,16 @@
 def stage_kernel(x_ref, w1_raw_ref, w2_raw_ref, taps_ref, w1_ref, w2_ref, wide_ref):
     channels, rows, cols = x_ref.shape
     hid = w2_ref.shape[1]
-    padded = wide_ref.shape[0] // rows
-    wide_ref[channels * rows :, :] = jnp.zeros(((padded - channels) * rows, cols), jnp.float32)
-    wide_ref[0 : channels * rows, :] = x_ref[...].astype(jnp.float32).reshape(channels * rows, cols)
+    padded = wide_ref.shape[1] // 8
+    value = x_ref[...].astype(jnp.float32)
+    for q in range(rows // 8):
+        wide_ref[q, channels * 8 :, :] = jnp.zeros(((padded - channels) * 8, cols), jnp.float32)
+        wide_ref[q, 0 : channels * 8, :] = value[:, q * 8 : (q + 1) * 8, :].reshape(channels * 8, cols)
     rest = jnp.zeros((LANES - padded, cols), jnp.float32)
     lane = lax.broadcasted_iota(jnp.int32, (cols, LANES), 1)
     sub = lax.broadcasted_iota(jnp.int32, (8, LANES), 0)
     for r in range(rows):
-        one = wide_ref[pl.ds(r, padded, stride=rows), :]
+        one = wide_ref[r // 8, pl.ds(r % 8, padded, stride=8), :]
         main = jnp.concatenate([one, rest], axis=0).T
         minus, plus = shifted(main, 0.0, 0.0, sub)
         low, high = pack(minus, main, plus, lane)
@@ -323,7 +334,7 @@
         ),
         in_specs=[vmem] * 3,
         out_specs=(vmem,) * 3,
-        scratch_shapes=[pltpu.VMEM((GROUP * rows, cols), jnp.float32)],
+        scratch_shapes=[pltpu.VMEM((rows // 8, GROUP * 8, cols), jnp.float32)],
         compiler_params=pltpu.CompilerParams(vmem_limit_bytes=16 * 2**20),
         cost_estimate=pl.CostEstimate(flops=2**25, bytes_accessed=2**22, transcendentals=0),
         name="stage",
@@ -366,15 +377,17 @@
         load(j).start()
     for j in range(n_lon):
         get(j).start()
-    padded = wide_ref.shape[0] // rows
-    wide_ref[channels * rows :, :] = jnp.zeros(((padded - channels) * rows, cols), jnp.float32)
+    padded = wide_ref.shape[1] // 8
+    for q in range(rows // 8):
+        wide_ref[q, channels * 8 :, :] = jnp.zeros(((padded - channels) * 8, cols), jnp.float32)
     partial_ref[:, channels * 8 :, :] = jnp.zeros((2, (padded - channels) * 8, cols), jnp.float32)
     for j in range(loads):
         load(j).wait()
         low, high = j * X_PART, min((j + 1) * X_PART, channels)
         count = high - low
         value = raw_ref[low:high].astype(jnp.float32)
-        wide_ref[low * rows : high * rows, :] = value.reshape(count * rows, cols)
+        for q in range(rows // 8):
+            wide_ref[q, low * 8 : high * 8, :] = value[:, q * 8 : (q + 1) * 8, :].reshape(count * 8, cols)
         value = value.reshape(count, rows // 8, 8, cols)
         partial_ref[0, low * 8 : high * 8, :] = jnp.sum(value, axis=1).reshape(count * 8, cols)
         partial_ref[1, low * 8 : high * 8, :] = jnp.sum(value * value, axis=1).reshape(count * 8, cols)
@@ -385,8 +398,11 @@
     columns = jnp.zeros((padded, cols), jnp.float32)
     kept = {}
     for r in range(rows):
-        one = wide_ref[pl.ds(r, padded, stride=rows), :]
+        one = wide_ref[r // 8, pl.ds(r % 8, padded, stride=8), :]
         columns = jnp.where(lane // 4 == r, pltpu.roll(one, (2 + 4 * r) % cols, axis=1), columns)
+        if r >= 16 and r % 2 == 1:
+            get(r // 2 - 8).wait()
+            put(r // 2 - 8).start()
         if r in (0, 1, rows - 2, rows - 1):
             kept[r] = jnp.concatenate([one, rest], axis=0).T
     for j in range(2):
@@ -439,9 +455,6 @@
     for j in range(n_lon):
         put_extra(j).start()
     for j in range(n_lon):
-        get(j).wait()
-        put(j).start()
-    for j in range(n_lon):
         put(j).wait()
         put_extra(j).wait()
     for halo in halos:
@@ -464,7 +477,7 @@
         out_specs=(hbm,) * 5,
         scratch_shapes=[
             pltpu.VMEM((channels, rows, cols), jnp.bfloat16),
-            pltpu.VMEM((GROUP * rows, cols), jnp.float32),
+            pltpu.VMEM((rows // 8, GROUP * 8, cols), jnp.float32),
             pltpu.VMEM((cols, LANES), jnp.float32),
             pltpu.VMEM((2, GROUP * 8, cols), jnp.float32),
             pltpu.VMEM((n_lon, height, cols), jnp.bfloat16),

time: 49.7 us -> 48.5 us (0.976)
  Pallas kernels: 17.9 us -> 16.4 us
    pallas_call x1, Pallas kernels: 12.1 us -> 11.1 us  [convs(): pl.pallas_call(functools.partial(conv_kernel, channels, rows, cols, hid),...]
  transfers between devices with their start and end apart: 5 -> 5, of which waited for: 2 -> 2; matrix products, arithmetic and copies ran while one was open for 2% -> 2% of each run, Pallas kernels for 4% -> 3%
where the time goes in v6:
time: 48.5 us; the launch traced here: 48.3 us
  starting transfers between devices  21.1 us (44%)
  Pallas kernels  16.4 us (34%)
  waiting for transfers between devices  5.7 us (12%)
  local copies, waits for them, and re-layouts  4.17 us (9%)
  between operations  0.95 us (2%)
    all_to_all x1, starting transfers between devices, body(): lax.all_to_all(blocks.reshape(n_lon * n_lat, rows + EXTRA, cols), LON + L...  11.5 us
    pallas_call x1, Pallas kernels, convs(): pl.pallas_call(functools.partial(conv_kernel, channels, rows, cols, hid),...  11.1 us
    ppermute x1, starting transfers between devices, body(): lon_two = lax.ppermute(sent_two, LON, far)  4.72 us
    pallas_call x1, Pallas kernels, prepare(): pl.pallas_call(functools.partial(prepare_kernel, channels), out_shape=(la...  3.61 us
    all_to_all x1, waiting for transfers between devices, body(): lax.all_to_all(blocks.reshape(n_lon * n_lat, rows + EXTRA, cols), LON + L...  3.61 us
    unnamed x24, local copies, waits for them, and re-layouts  3.16 us
    ppermute x1, starting transfers between devices, body(): lat_two = lax.ppermute(lat_two, LAT, far)  2.53 us
    ppermute x1, waiting for transfers between devices, body(): lat_two = lax.ppermute(lat_two, LAT, far)  2.08 us
  transfers between devices with their start and end apart: 5, of which 2 were waited for; matrix products, arithmetic and copies ran while one was open for 2% of the time, Pallas kernels for 3%

profile of v6, /device:TPU:1, one launch (start us, length us, event | category | flops | bytes accessed | tf_op | source)
XLA Modules:
  0.0 48.3 jit_solution(5654917968148892473)
XLA Ops:
  0.6 3.6 %prepare.1 = (bf16[2,128,128]{2,1,0:T(8,128)(2,1)}, bf16[2,128,128]{2,1,0:T(8,128)(2,1)}, bf16[2,32,128]{2,1,0:T(8,128)(2,1)}, bf16[2,32,128]{2,1,0:T(8,128)(2,1)}, bf16[8,16,40,128]{3,2,1,0:T(8,128)(2,1)}) custom-call(bf16[69,32,128]{2,1,0:T(8,128)(2,1)} %x_ref.3, bf16[1,512,1024]{2,1,0:T(8,128)(2,1)} %fields_ref.1), custom_call_target="tpu_custom_call" | custom-call | flops 16777216 | bytes 4194304 | tf_op jit(solution)/shard_map/prepare/pallas_call | solution.py:470
  4.3 0.0 copy-start.5
  4.3 0.0 copy-start.6
  4.3 0.0 copy-start.10
  4.3 0.0 copy-start.9
  4.3 0.0 copy-start.11
  4.3 0.0 copy-start
  4.3 0.0 copy-start.1
  4.3 11.5 %all-to-all-start = ((bf16[128,40,128]{2,1,0:T(8,128)(2,1)}), bf16[128,40,128]{2,1,0:T(8,128)(2,1)S(1)}, u32[]{:S(2)}, u32[]{:S(2)}) async-start(bf16[128,40,128]{2,1,0:T(8,128)(2,1)} %bitcast.6), calls=%async_computation | async-start | bytes 2621440 | tf_op jit(solution)/shard_map/all_to_all | solution.py:518
  15.8 0.0 copy-done.5
  15.8 1.4 %collective-permute-start.2 = (bf16[2,32,128]{2,1,0:T(8,128)(2,1)S(1)}, bf16[2,32,128]{2,1,0:T(8,128)(2,1)S(1)}, u32[]{:S(2)}, u32[]{:S(2)}) collective-permute-start(bf16[2,32,128]{2,1,0:T(8,128)(2,1)S(1)} %copy-done.5), channel_id=1, source_target_pairs={{0,1},{1,0},{2,3},{3,2},{4,5},{5,4},{6,7},{7,6},{8,9},{9,8},{10,11... | collective-permute-start | bytes 49160 | tf_op jit(solution)/shard_map/ppermute | solution.py:525
  17.3 0.0 copy-done.6
  17.3 4.7 %collective-permute-start.3 = (bf16[2,32,128]{2,1,0:T(8,128)(2,1)S(1)}, bf16[2,32,128]{2,1,0:T(8,128)(2,1)S(1)}, u32[]{:S(2)}, u32[]{:S(2)}) collective-permute-start(bf16[2,32,128]{2,1,0:T(8,128)(2,1)S(1)} %copy-done.6), channel_id=1, source_target_pairs={{0,7},{1,2},{2,1},{3,4},{4,3},{5,6},{6,5},{7,0},{8,15},{9,10},{10,... | collective-permute-start | bytes 49160 | tf_op jit(solution)/shard_map/ppermute | solution.py:526
  22.0 0.0 copy-done.10
  22.0 0.9 %collective-permute-start = (bf16[2,128,128]{2,1,0:T(8,128)(2,1)S(1)}, bf16[2,128,128]{2,1,0:T(8,128)(2,1)S(1)}, u32[]{:S(2)}, u32[]{:S(2)}) collective-permute-start(bf16[2,128,128]{2,1,0:T(8,128)(2,1)S(1)} %copy-done.10), channel_id=1, source_target_pairs={{0,8},{8,0},{16,24},{24,16},{32,40},{40,32},{48,56},{56,48},{64,72... | collective-permute-start | bytes 196616 | tf_op jit(solution)/shard_map/ppermute | solution.py:522
  22.9 0.0 copy-done.9
  23.0 2.5 %collective-permute-start.1 = (bf16[2,128,128]{2,1,0:T(8,128)(2,1)S(1)}, bf16[2,128,128]{2,1,0:T(8,128)(2,1)S(1)}, u32[]{:S(2)}, u32[]{:S(2)}) collective-permute-start(bf16[2,128,128]{2,1,0:T(8,128)(2,1)S(1)} %copy-done.9), channel_id=1, source_target_pairs={{8,16},{16,8},{24,32},{32,24},{40,48},{48,40},{56,64},{64,56},{72,... | collective-permute-start | bytes 196616 | tf_op jit(solution)/shard_map/ppermute | solution.py:523
  25.5 0.0 copy-done.11
  25.5 0.0 copy-start.7
  25.5 0.0 copy-start.8
  25.5 1.0 %pad.4.w1_raw_ref = bf16[9,72,256]{2,1,0:T(8,128)(2,1)S(1)} pad(bf16[9,69,256]{2,1,0:T(8,128)(2,1)} %bitcast.7, bf16[]{:T(256)} %constant.32.clone.1), padding=0_0x0_3x0_0 | pad | bytes 649730 | tf_op jit(solution)/shard_map/jit(_pad)/pad | solution.py:527
  26.6 1.7 %stage.1 = (bf16[32,128,256]{2,1,0:T(8,128)(2,1)S(1)}, bf16[768,256]{1,0:T(8,128)(2,1)S(1)}, bf16[2304,256]{1,0:T(8,128)(2,1)S(1)}) custom-call(bf16[69,32,128]{2,1,0:T(8,128)(2,1)S(1)} %copy-done, bf16[9,72,256]{2,1,0:T(8,128)(2,1)S(1)} %pad.4.w1_raw_ref, bf16[9,256,256]{2,1,0:T(8,128)(2,1)S(1)} %copy-done.1), custom_call_target="tpu_custom_call" | custom-call | flops 33554432 | bytes 4194304 | tf_op jit(solution)/shard_map/stage/pallas_call | solution.py:328
  28.3 1.3 %copy-done.2 = bf16[32,128,256]{2,1,0:T(8,128)(2,1)} copy-done((bf16[32,128,256]{2,1,0:T(8,128)(2,1)}, bf16[32,128,256]{2,1,0:T(8,128)(2,1)S(1)}, u32[]{:S(2)}) %copy-start.2) | copy-done | bytes 2097176
  29.6 1.0 %copy-done.3 = bf16[2304,256]{1,0:T(8,128)(2,1)} copy-done((bf16[2304,256]{1,0:T(8,128)(2,1)}, bf16[2304,256]{1,0:T(8,128)(2,1)S(1)}, u32[]{:S(2)}) %copy-start.3) | copy-done | bytes 1179672
  30.6 0.7 %copy-done.4 = bf16[768,256]{1,0:T(8,128)(2,1)} copy-done((bf16[768,256]{1,0:T(8,128)(2,1)}, bf16[768,256]{1,0:T(8,128)(2,1)S(1)}, u32[]{:S(2)}) %copy-start.4) | copy-done | bytes 393240
  31.4 0.0 collective-permute-done.2.lon_one_ref
  31.4 0.0 collective-permute-done.3.lon_two_ref
  31.4 0.0 collective-permute-done.lat_one_ref
  31.4 2.1 %collective-permute-done.1.lat_two_ref = bf16[2,128,128]{2,1,0:T(8,128)(2,1)S(1)} collective-permute-done((bf16[2,128,128]{2,1,0:T(8,128)(2,1)S(1)}, bf16[2,128,128]{2,1,0:T(8,128)(2,1)S(1)}, u32[]{:S(2)}, u32[]{:S(2)}) %collective-permute-start.1) | collective-permute-done | bytes 65568 | tf_op jit(solution)/shard_map/ppermute | solution.py:523
  33.5 3.6 %all-to-all-done.moved_ref = bf16[128,40,128]{2,1,0:T(8,128)(2,1)S(1)} async-done(((bf16[128,40,128]{2,1,0:T(8,128)(2,1)}), bf16[128,40,128]{2,1,0:T(8,128)(2,1)S(1)}, u32[]{:S(2)}, u32[]{:S(2)}) %all-to-all-start) | async-done | bytes 1310752 | tf_op jit(solution)/shard_map/all_to_all | solution.py:518
  37.1 0.0 copy-done.7
  37.1 11.1 %convs.1 = (bf16[256,32,128]{2,1,0:T(8,128)(2,1)}, bf16[69,32,128]{2,1,0:T(8,128)(2,1)}) custom-call(s32[69]{0:T(128)S(1)} %fusion.1.place_ref, bf16[32,128,256]{2,1,0:T(8,128)(2,1)} %copy-done.2, bf16[2,128,128]{2,1,0:T(8,128)(2,1)S(1)} %collective-permute-done.lat_one_ref, bf16[2,128,128]{2,1,0:T(8,128)(2,1)S(1)} %collective-permute-done.1.lat_two_ref, ...), custom_call_target="tpu_custom_call" | custom-call | flops 6569852928 | bytes 8388608 | tf_op jit(solution)/shard_map/convs/pallas_call | solution.py:264
  (7 shorter events, 0.0 us)
Async XLA Ops:
  4.3 11.6 %copy-start.5 = (bf16[2,32,128]{2,1,0:T(8,128)(2,1)S(1)}, bf16[2,32,128]{2,1,0:T(8,128)(2,1)}, u32[]{:S(2)}) copy-start(bf16[2,32,128]{2,1,0:T(8,128)(2,1)} %get-tuple-element.13.sent_one_ref) | copy-start | bytes 49156
  4.3 13.0 %copy-start.6 = (bf16[2,32,128]{2,1,0:T(8,128)(2,1)S(1)}, bf16[2,32,128]{2,1,0:T(8,128)(2,1)}, u32[]{:S(2)}) copy-start(bf16[2,32,128]{2,1,0:T(8,128)(2,1)} %get-tuple-element.14.sent_two_ref) | copy-start | bytes 49156
  4.3 17.7 %copy-start.10 = (bf16[2,128,128]{2,1,0:T(8,128)(2,1)S(1)}, bf16[2,128,128]{2,1,0:T(8,128)(2,1)}, u32[]{:S(2)}) copy-start(bf16[2,128,128]{2,1,0:T(8,128)(2,1)} %get-tuple-element.11) | copy-start | bytes 196612
  4.3 18.7 %copy-start.9 = (bf16[2,128,128]{2,1,0:T(8,128)(2,1)S(1)}, bf16[2,128,128]{2,1,0:T(8,128)(2,1)}, u32[]{:S(2)}) copy-start(bf16[2,128,128]{2,1,0:T(8,128)(2,1)} %get-tuple-element.12) | copy-start | bytes 196612
  4.3 21.2 %copy-start.11 = (s32[69]{0:T(128)S(1)}, s32[69]{0:T(128)}, u32[]{:S(2)}) copy-start(s32[69]{0:T(128)} %param.9) | copy-start | bytes 832
  4.3 22.3 %copy-start = (bf16[69,32,128]{2,1,0:T(8,128)(2,1)S(1)}, bf16[69,32,128]{2,1,0:T(8,128)(2,1)}, u32[]{:S(2)}) copy-start(bf16[69,32,128]{2,1,0:T(8,128)(2,1)} %x_ref.3) | copy-start | bytes 1695748
  4.3 22.2 %copy-start.1 = (bf16[9,256,256]{2,1,0:T(8,128)(2,1)S(1)}, bf16[9,256,256]{2,1,0:T(8,128)(2,1)}, u32[]{:S(2)}) copy-start(bf16[9,256,256]{2,1,0:T(8,128)(2,1)} %w2_raw_ref.1) | copy-start | bytes 3538948
  4.3 32.8 %all-to-all-start = ((bf16[128,40,128]{2,1,0:T(8,128)(2,1)}), bf16[128,40,128]{2,1,0:T(8,128)(2,1)S(1)}, u32[]{:S(2)}, u32[]{:S(2)}) async-start(bf16[128,40,128]{2,1,0:T(8,128)(2,1)} %bitcast.6), calls=%async_computation | async-start | bytes 2621440 | tf_op jit(solution)/shard_map/all_to_all | solution.py:518
  15.8 15.6 %collective-permute-start.2 = (bf16[2,32,128]{2,1,0:T(8,128)(2,1)S(1)}, bf16[2,32,128]{2,1,0:T(8,128)(2,1)S(1)}, u32[]{:S(2)}, u32[]{:S(2)}) collective-permute-start(bf16[2,32,128]{2,1,0:T(8,128)(2,1)S(1)} %copy-done.5), channel_id=1, source_target_pairs={{0,1},{1,0},{2,3},{3,2},{4,5},{5,4},{6,7},{7,6},{8,9},{9,8},{10,11... | collective-permute-start | bytes 49160 | tf_op jit(solution)/shard_map/ppermute | solution.py:525
  17.3 14.1 %collective-permute-start.3 = (bf16[2,32,128]{2,1,0:T(8,128)(2,1)S(1)}, bf16[2,32,128]{2,1,0:T(8,128)(2,1)S(1)}, u32[]{:S(2)}, u32[]{:S(2)}) collective-permute-start(bf16[2,32,128]{2,1,0:T(8,128)(2,1)S(1)} %copy-done.6), channel_id=1, source_target_pairs={{0,7},{1,2},{2,1},{3,4},{4,3},{5,6},{6,5},{7,0},{8,15},{9,10},{10,... | collective-permute-start | bytes 49160 | tf_op jit(solution)/shard_map/ppermute | solution.py:526
  22.0 9.4 %collective-permute-start = (bf16[2,128,128]{2,1,0:T(8,128)(2,1)S(1)}, bf16[2,128,128]{2,1,0:T(8,128)(2,1)S(1)}, u32[]{:S(2)}, u32[]{:S(2)}) collective-permute-start(bf16[2,128,128]{2,1,0:T(8,128)(2,1)S(1)} %copy-done.10), channel_id=1, source_target_pairs={{0,8},{8,0},{16,24},{24,16},{32,40},{40,32},{48,56},{56,48},{64,72... | collective-permute-start | bytes 196616 | tf_op jit(solution)/shard_map/ppermute | solution.py:522
  23.0 10.5 %collective-permute-start.1 = (bf16[2,128,128]{2,1,0:T(8,128)(2,1)S(1)}, bf16[2,128,128]{2,1,0:T(8,128)(2,1)S(1)}, u32[]{:S(2)}, u32[]{:S(2)}) collective-permute-start(bf16[2,128,128]{2,1,0:T(8,128)(2,1)S(1)} %copy-done.9), channel_id=1, source_target_pairs={{8,16},{16,8},{24,32},{32,24},{40,48},{48,40},{56,64},{64,56},{72,... | collective-permute-start | bytes 196616 | tf_op jit(solution)/shard_map/ppermute | solution.py:523
  25.5 11.6 %copy-start.7 = (f32[256]{0:T(256)S(1)}, f32[256]{0:T(256)}, u32[]{:S(2)}) copy-start(f32[256]{0:T(256)} %param.11) | copy-start | bytes 3076
  25.5 11.6 %copy-start.8 = (f32[256]{0:T(256)S(1)}, f32[256]{0:T(256)}, u32[]{:S(2)}) copy-start(f32[256]{0:T(256)} %param.13) | copy-start | bytes 3076
  28.3 1.3 %copy-start.2 = (bf16[32,128,256]{2,1,0:T(8,128)(2,1)}, bf16[32,128,256]{2,1,0:T(8,128)(2,1)S(1)}, u32[]{:S(2)}) copy-start(bf16[32,128,256]{2,1,0:T(8,128)(2,1)S(1)} %get-tuple-element.10.taps_hbm_ref) | copy-start | bytes 6291460
  29.6 1.0 %copy-start.3 = (bf16[2304,256]{1,0:T(8,128)(2,1)}, bf16[2304,256]{1,0:T(8,128)(2,1)S(1)}, u32[]{:S(2)}) copy-start(bf16[2304,256]{1,0:T(8,128)(2,1)S(1)} %get-tuple-element.16.w2_hbm_ref) | copy-start | bytes 3538948
  30.6 0.7 %copy-start.4 = (bf16[768,256]{1,0:T(8,128)(2,1)}, bf16[768,256]{1,0:T(8,128)(2,1)S(1)}, u32[]{:S(2)}) copy-start(bf16[768,256]{1,0:T(8,128)(2,1)S(1)} %get-tuple-element.15.w1_hbm_ref) | copy-start | bytes 1179652

commit v7 on v6

--- a/solution.py
+++ b/solution.py
@@ -17,7 +17,7 @@
 X_PART = 24
 SPILL = 13
 GROUP = 72
-PREPARE_VMEM = 60 * 2**20
+PREPARE_VMEM = 16 * 2**20
 CONVS_VMEM = 40 * 2**20
 GELU_C = 0.7978845608028654
 
@@ -344,8 +344,8 @@
 def prepare_kernel(
     channels, x_ref, fields_ref,
     lat_one_ref, lat_two_ref, lon_one_ref, lon_two_ref, blocks_ref,
-    raw_ref, wide_ref, gather_ref, partial_ref, held_ref, extra_ref, lat_ref, lon_ref, first_ref, last_ref,
-    x_sem, in_sem, out_sem, extra_sem, halo_sem,
+    raw_ref, wide_ref, gather_ref, partial_ref, held_ref, extra_ref, first_ref, last_ref,
+    x_sem, in_sem, out_sem, extra_sem,
 ):
     rows, cols = raw_ref.shape[1], raw_ref.shape[2]
     n_lon, n_lat = blocks_ref.shape[0], blocks_ref.shape[1]
@@ -366,12 +366,6 @@
     def put_extra(j):
         return pltpu.make_async_copy(extra_ref.at[j], blocks_ref.at[j, :, rows : rows + EXTRA, :], extra_sem.at[j])
 
-    halos = [
-        pltpu.make_async_copy(lat_ref.at[0], lat_one_ref, halo_sem.at[0]),
-        pltpu.make_async_copy(lat_ref.at[1], lat_two_ref, halo_sem.at[1]),
-        pltpu.make_async_copy(lon_ref.at[0], lon_one_ref, halo_sem.at[2]),
-        pltpu.make_async_copy(lon_ref.at[1], lon_two_ref, halo_sem.at[3]),
-    ]
     loads = (channels + X_PART - 1) // X_PART
     for j in range(loads):
         load(j).start()
@@ -394,32 +388,9 @@
     rest = jnp.zeros((LANES - padded, cols), jnp.float32)
     odd_lat = lat % 2 == 1
     odd_lon = lon % 2 == 1
-    lane = lax.broadcasted_iota(jnp.int32, (padded, cols), 1)
-    columns = jnp.zeros((padded, cols), jnp.float32)
-    kept = {}
-    for r in range(rows):
-        one = wide_ref[r // 8, pl.ds(r % 8, padded, stride=8), :]
-        columns = jnp.where(lane // 4 == r, pltpu.roll(one, (2 + 4 * r) % cols, axis=1), columns)
-        if r >= 16 and r % 2 == 1:
-            get(r // 2 - 8).wait()
-            put(r // 2 - 8).start()
-        if r in (0, 1, rows - 2, rows - 1):
-            kept[r] = jnp.concatenate([one, rest], axis=0).T
-    for j in range(2):
-        low, high = kept[j], kept[rows - 2 + j]
-        lat_ref[0, j] = jnp.where(odd_lat, low, high).astype(jnp.bfloat16)
-        lat_ref[1, j] = jnp.where(odd_lat, high, low).astype(jnp.bfloat16)
-    halos[0].start()
-    halos[1].start()
-    gather_ref[...] = jnp.concatenate([columns, rest], axis=0).T
-    for j in range(2):
-        last_ref[j] = gather_ref[pl.ds(j, rows, stride=4), :]
-        first_ref[j] = gather_ref[pl.ds(2 + j, rows, stride=4), :]
-    low, high = first_ref[...], last_ref[...]
-    lon_ref[0] = jnp.where(odd_lon, low, high).astype(jnp.bfloat16)
-    lon_ref[1] = jnp.where(odd_lon, high, low).astype(jnp.bfloat16)
-    halos[2].start()
-    halos[3].start()
+
+    def row(r):
+        return wide_ref[r // 8, pl.ds(r % 8, padded, stride=8), :]
 
     def parts(which):
         value = partial_ref[which, pl.ds(0, padded, stride=8), :]
@@ -431,14 +402,20 @@
         middle = value.astype(jnp.bfloat16).astype(jnp.float32)
         return [high, middle, value - middle]
 
+    kept = {r: jnp.concatenate([row(r), rest], axis=0).T for r in (0, 1, rows - 2, rows - 1)}
+    for j in range(2):
+        low, high = kept[j], kept[rows - 2 + j]
+        lat_one_ref[j] = jnp.where(odd_lat, low, high).astype(jnp.bfloat16)
+        lat_two_ref[j] = jnp.where(odd_lat, high, low).astype(jnp.bfloat16)
+
     sums = parts(0) + parts(1)
     line = lax.broadcasted_iota(jnp.int32, (1, LANES), 1)
 
     def extra(down, right):
-        cols_ref = last_ref if right > 0 else first_ref
-        row = rows - 2 if down > 0 else 0
-        near = [cols_ref[j, row : row + 1, :] for j in range(2)]
-        far = [cols_ref[j, row + 1 : row + 2, :] for j in range(2)]
+        col = cols - 2 if right > 0 else 0
+        top = rows - 2 if down > 0 else 0
+        near = [kept[top][col + j : col + j + 1] for j in range(2)]
+        far = [kept[top + 1][col + j : col + j + 1] for j in range(2)]
         spill = [
             jnp.where(
                 jnp.logical_and(line >= SPILL + LANES - channels, line < SPILL + channels),
@@ -454,15 +431,28 @@
         extra_ref[(lon + n_lon + right) % n_lon, (lat + n_lat + down) % n_lat] = extra(down, right)
     for j in range(n_lon):
         put_extra(j).start()
+    lane = lax.broadcasted_iota(jnp.int32, (padded, cols), 1)
+    columns = jnp.zeros((padded, cols), jnp.float32)
+    for r in range(rows):
+        columns = jnp.where(lane // 4 == r, pltpu.roll(row(r), (2 + 4 * r) % cols, axis=1), columns)
+        if r % 4 == 3:
+            get(r // 4).wait()
+            put(r // 4).start()
+    gather_ref[...] = jnp.concatenate([columns, rest], axis=0).T
+    for j in range(2):
+        last_ref[j] = gather_ref[pl.ds(j, rows, stride=4), :]
+        first_ref[j] = gather_ref[pl.ds(2 + j, rows, stride=4), :]
+    low, high = first_ref[...], last_ref[...]
+    lon_one_ref[...] = jnp.where(odd_lon, low, high).astype(jnp.bfloat16)
+    lon_two_ref[...] = jnp.where(odd_lon, high, low).astype(jnp.bfloat16)
     for j in range(n_lon):
         put(j).wait()
         put_extra(j).wait()
-    for halo in halos:
-        halo.wait()
 
 
 def prepare(current, next_fields, n_lon):
     channels, rows, cols = current.shape
+    vmem = pl.BlockSpec(memory_space=pltpu.VMEM)
     hbm = pl.BlockSpec(memory_space=pl.ANY)
     height = next_fields.shape[1]
     lat_row = jax.ShapeDtypeStruct((2, cols, LANES), jnp.bfloat16)
@@ -474,7 +464,7 @@
             jax.ShapeDtypeStruct((n_lon, height // rows, rows + EXTRA, cols), jnp.bfloat16),
         ),
         in_specs=[hbm, hbm],
-        out_specs=(hbm,) * 5,
+        out_specs=(vmem,) * 4 + (hbm,),
         scratch_shapes=[
             pltpu.VMEM((channels, rows, cols), jnp.bfloat16),
             pltpu.VMEM((rows // 8, GROUP * 8, cols), jnp.float32),
@@ -482,15 +472,12 @@
             pltpu.VMEM((2, GROUP * 8, cols), jnp.float32),
             pltpu.VMEM((n_lon, height, cols), jnp.bfloat16),
             pltpu.VMEM((n_lon, height // rows, EXTRA, cols), jnp.bfloat16),
-            pltpu.VMEM((2, 2, cols, LANES), jnp.bfloat16),
-            pltpu.VMEM((2, 2, rows, LANES), jnp.bfloat16),
             pltpu.VMEM((2, rows, LANES), jnp.float32),
             pltpu.VMEM((2, rows, LANES), jnp.float32),
             pltpu.SemaphoreType.DMA(((channels + X_PART - 1) // X_PART,)),
             pltpu.SemaphoreType.DMA((n_lon,)),
             pltpu.SemaphoreType.DMA((n_lon,)),
             pltpu.SemaphoreType.DMA((n_lon,)),
-            pltpu.SemaphoreType.DMA((4,)),
         ],
         compiler_params=pltpu.CompilerParams(vmem_limit_bytes=PREPARE_VMEM),
         cost_estimate=pl.CostEstimate(flops=2**24, bytes_accessed=2**22, transcendentals=0),
@@ -514,7 +501,7 @@
     channels, rows, cols = current.shape
     n_lat = lax.axis_size(LAT)
     n_lon = lax.axis_size(LON)
-    lat_one, lat_two, sent_one, sent_two, blocks = prepare(current, next_fields, n_lon)
+    lat_one, lat_two, sent_one, sent_two, blocks = prepare(in_hbm(current), in_hbm(next_fields), n_lon)
     moved = lax.all_to_all(
         blocks.reshape(n_lon * n_lat, rows + EXTRA, cols), LON + LAT, split_axis=0, concat_axis=0, tiled=True
     )

time: 48.5 us -> 48.3 us (level)
    unnamed x24 -> x16, local copies, waits for them, and re-layouts: 3.16 us -> 3.11 us
  transfers between devices with their start and end apart: 5 -> 5, of which waited for: 2 -> 2; matrix products, arithmetic and copies ran while one was open for 2% -> 2% of each run, Pallas kernels for 3% -> 4%
where the time goes in v7:
time: 48.3 us; the launch traced here: 48.1 us
  starting transfers between devices  21.1 us (44%)
  Pallas kernels  16.2 us (34%)
  waiting for transfers between devices  5.76 us (12%)
  local copies, waits for them, and re-layouts  4.12 us (9%)
  between operations  0.91 us (2%)
    all_to_all x1, starting transfers between devices, body(): lax.all_to_all(blocks.reshape(n_lon * n_lat, rows + EXTRA, cols), LON + L...  11.5 us
    pallas_call x1, Pallas kernels, convs(): pl.pallas_call(functools.partial(conv_kernel, channels, rows, cols, hid),...  11.1 us
    ppermute x1, starting transfers between devices, body(): lon_two = lax.ppermute(sent_two, LON, far)  4.72 us
    all_to_all x1, waiting for transfers between devices, body(): lax.all_to_all(blocks.reshape(n_lon * n_lat, rows + EXTRA, cols), LON + L...  3.61 us
    pallas_call x1, Pallas kernels, prepare(): pl.pallas_call(functools.partial(prepare_kernel, channels), out_shape=(la...  3.41 us
    unnamed x16, local copies, waits for them, and re-layouts  3.11 us
    ppermute x1, starting transfers between devices, body(): lat_two = lax.ppermute(lat_two, LAT, far)  2.52 us
    ppermute x1, waiting for transfers between devices, body(): lat_two = lax.ppermute(lat_two, LAT, far)  2.15 us
  transfers between devices with their start and end apart: 5, of which 2 were waited for; matrix products, arithmetic and copies ran while one was open for 2% of the time, Pallas kernels for 4%

profile of v7, /device:TPU:1, one launch (start us, length us, event | category | flops | bytes accessed | tf_op | source)
XLA Modules:
  0.0 48.1 jit_solution(3895874498867649167)
XLA Ops:
  0.6 3.4 %prepare.1 = (bf16[2,128,128]{2,1,0:T(8,128)(2,1)S(1)}, bf16[2,128,128]{2,1,0:T(8,128)(2,1)S(1)}, bf16[2,32,128]{2,1,0:T(8,128)(2,1)S(1)}, bf16[2,32,128]{2,1,0:T(8,128)(2,1)S(1)}, bf16[8,16,40,128]{3,2,1,0:T(8,128)(2,1)}) custom-call(bf16[69,32,128]{2,1,0:T(8,128)(2,1)} %x_ref.3, bf16[1,512,1024]{2,1,0:T(8,128)(2,1)} %fields_ref.1), custom_call_target="tpu_custom_call" | custom-call | flops 16777216 | bytes 4194304 | tf_op jit(solution)/shard_map/prepare/pallas_call | solution.py:460
  4.1 0.0 copy-start.7
  4.1 0.0 copy-start
  4.1 0.0 copy-start.1
  4.1 11.5 %all-to-all-start = ((bf16[128,40,128]{2,1,0:T(8,128)(2,1)}), bf16[128,40,128]{2,1,0:T(8,128)(2,1)S(1)}, u32[]{:S(2)}, u32[]{:S(2)}) async-start(bf16[128,40,128]{2,1,0:T(8,128)(2,1)} %bitcast.3), calls=%async_computation | async-start | bytes 2621440 | tf_op jit(solution)/shard_map/all_to_all | solution.py:505
  15.6 1.4 %collective-permute-start.2 = (bf16[2,32,128]{2,1,0:T(8,128)(2,1)S(1)}, bf16[2,32,128]{2,1,0:T(8,128)(2,1)S(1)}, u32[]{:S(2)}, u32[]{:S(2)}) collective-permute-start(bf16[2,32,128]{2,1,0:T(8,128)(2,1)S(1)} %get-tuple-element.13.sent_one_ref), channel_id=1, source_target_pairs={{0,1},{1,0},{2,3},{3,2},{4,5},{5,4},{6,7},{7,6},{8,9},{9,8},{10,11... | collective-permute-start | bytes 49160 | tf_op jit(solution)/shard_map/ppermute | solution.py:512
  17.0 4.7 %collective-permute-start.3 = (bf16[2,32,128]{2,1,0:T(8,128)(2,1)S(1)}, bf16[2,32,128]{2,1,0:T(8,128)(2,1)S(1)}, u32[]{:S(2)}, u32[]{:S(2)}) collective-permute-start(bf16[2,32,128]{2,1,0:T(8,128)(2,1)S(1)} %get-tuple-element.14.sent_two_ref), channel_id=1, source_target_pairs={{0,7},{1,2},{2,1},{3,4},{4,3},{5,6},{6,5},{7,0},{8,15},{9,10},{10,... | collective-permute-start | bytes 49160 | tf_op jit(solution)/shard_map/ppermute | solution.py:513
  21.7 0.9 %collective-permute-start = (bf16[2,128,128]{2,1,0:T(8,128)(2,1)S(1)}, bf16[2,128,128]{2,1,0:T(8,128)(2,1)S(1)}, u32[]{:S(2)}, u32[]{:S(2)}) collective-permute-start(bf16[2,128,128]{2,1,0:T(8,128)(2,1)S(1)} %get-tuple-element.11), channel_id=1, source_target_pairs={{0,8},{8,0},{16,24},{24,16},{32,40},{40,32},{48,56},{56,48},{64,72... | collective-permute-start | bytes 196616 | tf_op jit(solution)/shard_map/ppermute | solution.py:509
  22.7 2.5 %collective-permute-start.1 = (bf16[2,128,128]{2,1,0:T(8,128)(2,1)S(1)}, bf16[2,128,128]{2,1,0:T(8,128)(2,1)S(1)}, u32[]{:S(2)}, u32[]{:S(2)}) collective-permute-start(bf16[2,128,128]{2,1,0:T(8,128)(2,1)S(1)} %get-tuple-element.12), channel_id=1, source_target_pairs={{8,16},{16,8},{24,32},{32,24},{40,48},{48,40},{56,64},{64,56},{72,... | collective-permute-start | bytes 196616 | tf_op jit(solution)/shard_map/ppermute | solution.py:510
  25.2 0.0 copy-done.7
  25.2 0.0 copy-start.5
  25.3 0.0 copy-start.6
  25.3 1.0 %pad.4.w1_raw_ref = bf16[9,72,256]{2,1,0:T(8,128)(2,1)S(1)} pad(bf16[9,69,256]{2,1,0:T(8,128)(2,1)} %bitcast.6, bf16[]{:T(256)} %constant.32.clone.1), padding=0_0x0_3x0_0 | pad | bytes 649730 | tf_op jit(solution)/shard_map/jit(_pad)/pad | solution.py:514
  26.3 0.0 copy-done
  26.3 0.0 copy-done.1
  26.3 1.7 %stage.1 = (bf16[32,128,256]{2,1,0:T(8,128)(2,1)S(1)}, bf16[768,256]{1,0:T(8,128)(2,1)S(1)}, bf16[2304,256]{1,0:T(8,128)(2,1)S(1)}) custom-call(bf16[69,32,128]{2,1,0:T(8,128)(2,1)S(1)} %copy-done, bf16[9,72,256]{2,1,0:T(8,128)(2,1)S(1)} %pad.4.w1_raw_ref, bf16[9,256,256]{2,1,0:T(8,128)(2,1)S(1)} %copy-done.1), custom_call_target="tpu_custom_call" | custom-call | flops 33554432 | bytes 4194304 | tf_op jit(solution)/shard_map/stage/pallas_call | solution.py:328
  28.0 0.0 copy-start.2
  28.0 1.3 %copy-done.2 = bf16[32,128,256]{2,1,0:T(8,128)(2,1)} copy-done((bf16[32,128,256]{2,1,0:T(8,128)(2,1)}, bf16[32,128,256]{2,1,0:T(8,128)(2,1)S(1)}, u32[]{:S(2)}) %copy-start.2) | copy-done | bytes 2097176
  29.3 0.0 copy-start.3
  29.3 1.0 %copy-done.3 = bf16[2304,256]{1,0:T(8,128)(2,1)} copy-done((bf16[2304,256]{1,0:T(8,128)(2,1)}, bf16[2304,256]{1,0:T(8,128)(2,1)S(1)}, u32[]{:S(2)}) %copy-start.3) | copy-done | bytes 1179672
  30.3 0.0 copy-start.4
  30.3 0.7 %copy-done.4 = bf16[768,256]{1,0:T(8,128)(2,1)} copy-done((bf16[768,256]{1,0:T(8,128)(2,1)}, bf16[768,256]{1,0:T(8,128)(2,1)S(1)}, u32[]{:S(2)}) %copy-start.4) | copy-done | bytes 393240
  31.1 0.0 collective-permute-done.2.lon_one_ref
  31.1 0.0 collective-permute-done.3.lon_two_ref
  31.1 0.0 collective-permute-done.lat_one_ref
  31.1 2.1 %collective-permute-done.1.lat_two_ref = bf16[2,128,128]{2,1,0:T(8,128)(2,1)S(1)} collective-permute-done((bf16[2,128,128]{2,1,0:T(8,128)(2,1)S(1)}, bf16[2,128,128]{2,1,0:T(8,128)(2,1)S(1)}, u32[]{:S(2)}, u32[]{:S(2)}) %collective-permute-start.1) | collective-permute-done | bytes 65568 | tf_op jit(solution)/shard_map/ppermute | solution.py:510
  33.2 3.6 %all-to-all-done.moved_ref = bf16[128,40,128]{2,1,0:T(8,128)(2,1)S(1)} async-done(((bf16[128,40,128]{2,1,0:T(8,128)(2,1)}), bf16[128,40,128]{2,1,0:T(8,128)(2,1)S(1)}, u32[]{:S(2)}, u32[]{:S(2)}) %all-to-all-start) | async-done | bytes 1310752 | tf_op jit(solution)/shard_map/all_to_all | solution.py:505
  36.9 0.0 copy-done.5
  36.9 0.0 copy-done.6
  36.9 11.1 %convs.1 = (bf16[256,32,128]{2,1,0:T(8,128)(2,1)}, bf16[69,32,128]{2,1,0:T(8,128)(2,1)}) custom-call(s32[69]{0:T(128)S(1)} %fusion.1.place_ref, bf16[32,128,256]{2,1,0:T(8,128)(2,1)} %copy-done.2, bf16[2,128,128]{2,1,0:T(8,128)(2,1)S(1)} %collective-permute-done.lat_one_ref, bf16[2,128,128]{2,1,0:T(8,128)(2,1)S(1)} %collective-permute-done.1.lat_two_ref, ...), custom_call_target="tpu_custom_call" | custom-call | flops 6569852928 | bytes 8388608 | tf_op jit(solution)/shard_map/convs/pallas_call | solution.py:264
  (1 shorter events, 0.0 us)
Async XLA Ops:
  4.1 21.2 %copy-start.7 = (s32[69]{0:T(128)S(1)}, s32[69]{0:T(128)}, u32[]{:S(2)}) copy-start(s32[69]{0:T(128)} %param.9) | copy-start | bytes 832
  4.1 22.2 %copy-start = (bf16[69,32,128]{2,1,0:T(8,128)(2,1)S(1)}, bf16[69,32,128]{2,1,0:T(8,128)(2,1)}, u32[]{:S(2)}) copy-start(bf16[69,32,128]{2,1,0:T(8,128)(2,1)} %x_ref.3) | copy-start | bytes 1695748
  4.1 22.2 %copy-start.1 = (bf16[9,256,256]{2,1,0:T(8,128)(2,1)S(1)}, bf16[9,256,256]{2,1,0:T(8,128)(2,1)}, u32[]{:S(2)}) copy-start(bf16[9,256,256]{2,1,0:T(8,128)(2,1)} %w2_raw_ref.1) | copy-start | bytes 3538948
  4.1 32.8 %all-to-all-start = ((bf16[128,40,128]{2,1,0:T(8,128)(2,1)}), bf16[128,40,128]{2,1,0:T(8,128)(2,1)S(1)}, u32[]{:S(2)}, u32[]{:S(2)}) async-start(bf16[128,40,128]{2,1,0:T(8,128)(2,1)} %bitcast.3), calls=%async_computation | async-start | bytes 2621440 | tf_op jit(solution)/shard_map/all_to_all | solution.py:505
  15.6 15.5 %collective-permute-start.2 = (bf16[2,32,128]{2,1,0:T(8,128)(2,1)S(1)}, bf16[2,32,128]{2,1,0:T(8,128)(2,1)S(1)}, u32[]{:S(2)}, u32[]{:S(2)}) collective-permute-start(bf16[2,32,128]{2,1,0:T(8,128)(2,1)S(1)} %get-tuple-element.13.sent_one_ref), channel_id=1, source_target_pairs={{0,1},{1,0},{2,3},{3,2},{4,5},{5,4},{6,7},{7,6},{8,9},{9,8},{10,11... | collective-permute-start | bytes 49160 | tf_op jit(solution)/shard_map/ppermute | solution.py:512
  17.0 14.1 %collective-permute-start.3 = (bf16[2,32,128]{2,1,0:T(8,128)(2,1)S(1)}, bf16[2,32,128]{2,1,0:T(8,128)(2,1)S(1)}, u32[]{:S(2)}, u32[]{:S(2)}) collective-permute-start(bf16[2,32,128]{2,1,0:T(8,128)(2,1)S(1)} %get-tuple-element.14.sent_two_ref), channel_id=1, source_target_pairs={{0,7},{1,2},{2,1},{3,4},{4,3},{5,6},{6,5},{7,0},{8,15},{9,10},{10,... | collective-permute-start | bytes 49160 | tf_op jit(solution)/shard_map/ppermute | solution.py:513
  21.7 9.3 %collective-permute-start = (bf16[2,128,128]{2,1,0:T(8,128)(2,1)S(1)}, bf16[2,128,128]{2,1,0:T(8,128)(2,1)S(1)}, u32[]{:S(2)}, u32[]{:S(2)}) collective-permute-start(bf16[2,128,128]{2,1,0:T(8,128)(2,1)S(1)} %get-tuple-element.11), channel_id=1, source_target_pairs={{0,8},{8,0},{16,24},{24,16},{32,40},{40,32},{48,56},{56,48},{64,72... | collective-permute-start | bytes 196616 | tf_op jit(solution)/shard_map/ppermute | solution.py:509
  22.7 10.6 %collective-permute-start.1 = (bf16[2,128,128]{2,1,0:T(8,128)(2,1)S(1)}, bf16[2,128,128]{2,1,0:T(8,128)(2,1)S(1)}, u32[]{:S(2)}, u32[]{:S(2)}) collective-permute-start(bf16[2,128,128]{2,1,0:T(8,128)(2,1)S(1)} %get-tuple-element.12), channel_id=1, source_target_pairs={{8,16},{16,8},{24,32},{32,24},{40,48},{48,40},{56,64},{64,56},{72,... | collective-permute-start | bytes 196616 | tf_op jit(solution)/shard_map/ppermute | solution.py:510
  25.2 11.6 %copy-start.5 = (f32[256]{0:T(256)S(1)}, f32[256]{0:T(256)}, u32[]{:S(2)}) copy-start(f32[256]{0:T(256)} %param.11) | copy-start | bytes 3076
  25.3 11.6 %copy-start.6 = (f32[256]{0:T(256)S(1)}, f32[256]{0:T(256)}, u32[]{:S(2)}) copy-start(f32[256]{0:T(256)} %param.13) | copy-start | bytes 3076
  28.0 1.3 %copy-start.2 = (bf16[32,128,256]{2,1,0:T(8,128)(2,1)}, bf16[32,128,256]{2,1,0:T(8,128)(2,1)S(1)}, u32[]{:S(2)}) copy-start(bf16[32,128,256]{2,1,0:T(8,128)(2,1)S(1)} %get-tuple-element.10.taps_hbm_ref) | copy-start | bytes 6291460
  29.3 1.0 %copy-start.3 = (bf16[2304,256]{1,0:T(8,128)(2,1)}, bf16[2304,256]{1,0:T(8,128)(2,1)S(1)}, u32[]{:S(2)}) copy-start(bf16[2304,256]{1,0:T(8,128)(2,1)S(1)} %get-tuple-element.16.w2_hbm_ref) | copy-start | bytes 3538948
  30.3 0.7 %copy-start.4 = (bf16[768,256]{1,0:T(8,128)(2,1)}, bf16[768,256]{1,0:T(8,128)(2,1)S(1)}, u32[]{:S(2)}) copy-start(bf16[768,256]{1,0:T(8,128)(2,1)S(1)} %get-tuple-element.15.w1_hbm_ref) | copy-start | bytes 1179652

commit v8 on v7

--- a/solution.py
+++ b/solution.py
@@ -46,7 +46,7 @@
 def conv_kernel(
     channels, rows, cols, hid,
     place_ref, taps_hbm_ref, lat_one_ref, lat_two_ref, sent_one_ref, sent_two_ref, lon_one_ref, lon_two_ref,
-    w1_hbm_ref, b1_ref, w2_hbm_ref, b2_ref, moved_ref, out_ref, tile_ref,
+    w1_hbm_ref, b1_ref, w2_raw_ref, b2_ref, moved_ref, out_ref, tile_ref,
     raw_taps_ref, w1_ref, w2_ref, taps_ref, edge_ref, edge_taps_ref, edge_hid_ref, west_ref, mid_ref, east_ref,
     turned_ref, done_ref, sem, take_sem, load_sem,
 ):
@@ -61,8 +61,6 @@
     sub = lax.broadcasted_iota(jnp.int32, (8, LANES), 0)
     lane8 = lax.broadcasted_iota(jnp.int32, (8, LANES), 1)
     sub_hid = lax.broadcasted_iota(jnp.int32, (8, hid), 0)
-    group = GROUP
-    over = 2 * group - LANES
 
     def norm(raw):
         return (raw.astype(jnp.float32) - mean) * scale
@@ -76,20 +74,12 @@
     def build(row):
         before, after = edge_ref[0, 1, row : row + 1, :], edge_ref[1, 1, row : row + 1, :]
         if 2 <= row < rows + 2:
-            raw = raw_taps_ref[row - 2].astype(jnp.float32)
-            low = (raw[:, 0:LANES] - mean_low) * scale_low
-            high = (raw[:, LANES : 2 * LANES] - mean_high) * scale_high
-            head = jnp.where(jnp.logical_and(sub == 0, lane8 < group), before, low[:8])
-            tail = jnp.where(
-                jnp.logical_and(sub == 7, lane8 >= over), pltpu.roll(after, over, axis=1), high[cols - 8 :]
-            )
-            low = jnp.concatenate([head, low[8:]], axis=0)
-            high = jnp.concatenate([high[: cols - 8], tail], axis=0)
+            main = norm(raw_taps_ref[row - 2])
         else:
             raw, keep = lat_row(row)
             main = jnp.where(keep, norm(raw), 0.0)
-            minus, plus = shifted(main, before, after, sub)
-            low, high = pack(minus, main, plus, lane)
+        minus, plus = shifted(main, before, after, sub)
+        low, high = pack(minus, main, plus, lane)
         taps_ref[row, :, 0:LANES] = low.astype(jnp.bfloat16)
         taps_ref[row, :, LANES : 2 * LANES] = high.astype(jnp.bfloat16)
 
@@ -204,11 +194,9 @@
         part = pl.ds(low, min((t + 1) * BLOCK + 2, rows) - low)
         return pltpu.make_async_copy(taps_hbm_ref.at[part], raw_taps_ref.at[part], load_sem.at[t])
 
-    load_weights = pltpu.make_async_copy(w2_hbm_ref, w2_ref, load_sem.at[steps])
     load_first = pltpu.make_async_copy(w1_hbm_ref, w1_ref, load_sem.at[steps + 1])
     load_taps(0).start()
     load_first.start()
-    load_weights.start()
     for t in range(1, steps):
         load_taps(t).start()
 
@@ -224,16 +212,17 @@
     scale_low, scale_high = pack(scale, scale, scale, line)
     edges()
     load_taps(0).wait()
+    load_first.wait()
+    for t in range(1, steps):
+        load_taps(t).wait()
     for r in range(UNIT + 4):
         build(r)
-    load_first.wait()
     edges_hidden()
     hidden(0, UNIT + 2)
+    for tap in range(9):
+        w2_ref[tap * hid : (tap + 1) * hid, :] = w2_raw_ref[tap].T
     for c in range(taken):
         pltpu.make_async_copy(moved_ref.at[place_ref[c], 0:rows, :], tile_ref.at[c], take_sem).start()
-    for t in range(1, steps):
-        load_taps(t).wait()
-    load_weights.wait()
     units = rows // UNIT
 
     def more(u):
@@ -267,10 +256,10 @@
             jax.ShapeDtypeStruct((hid, rows, cols), jnp.bfloat16),
             jax.ShapeDtypeStruct((taken, rows, cols), jnp.bfloat16),
         ),
-        in_specs=[smem, hbm] + [vmem] * 6 + [hbm, vmem, hbm, vmem, vmem],
+        in_specs=[smem, hbm] + [vmem] * 6 + [hbm] + [vmem] * 4,
         out_specs=(hbm, hbm),
         scratch_shapes=[
-            pltpu.VMEM((rows, cols, 2 * LANES), jnp.bfloat16),
+            pltpu.VMEM((rows, cols, LANES), jnp.bfloat16),
             pltpu.VMEM((6 * LANES, hid), jnp.bfloat16),
             pltpu.VMEM((9 * hid, hid), jnp.bfloat16),
             pltpu.VMEM((rows + 4, cols, 2 * LANES), jnp.bfloat16),
@@ -292,9 +281,9 @@
     )(place, taps, lat_one, lat_two, sent_one, sent_two, lon_one, lon_two, w1, b1, w2, b2, moved)
 
 
-def stage_kernel(x_ref, w1_raw_ref, w2_raw_ref, taps_ref, w1_ref, w2_ref, wide_ref):
+def stage_kernel(x_ref, w1_raw_ref, taps_ref, w1_ref, wide_ref):
     channels, rows, cols = x_ref.shape
-    hid = w2_ref.shape[1]
+    hid = w1_ref.shape[1]
     padded = wide_ref.shape[1] // 8
     value = x_ref[...].astype(jnp.float32)
     for q in range(rows // 8):
@@ -306,10 +295,7 @@
     for r in range(rows):
         one = wide_ref[r // 8, pl.ds(r % 8, padded, stride=8), :]
         main = jnp.concatenate([one, rest], axis=0).T
-        minus, plus = shifted(main, 0.0, 0.0, sub)
-        low, high = pack(minus, main, plus, lane)
-        taps_ref[r, :, 0:LANES] = low.astype(jnp.bfloat16)
-        taps_ref[r, :, LANES : 2 * LANES] = high.astype(jnp.bfloat16)
+        taps_ref[r] = main.astype(jnp.bfloat16)
     group = w1_raw_ref.shape[1]
     for a in range(3):
         for b in range(3):
@@ -317,28 +303,25 @@
         w1_ref[a * 2 * LANES + 3 * group : (a + 1) * 2 * LANES, :] = jnp.zeros(
             (2 * LANES - 3 * group, hid), jnp.bfloat16
         )
-    for tap in range(9):
-        w2_ref[tap * hid : (tap + 1) * hid, :] = w2_raw_ref[tap].T
-
-
-def stage(current, w1, w2):
+
+
+def stage(current, w1):
     _, rows, cols = current.shape
-    hid = w2.shape[1]
+    hid = w1.shape[2]
     vmem = pl.BlockSpec(memory_space=pltpu.VMEM)
     return pl.pallas_call(
         stage_kernel,
         out_shape=(
-            jax.ShapeDtypeStruct((rows, cols, 2 * LANES), jnp.bfloat16),
+            jax.ShapeDtypeStruct((rows, cols, LANES), jnp.bfloat16),
             jax.ShapeDtypeStruct((6 * LANES, hid), jnp.bfloat16),
-            jax.ShapeDtypeStruct((9 * hid, hid), jnp.bfloat16),
         ),
-        in_specs=[vmem] * 3,
-        out_specs=(vmem,) * 3,
+        in_specs=[vmem] * 2,
+        out_specs=(vmem,) * 2,
         scratch_shapes=[pltpu.VMEM((rows // 8, GROUP * 8, cols), jnp.float32)],
         compiler_params=pltpu.CompilerParams(vmem_limit_bytes=16 * 2**20),
         cost_estimate=pl.CostEstimate(flops=2**25, bytes_accessed=2**22, transcendentals=0),
         name="stage",
-    )(current, w1, w2)
+    )(current, w1)
 
 
 def prepare_kernel(
@@ -512,12 +495,12 @@
     lon_one = lax.ppermute(sent_one, LON, near)
     lon_two = lax.ppermute(sent_two, LON, far)
     w1 = jnp.pad(first_weight.transpose(0, 2, 1), ((0, 0), (0, GROUP - channels), (0, 0)))
-    taps, w1, w2 = stage(current, w1, second_weight)
+    taps, w1 = stage(current, w1)
     place = (reader_slot % n_lon) * n_lat + reader_slot // n_lon
-    taps, w1, w2 = in_hbm(taps), in_hbm(w1), in_hbm(w2)
+    taps, w1 = in_hbm(taps), in_hbm(w1)
     return convs(
         channels, place, taps, lat_one, lat_two, sent_one, sent_two, lon_one, lon_two,
-        w1, first_bias[None], w2, second_bias[None], moved,
+        w1, first_bias[None], second_weight, second_bias[None], moved,
     )
 
 

time: 48.3 us -> 48.1 us (level)
  waiting for transfers between devices: 5.76 us -> 8.6 us
  Pallas kernels: 16.2 us -> 14.7 us
  local copies, waits for them, and re-layouts: 4.12 us -> 2.77 us
    ppermute x1, waiting for transfers between devices: 2.15 us -> 4.65 us  [body(): lat_two = lax.ppermute(lat_two, LAT, far)]
    unnamed x16 -> x14, local copies, waits for them, and re-layouts: 3.11 us -> 1.76 us
    pallas_call x1, Pallas kernels: 1.68 us -> 0.38 us  [stage(): pl.pallas_call(stage_kernel, out_shape=(jax.ShapeDtypeStruct((rows, cols,...]
  transfers between devices with their start and end apart: 5 -> 5, of which waited for: 2 -> 3; matrix products, arithmetic and copies ran while one was open for 2% -> 2% of each run, Pallas kernels for 4% -> 1%
where the time goes in v8:
time: 48.1 us; the launch traced here: 47.8 us
  starting transfers between devices  20.9 us (43%)
  Pallas kernels  14.7 us (31%)
  waiting for transfers between devices  8.6 us (18%)
  local copies, waits for them, and re-layouts  2.77 us (6%)
  between operations  0.74 us (2%)
    all_to_all x1, starting transfers between devices, body(): lax.all_to_all(blocks.reshape(n_lon * n_lat, rows + EXTRA, cols), LON + L...  11.5 us
    pallas_call x1, Pallas kernels, convs(): pl.pallas_call(functools.partial(conv_kernel, channels, rows, cols, hid),...  10.9 us
    ppermute x1, starting transfers between devices, body(): lon_two = lax.ppermute(sent_two, LON, far)  4.72 us
    ppermute x1, waiting for transfers between devices, body(): lat_two = lax.ppermute(lat_two, LAT, far)  4.65 us
    all_to_all x1, waiting for transfers between devices, body(): lax.all_to_all(blocks.reshape(n_lon * n_lat, rows + EXTRA, cols), LON + L...  3.61 us
    pallas_call x1, Pallas kernels, prepare(): pl.pallas_call(functools.partial(prepare_kernel, channels), out_shape=(la...  3.41 us
    ppermute x1, starting transfers between devices, body(): lat_two = lax.ppermute(lat_two, LAT, far)  2.34 us
    unnamed x14, local copies, waits for them, and re-layouts  1.76 us
  transfers between devices with their start and end apart: 5, of which 3 were waited for; matrix products, arithmetic and copies ran while one was open for 2% of the time, Pallas kernels for 1%

profile of v8, /device:TPU:1, one launch (start us, length us, event | category | flops | bytes accessed | tf_op | source)
XLA Modules:
  0.0 47.8 jit_solution(15172856388517210133)
XLA Ops:
  0.6 3.4 %prepare.1 = (bf16[2,128,128]{2,1,0:T(8,128)(2,1)S(1)}, bf16[2,128,128]{2,1,0:T(8,128)(2,1)S(1)}, bf16[2,32,128]{2,1,0:T(8,128)(2,1)S(1)}, bf16[2,32,128]{2,1,0:T(8,128)(2,1)S(1)}, bf16[8,16,40,128]{3,2,1,0:T(8,128)(2,1)}) custom-call(bf16[69,32,128]{2,1,0:T(8,128)(2,1)} %x_ref.3, bf16[1,512,1024]{2,1,0:T(8,128)(2,1)} %fields_ref.1), custom_call_target="tpu_custom_call" | custom-call | flops 16777216 | bytes 4194304 | tf_op jit(solution)/shard_map/prepare/pallas_call | solution.py:443
  4.1 0.0 copy-start.6
  4.1 0.0 copy-start
  4.1 11.5 %all-to-all-start = ((bf16[128,40,128]{2,1,0:T(8,128)(2,1)}), bf16[128,40,128]{2,1,0:T(8,128)(2,1)S(1)}, u32[]{:S(2)}, u32[]{:S(2)}) async-start(bf16[128,40,128]{2,1,0:T(8,128)(2,1)} %bitcast.3), calls=%async_computation | async-start | bytes 2621440 | tf_op jit(solution)/shard_map/all_to_all | solution.py:488
  15.6 0.0 copy-start.1
  15.6 0.0 copy-start.4
  15.6 0.0 copy-start.5
  15.6 1.4 %collective-permute-start.2 = (bf16[2,32,128]{2,1,0:T(8,128)(2,1)S(1)}, bf16[2,32,128]{2,1,0:T(8,128)(2,1)S(1)}, u32[]{:S(2)}, u32[]{:S(2)}) collective-permute-start(bf16[2,32,128]{2,1,0:T(8,128)(2,1)S(1)} %get-tuple-element.12.sent_one_ref), channel_id=1, source_target_pairs={{0,1},{1,0},{2,3},{3,2},{4,5},{5,4},{6,7},{7,6},{8,9},{9,8},{10,11... | collective-permute-start | bytes 49160 | tf_op jit(solution)/shard_map/ppermute | solution.py:495
  17.0 4.7 %collective-permute-start.3 = (bf16[2,32,128]{2,1,0:T(8,128)(2,1)S(1)}, bf16[2,32,128]{2,1,0:T(8,128)(2,1)S(1)}, u32[]{:S(2)}, u32[]{:S(2)}) collective-permute-start(bf16[2,32,128]{2,1,0:T(8,128)(2,1)S(1)} %get-tuple-element.13.sent_two_ref), channel_id=1, source_target_pairs={{0,7},{1,2},{2,1},{3,4},{4,3},{5,6},{6,5},{7,0},{8,15},{9,10},{10,... | collective-permute-start | bytes 49160 | tf_op jit(solution)/shard_map/ppermute | solution.py:496
  21.8 0.9 %collective-permute-start = (bf16[2,128,128]{2,1,0:T(8,128)(2,1)S(1)}, bf16[2,128,128]{2,1,0:T(8,128)(2,1)S(1)}, u32[]{:S(2)}, u32[]{:S(2)}) collective-permute-start(bf16[2,128,128]{2,1,0:T(8,128)(2,1)S(1)} %get-tuple-element.10), channel_id=1, source_target_pairs={{0,8},{8,0},{16,24},{24,16},{32,40},{40,32},{48,56},{56,48},{64,72... | collective-permute-start | bytes 196616 | tf_op jit(solution)/shard_map/ppermute | solution.py:492
  22.7 2.3 %collective-permute-start.1 = (bf16[2,128,128]{2,1,0:T(8,128)(2,1)S(1)}, bf16[2,128,128]{2,1,0:T(8,128)(2,1)S(1)}, u32[]{:S(2)}, u32[]{:S(2)}) collective-permute-start(bf16[2,128,128]{2,1,0:T(8,128)(2,1)S(1)} %get-tuple-element.11), channel_id=1, source_target_pairs={{8,16},{16,8},{24,32},{32,24},{40,48},{48,40},{56,64},{64,56},{72,... | collective-permute-start | bytes 196616 | tf_op jit(solution)/shard_map/ppermute | solution.py:493
  25.1 0.0 copy-done.6
  25.1 1.0 %pad.4.w1_raw_ref = bf16[9,72,256]{2,1,0:T(8,128)(2,1)S(1)} pad(bf16[9,69,256]{2,1,0:T(8,128)(2,1)} %bitcast.6, bf16[]{:T(256)} %constant.32.clone.1), padding=0_0x0_3x0_0 | pad | bytes 649730 | tf_op jit(solution)/shard_map/jit(_pad)/pad | solution.py:497
  26.1 0.0 copy-done
  26.1 0.4 stage.1
  26.5 0.0 copy-start.2
  26.5 1.0 %copy-done.2 = bf16[32,128,128]{2,1,0:T(8,128)(2,1)} copy-done((bf16[32,128,128]{2,1,0:T(8,128)(2,1)}, bf16[32,128,128]{2,1,0:T(8,128)(2,1)S(1)}, u32[]{:S(2)}) %copy-start.2) | copy-done | bytes 1048600
  27.5 0.0 copy-start.3
  27.5 0.8 %copy-done.3 = bf16[768,256]{1,0:T(8,128)(2,1)} copy-done((bf16[768,256]{1,0:T(8,128)(2,1)}, bf16[768,256]{1,0:T(8,128)(2,1)S(1)}, u32[]{:S(2)}) %copy-start.3) | copy-done | bytes 393240
  28.2 0.0 collective-permute-done.2.lon_one_ref
  28.2 0.3 collective-permute-done.3.lon_two_ref
  28.6 0.0 collective-permute-done.lat_one_ref
  28.6 4.6 %collective-permute-done.1.lat_two_ref = bf16[2,128,128]{2,1,0:T(8,128)(2,1)S(1)} collective-permute-done((bf16[2,128,128]{2,1,0:T(8,128)(2,1)S(1)}, bf16[2,128,128]{2,1,0:T(8,128)(2,1)S(1)}, u32[]{:S(2)}, u32[]{:S(2)}) %collective-permute-start.1) | collective-permute-done | bytes 65568 | tf_op jit(solution)/shard_map/ppermute | solution.py:493
  33.2 3.6 %all-to-all-done.moved_ref = bf16[128,40,128]{2,1,0:T(8,128)(2,1)S(1)} async-done(((bf16[128,40,128]{2,1,0:T(8,128)(2,1)}), bf16[128,40,128]{2,1,0:T(8,128)(2,1)S(1)}, u32[]{:S(2)}, u32[]{:S(2)}) %all-to-all-start) | async-done | bytes 1310752 | tf_op jit(solution)/shard_map/all_to_all | solution.py:488
  36.8 0.0 copy-done.1
  36.8 0.0 copy-done.4
  36.8 0.0 copy-done.5
  36.9 10.9 %convs.1 = (bf16[256,32,128]{2,1,0:T(8,128)(2,1)}, bf16[69,32,128]{2,1,0:T(8,128)(2,1)}) custom-call(s32[69]{0:T(128)S(1)} %fusion.1.place_ref, bf16[32,128,128]{2,1,0:T(8,128)(2,1)} %copy-done.2, bf16[2,128,128]{2,1,0:T(8,128)(2,1)S(1)} %collective-permute-done.lat_one_ref, bf16[2,128,128]{2,1,0:T(8,128)(2,1)S(1)} %collective-permute-done.1.lat_two_ref, ...), custom_call_target="tpu_custom_call" | custom-call | flops 6569852928 | bytes 8388608 | tf_op jit(solution)/shard_map/convs/pallas_call | solution.py:253
  (1 shorter events, 0.0 us)
Async XLA Ops:
  4.1 21.0 %copy-start.6 = (s32[69]{0:T(128)S(1)}, s32[69]{0:T(128)}, u32[]{:S(2)}) copy-start(s32[69]{0:T(128)} %param.9) | copy-start | bytes 832
  4.1 22.0 %copy-start = (bf16[69,32,128]{2,1,0:T(8,128)(2,1)S(1)}, bf16[69,32,128]{2,1,0:T(8,128)(2,1)}, u32[]{:S(2)}) copy-start(bf16[69,32,128]{2,1,0:T(8,128)(2,1)} %x_ref.3) | copy-start | bytes 1695748
  4.1 32.8 %all-to-all-start = ((bf16[128,40,128]{2,1,0:T(8,128)(2,1)}), bf16[128,40,128]{2,1,0:T(8,128)(2,1)S(1)}, u32[]{:S(2)}, u32[]{:S(2)}) async-start(bf16[128,40,128]{2,1,0:T(8,128)(2,1)} %bitcast.3), calls=%async_computation | async-start | bytes 2621440 | tf_op jit(solution)/shard_map/all_to_all | solution.py:488
  15.6 21.3 %copy-start.1 = (bf16[9,256,256]{2,1,0:T(8,128)(2,1)S(1)}, bf16[9,256,256]{2,1,0:T(8,128)(2,1)}, u32[]{:S(2)}) copy-start(bf16[9,256,256]{2,1,0:T(8,128)(2,1)} %w2_raw_ref.1) | copy-start | bytes 3538948
  15.6 21.3 %copy-start.4 = (f32[256]{0:T(256)S(1)}, f32[256]{0:T(256)}, u32[]{:S(2)}) copy-start(f32[256]{0:T(256)} %param.11) | copy-start | bytes 3076
  15.6 21.2 %copy-start.5 = (f32[256]{0:T(256)S(1)}, f32[256]{0:T(256)}, u32[]{:S(2)}) copy-start(f32[256]{0:T(256)} %param.13) | copy-start | bytes 3076
  15.6 12.6 %collective-permute-start.2 = (bf16[2,32,128]{2,1,0:T(8,128)(2,1)S(1)}, bf16[2,32,128]{2,1,0:T(8,128)(2,1)S(1)}, u32[]{:S(2)}, u32[]{:S(2)}) collective-permute-start(bf16[2,32,128]{2,1,0:T(8,128)(2,1)S(1)} %get-tuple-element.12.sent_one_ref), channel_id=1, source_target_pairs={{0,1},{1,0},{2,3},{3,2},{4,5},{5,4},{6,7},{7,6},{8,9},{9,8},{10,11... | collective-permute-start | bytes 49160 | tf_op jit(solution)/shard_map/ppermute | solution.py:495
  17.0 11.5 %collective-permute-start.3 = (bf16[2,32,128]{2,1,0:T(8,128)(2,1)S(1)}, bf16[2,32,128]{2,1,0:T(8,128)(2,1)S(1)}, u32[]{:S(2)}, u32[]{:S(2)}) collective-permute-start(bf16[2,32,128]{2,1,0:T(8,128)(2,1)S(1)} %get-tuple-element.13.sent_two_ref), channel_id=1, source_target_pairs={{0,7},{1,2},{2,1},{3,4},{4,3},{5,6},{6,5},{7,0},{8,15},{9,10},{10,... | collective-permute-start | bytes 49160 | tf_op jit(solution)/shard_map/ppermute | solution.py:496
  21.8 6.8 %collective-permute-start = (bf16[2,128,128]{2,1,0:T(8,128)(2,1)S(1)}, bf16[2,128,128]{2,1,0:T(8,128)(2,1)S(1)}, u32[]{:S(2)}, u32[]{:S(2)}) collective-permute-start(bf16[2,128,128]{2,1,0:T(8,128)(2,1)S(1)} %get-tuple-element.10), channel_id=1, source_target_pairs={{0,8},{8,0},{16,24},{24,16},{32,40},{40,32},{48,56},{56,48},{64,72... | collective-permute-start | bytes 196616 | tf_op jit(solution)/shard_map/ppermute | solution.py:492
  22.7 10.5 %collective-permute-start.1 = (bf16[2,128,128]{2,1,0:T(8,128)(2,1)S(1)}, bf16[2,128,128]{2,1,0:T(8,128)(2,1)S(1)}, u32[]{:S(2)}, u32[]{:S(2)}) collective-permute-start(bf16[2,128,128]{2,1,0:T(8,128)(2,1)S(1)} %get-tuple-element.11), channel_id=1, source_target_pairs={{8,16},{16,8},{24,32},{32,24},{40,48},{48,40},{56,64},{64,56},{72,... | collective-permute-start | bytes 196616 | tf_op jit(solution)/shard_map/ppermute | solution.py:493
  26.5 1.0 %copy-start.2 = (bf16[32,128,128]{2,1,0:T(8,128)(2,1)}, bf16[32,128,128]{2,1,0:T(8,128)(2,1)S(1)}, u32[]{:S(2)}) copy-start(bf16[32,128,128]{2,1,0:T(8,128)(2,1)S(1)} %get-tuple-element.9.taps_hbm_ref) | copy-start | bytes 3145732
  27.5 0.8 %copy-start.3 = (bf16[768,256]{1,0:T(8,128)(2,1)}, bf16[768,256]{1,0:T(8,128)(2,1)S(1)}, u32[]{:S(2)}) copy-start(bf16[768,256]{1,0:T(8,128)(2,1)S(1)} %get-tuple-element.14.w1_hbm_ref) | copy-start | bytes 1179652
